TPU v7x, 32 devices: a whole 2x2x4 slice. The times are simulated.
32 devices in a mesh: fsdp: 4 (over y, x), tp: 8 (over z, core).
Axes of the slice: x: 2, y: 2, z: 4, core: 2. Of those that a mesh axis runs over, the one named last changes fastest.
Arguments:
- inputs: bfloat16 [2, 4, 2048, 2048], P(None, 'fsdp', 'tp'), may hold values from -6 to 6
- out_grad: bfloat16 [2, 4, 2048, 2048], P(None, 'fsdp', 'tp'), may hold values from -6 to 6
- lengths: int32 [2, 4], replicated, may hold values from 1024 to 2048, as said below
- norm1_gain: bfloat16 [2048], P('fsdp'), may hold values from 0.099609375 to 1.8984375
- qkv_weight: bfloat16 [2048, 3, 2048], P('fsdp', None, 'tp'), may hold values from -0.125 to 0.125
- out_weight: bfloat16 [2048, 2048], P('tp', 'fsdp'), may hold values from -0.75 to 0.75
- norm2_gain: bfloat16 [2048], P('fsdp'), may hold values from 0.099609375 to 1.8984375
- gate_up_weight: bfloat16 [2048, 2, 8192], P('fsdp', None, 'tp'), may hold values from -0.125 to 0.125
- down_weight: bfloat16 [8192, 2048], P('tp', 'fsdp'), may hold values from -0.0625 to 0.0625
Outputs:
- outputs: bfloat16 [2, 4, 2048, 2048], P(None, 'fsdp', 'tp')
- input_grad: bfloat16 [2, 4, 2048, 2048], P(None, 'fsdp', 'tp')
- norm1_gain_grad: float32 [2048], P('fsdp')
- qkv_grad: float32 [2048, 3, 2048], P('fsdp', None, 'tp')
- out_weight_grad: float32 [2048, 2048], P('tp', 'fsdp')
- norm2_gain_grad: float32 [2048], P('fsdp')
- gate_up_grad: float32 [2048, 2, 8192], P('fsdp', None, 'tp')
- down_grad: float32 [8192, 2048], P('tp', 'fsdp')
Inputs may be any that keep to these rules, and one draw needn't show every extreme that they name: lengths[m, g] tokens of the sequence of micro-batch m and group g are live, at its start; where m + g is even there are more than 1536 of them, else fewer than 1536.
All inputs are finite; a program needn't handle non-finite values.
Results may differ from a plain program's by a relative error of at most 0.024.
Values may be sent and summed in bfloat16 or wider, within the bound.
A program may use at most 184 MiB of HBM per device.

v0:
```python
import functools
import math

import jax
import jax.numpy as jnp
from jax import lax
from jax.experimental import pallas as pl
from jax.experimental.pallas import tpu as pltpu
from jax.sharding import Mesh
from jax.sharding import PartitionSpec as P


HD = 64
NORM_EPS = 1e-05
ROPE_THETA = 130000.0
BLK = 256
SEG = 2
BF = jnp.bfloat16
F32 = jnp.float32
NEG = -1e30
SCALE = 1.0 / math.sqrt(HD)
LOG2E = math.log2(math.e)
VMEM_BYTES = 60 * 1024 * 1024


OWN, OTHER = 0, 1


def swap(x, axis, bit):
    size = lax.axis_size(axis)
    return lax.ppermute(x, axis, [(i, i ^ bit) for i in range(size)])


def gather_slots(x, axis):
    size = lax.axis_size(axis)
    slots = {0: x}
    bit = size // 2
    while bit:
        for k in list(slots):
            slots[k | bit] = swap(slots[k], axis, bit)
        bit //= 2
    return [slots[k] for k in range(size)]


def scatter_slots(parts, axis):
    slots = dict(enumerate(parts))
    bit = 1
    while bit < lax.axis_size(axis):
        for k in [k for k in slots if k & bit]:
            got = swap(slots.pop(k), axis, bit)
            kept = slots[k ^ bit].astype(F32) + got.astype(F32)
            slots[k ^ bit] = kept if bit * 2 == lax.axis_size(axis) else kept.astype(BF)
        bit *= 2
    return slots[0]


def gather_rows(local):
    blocks = gather_slots(local, "tp")
    return jnp.concatenate([b[h] for h in range(2) for b in blocks], axis=0)


def scatter_rows(full, rows):
    size = lax.axis_size("tp")
    parts = full.reshape(2, size, rows, full.shape[-1])
    return scatter_slots([parts[:, k] for k in range(size)], "tp")


def scatter_half(half, rows):
    parts = half.reshape(-1, rows, half.shape[-1])
    return scatter_slots([parts[k] for k in range(parts.shape[0])], "tp")


def sum_all(x, axes):
    for axis in axes:
        bit = 1
        while bit < lax.axis_size(axis):
            x = x + swap(x, axis, bit)
            bit *= 2
    return x


def qkv_kernel(x_ref, w_ref, cos_ref, sa_ref, sb_ref, o_ref):
    acc = jnp.dot(x_ref[...], w_ref[...], preferred_element_type=F32)
    cos, sin_a, sin_b = cos_ref[...], sa_ref[...], sb_ref[...]
    for part in range(o_ref.shape[1] // 128):
        lanes = slice(part * 128, part * 128 + 128)
        u = acc[:, lanes]
        if part % 3 < 2:
            u = u * cos + pltpu.roll(u, 96, 1) * sin_a + pltpu.roll(u, 32, 1) * sin_b
        o_ref[:, lanes] = u.astype(BF)


def qkv_project(rows, weight, cos, sin_a, sin_b):
    seq, dim = rows.shape
    cols = weight.shape[1] // 4 * 3
    row_block = min(BLK, seq)
    return pl.pallas_call(
        qkv_kernel,
        grid=(seq // row_block,),
        in_specs=[
            pl.BlockSpec((row_block, dim), lambda i: (i, 0)),
            pl.BlockSpec((dim, cols), lambda i: (0, 0), pipeline_mode=pl.Buffered(1)),
        ]
        + [pl.BlockSpec((row_block, 128), lambda i: (i, 0))] * 3,
        out_specs=pl.BlockSpec((row_block, cols), lambda i: (i, 0)),
        out_shape=jax.ShapeDtypeStruct((seq, cols), BF),
        compiler_params=pltpu.CompilerParams(vmem_limit_bytes=VMEM_BYTES),
        cost_estimate=pl.CostEstimate(
            flops=2 * seq * dim * cols, bytes_accessed=2 * (seq * dim + dim * cols + seq * cols), transcendentals=0
        ),
        name="qkv_project",
    )(rows, weight, cos, sin_a, sin_b)


def slot_of(block, group, turn, side):
    return jnp.bitwise_xor(block // group, side) * group + jnp.bitwise_xor(block % group, turn)


def lane_masks(rows):
    lane = lax.broadcasted_iota(jnp.int32, (rows, 128), 1)
    return lane < HD, lane >= HD


def diagonal_mask(block, length):
    key = lax.broadcasted_iota(jnp.int32, (BLK, BLK), 0)
    query = lax.broadcasted_iota(jnp.int32, (BLK, BLK), 1)
    return (key <= query) & (key + block * BLK < length)


def attend_kernel(group, info_ref, qkv_ref, o_ref, lse_ref, vt_ref):
    count = qkv_ref.shape[0] // BLK
    length, turn, side = info_ref[0], info_ref[1], info_ref[2]

    def rows_of(block):
        return pl.ds(pl.multiple_of(slot_of(block, group, turn, side) * BLK, BLK), BLK)

    masks = lane_masks(BLK)
    for i in range(count):

        @pl.when(i * BLK < length)
        def _():
            where_q = rows_of(i)
            vt_ref[i] = qkv_ref[where_q, 256:384].T
            q = qkv_ref[where_q, 0:128]
            outs = []
            for h in range(2):
                qt = jnp.where(masks[h], q, jnp.zeros_like(q)).T
                top = total = acc = None
                step = 2
                first = 0
                while first <= i:
                    blocks = list(range(first, min(first + step, i + 1)))
                    scores = []
                    for b in blocks:
                        s = jnp.dot(qkv_ref[rows_of(b), 128:256], qt, preferred_element_type=F32) * (SCALE * LOG2E)
                        if b == i:
                            s = jnp.where(diagonal_mask(i, length), s, NEG)
                        scores.append(s)
                    new_top = functools.reduce(jnp.maximum, [jnp.max(s, axis=0, keepdims=True) for s in scores])
                    if top is not None:
                        new_top = jnp.maximum(top, new_top)
                        fade = jnp.exp2(top - new_top)
                        total, acc = total * fade, acc * fade
                    for b, s in zip(blocks, scores):
                        p = jnp.exp2(s - new_top)
                        p_sum = jnp.sum(p, axis=0, keepdims=True)
                        mixed = jnp.dot(
                            vt_ref[b, h * HD : h * HD + HD, :], p.astype(BF), preferred_element_type=F32
                        )
                        total = p_sum if total is None else total + p_sum
                        acc = mixed if acc is None else acc + mixed
                    top = new_top
                    first += step
                outs.append(acc / total)
                lse_ref[i, h : h + 1, :] = top + jnp.log2(total)
            o_ref[where_q, :] = jnp.concatenate(outs, axis=0).T.astype(BF)

        @pl.when(i * BLK >= length)
        def _():
            o_ref[rows_of(i), :] = jnp.zeros((BLK, 128), BF)
            lse_ref[i] = jnp.zeros((2, BLK), F32)


def attend(info, qkv, group):
    seq, cols = qkv.shape
    pairs = cols // 384
    count = seq // BLK
    return pl.pallas_call(
        functools.partial(attend_kernel, group),
        grid_spec=pltpu.PrefetchScalarGridSpec(
            num_scalar_prefetch=1,
            grid=(pairs,),
            in_specs=[pl.BlockSpec((seq, 384), lambda p, s: (0, p))],
            out_specs=[
                pl.BlockSpec((seq, 128), lambda p, s: (0, p)),
                pl.BlockSpec((None, count, 2, BLK), lambda p, s: (p, 0, 0, 0)),
            ],
            scratch_shapes=[pltpu.VMEM((count, 128, BLK), BF)],
        ),
        out_shape=[
            jax.ShapeDtypeStruct((seq, pairs * 128), BF),
            jax.ShapeDtypeStruct((pairs, count, 2, BLK), F32),
        ],
        compiler_params=pltpu.CompilerParams(vmem_limit_bytes=VMEM_BYTES),
        cost_estimate=pl.CostEstimate(
            flops=pairs * 2 * seq * seq * 2 * 256, bytes_accessed=2 * seq * pairs * 512, transcendentals=pairs * seq * seq
        ),
        name="attend",
    )(info, qkv)


def rope_back(w, cos_t, sin_t):
    half = HD // 2
    upper, lower = w[:half], w[half:]
    return jnp.concatenate([upper * cos_t + lower * sin_t, lower * cos_t - upper * sin_t], axis=0)


def attend_back_kernel(
    group, info_ref, qkv_ref, o_ref, do_ref, lse_ref, cos_ref, sin_ref, d_ref, kt_ref, dk_ref, dv_ref
):
    count = qkv_ref.shape[0] // BLK
    length, turn, side = info_ref[0], info_ref[1], info_ref[2]

    def rows_of(block):
        return pl.ds(pl.multiple_of(slot_of(block, group, turn, side) * BLK, BLK), BLK)

    masks = lane_masks(BLK)
    for i in range(count):

        @pl.when(i * BLK < length)
        def _():
            where_q = rows_of(i)
            kt_ref[i] = qkv_ref[where_q, 128:256].T
            q = qkv_ref[where_q, 0:128]
            do = do_ref[where_q, :]
            product = (o_ref[where_q, :].astype(F32) * do.astype(F32)).T
            zero = jnp.zeros_like(q)
            dq_t = []
            for h in range(2):
                q_h = jnp.where(masks[h], q, zero)
                do_h = jnp.where(masks[h], do, zero)
                qt, dot_t = q_h.T, do_h.T
                lse = lse_ref[i, h : h + 1, :]
                delta = jnp.sum(product[h * HD : h * HD + HD], axis=0, keepdims=True)
                dq = None
                for b in range(i + 1):
                    rows_b = rows_of(b)
                    s = jnp.dot(qkv_ref[rows_b, 128:256], qt, preferred_element_type=F32)
                    s = s * (SCALE * LOG2E) - lse
                    if b == i:
                        s = jnp.where(diagonal_mask(i, length), s, NEG)
                    p = jnp.exp2(s)
                    dp = jnp.dot(qkv_ref[rows_b, 256:384], dot_t, preferred_element_type=F32)
                    ds = (p * (dp - delta)).astype(BF)
                    dv = jnp.dot(p.astype(BF), do_h, preferred_element_type=F32)
                    dk = jnp.dot(ds, q_h, preferred_element_type=F32)
                    if b == i and h == 0:
                        dv_ref[b] = dv
                        dk_ref[b] = dk
                    else:
                        dv_ref[b] += dv
                        dk_ref[b] += dk
                    part = jnp.dot(kt_ref[b, h * HD : h * HD + HD, :], ds, preferred_element_type=F32)
                    dq = part if dq is None else dq + part
                dq_t.append(rope_back(dq * SCALE, cos_ref[i], sin_ref[i]))
            d_ref[where_q, 0:128] = jnp.concatenate(dq_t, axis=0).T.astype(BF)

        @pl.when(i * BLK >= length)
        def _():
            d_ref[rows_of(i), :] = jnp.zeros((BLK, 384), BF)

    for i in range(count):

        @pl.when(i * BLK < length)
        def _():
            where_k = rows_of(i)
            dk_t = dk_ref[i].T * SCALE
            parts = [rope_back(dk_t[h * HD : h * HD + HD], cos_ref[i], sin_ref[i]) for h in range(2)]
            d_ref[where_k, 128:256] = jnp.concatenate(parts, axis=0).T.astype(BF)
            d_ref[where_k, 256:384] = dv_ref[i].astype(BF)


def attend_back(info, qkv, mixed, grad_mixed, lse, cos_t, sin_t, group):
    seq, cols = qkv.shape
    pairs = cols // 384
    count = seq // BLK
    return pl.pallas_call(
        functools.partial(attend_back_kernel, group),
        grid_spec=pltpu.PrefetchScalarGridSpec(
            num_scalar_prefetch=1,
            grid=(pairs,),
            in_specs=[
                pl.BlockSpec((seq, 384), lambda p, s: (0, p)),
                pl.BlockSpec((seq, 128), lambda p, s: (0, p)),
                pl.BlockSpec((seq, 128), lambda p, s: (0, p)),
                pl.BlockSpec((None, count, 2, BLK), lambda p, s: (p, 0, 0, 0)),
                pl.BlockSpec((count, HD // 2, BLK), lambda p, s: (0, 0, 0)),
                pl.BlockSpec((count, HD // 2, BLK), lambda p, s: (0, 0, 0)),
            ],
            out_specs=pl.BlockSpec((seq, 384), lambda p, s: (0, p)),
            scratch_shapes=[
                pltpu.VMEM((count, 128, BLK), BF),
                pltpu.VMEM((count, BLK, 128), F32),
                pltpu.VMEM((count, BLK, 128), F32),
            ],
        ),
        out_shape=jax.ShapeDtypeStruct((seq, pairs * 384), BF),
        compiler_params=pltpu.CompilerParams(vmem_limit_bytes=VMEM_BYTES),
        cost_estimate=pl.CostEstimate(
            flops=pairs * 2 * seq * seq * 5 * 256, bytes_accessed=2 * seq * pairs * 1024, transcendentals=pairs * seq * seq
        ),
        name="attend_back",
    )(info, qkv, mixed, grad_mixed, lse, cos_t, sin_t)


def norm_forward(residual, gain_vec):
    factor = lax.rsqrt(jnp.mean(residual * residual, axis=-1, keepdims=True) + NORM_EPS)
    return residual * factor * gain_vec, factor


def norm_backward(residual, factor, gain_vec, grad_in):
    scaled = grad_in * gain_vec
    grad_resid = factor * scaled - residual * factor**3 * jnp.mean(scaled * residual, axis=-1, keepdims=True)
    grad_gain = jnp.sum(grad_in * residual * factor, axis=tuple(range(grad_in.ndim - 1)))
    return grad_resid, grad_gain


def mul(a, b, dims):
    return lax.dot_general(a, b, (dims, ((), ())), preferred_element_type=F32)


NN, NT, TN = ((1,), (0,)), ((1,), (1,)), ((0,), (0,))


def after(value, *anchors):
    return lax.optimization_barrier((value, *anchors))[0]


def layer(inputs, out_grad, lengths, norm1_gain, qkv_weight, out_weight, norm2_gain, gate_up_weight, down_weight):
    rows, _ = inputs.shape[2:]
    group = lax.axis_size("tp")
    seq = SEG * group * rows
    seg, fsdp, me = lax.axis_index("seg"), lax.axis_index("fsdp"), lax.axis_index("tp")
    length = jnp.sum(
        jnp.where(
            (jnp.arange(lengths.shape[0])[:, None] == seg) & (jnp.arange(lengths.shape[1])[None] == fsdp), lengths, 0
        )
    )

    def parted(stacked):
        mine = lax.dynamic_index_in_dim(stacked[:, 0], seg, 0, keepdims=False)
        other = lax.dynamic_index_in_dim(stacked[:, 0], 1 - seg, 0, keepdims=False)
        return mine, other

    def joined(mine, got):
        return jnp.where(seg == 0, jnp.stack([mine, got]), jnp.stack([got, mine]))[:, None]

    def rows_full(shard):
        return lax.all_gather(shard, "fsdp", axis=0, tiled=True)

    def wide(shard):
        return [rows_full(shard), rows_full(swap(shard, "seg", 1))]

    depth = qkv_weight.shape[0]
    head_cols = qkv_weight.shape[2]
    ff = down_weight.shape[0]
    whole_pairs = head_cols % 128 == 0

    def paired(qkv_cols, out_cols):
        count = out_cols.shape[1] // 128
        by_pair = qkv_cols.reshape(depth, 3, count, 128).transpose(0, 2, 1, 3).reshape(depth, count * 384)
        return jnp.concatenate([by_pair, out_cols], axis=1)

    def unpaired(joint):
        count = joint.shape[1] // 512
        by_pair = joint[:, : count * 384].reshape(depth, count, 3, 128).transpose(0, 2, 1, 3)
        return by_pair.reshape(depth, 3, count * 128), joint[:, count * 384 :]

    x_mine, x_other = parted(inputs)
    x_got = swap(x_other, "seg", 1)
    if whole_pairs:
        w_qkvo = wide(paired(qkv_weight, out_weight.T))
    else:
        both = [jnp.stack([w, swap(w, "seg", 1)], axis=-2) for w in (qkv_weight, out_weight.T)]
        w_qkvo = [rows_full(paired(both[0].reshape(depth, 3, -1), both[1].reshape(depth, -1)))]
    gains = lax.all_gather(jnp.stack([norm1_gain, norm2_gain]), "fsdp", axis=0).astype(F32)
    gain_one = gains[:, 0].reshape(-1)
    gain_two = gains[:, 1].reshape(-1)
    w_down = wide(down_weight.T)
    w_gu = wide(gate_up_weight.reshape(depth, 2 * ff))
    cut = w_qkvo[0].shape[1] // 4 * 3
    w_out = jnp.concatenate([w[:, cut:] for w in w_qkvo], axis=1)

    slot = jnp.arange(group)
    position = (
        jnp.bitwise_xor(jnp.arange(SEG), seg)[:, None, None] * (group * rows)
        + jnp.bitwise_xor(slot, me)[None, :, None] * rows
        + jnp.arange(rows)[None, None, :]
    ).reshape(seq)
    inverse = ROPE_THETA ** (-(jnp.arange(HD // 2).astype(F32) * 2.0) / HD)
    angles = position.astype(F32)[:, None] * jnp.tile(inverse, 4)[None, :]
    cos_tab, sin = jnp.cos(angles), jnp.sin(angles)
    first = (jnp.arange(128) % HD < HD // 2)[None, :]
    sin_a = jnp.where(first, -sin, 0.0)
    sin_b = jnp.where(first, 0.0, sin)
    natural = jnp.arange(seq).astype(F32)
    angles_t = inverse[None, :, None] * natural.reshape(seq // BLK, 1, BLK)
    cos_t, sin_t = jnp.cos(angles_t), jnp.sin(angles_t)
    in_kernel = rows == BLK
    none = jnp.int32(0)
    info = jnp.stack([length, me if in_kernel else none, seg if in_kernel else none]).astype(jnp.int32)
    kernel_group = group if in_kernel else seq // BLK // SEG

    def reorder(full):
        if in_kernel:
            return full
        split = full.reshape(SEG, group, rows, full.shape[-1])
        split = jnp.take(split, jnp.bitwise_xor(jnp.arange(SEG), seg), axis=0)
        return jnp.take(split, jnp.bitwise_xor(slot, me), axis=1).reshape(full.shape)

    own_position = (
        jnp.bitwise_xor(jnp.arange(SEG), seg)[:, None, None] * (group * rows)
        + me * rows
        + jnp.arange(rows)[None, :, None]
    )
    live = (own_position < length).astype(F32)

    halves = [x_mine.astype(F32), x_got.astype(F32)]
    blocks, factor_one = [], []
    for x in halves:
        normed, factor = norm_forward(x, gain_one)
        blocks.append(gather_slots(normed.astype(BF), "tp"))
        factor_one.append(factor)
    normed_rows = jnp.concatenate(blocks[0] + blocks[1], axis=0)
    residual = jnp.stack(halves)
    qkv, mixed, lse = [], [], []
    for part, weight in enumerate(w_qkvo):
        projected = qkv_project(normed_rows, weight, cos_tab, sin_a, sin_b)
        qkv.append(reorder(projected))
        outs = attend(info, qkv[part], kernel_group)
        mixed.append(outs[0])
        lse.append(outs[1])
    mixed_slots = [reorder(m) for m in mixed]
    product = mul(jnp.concatenate(mixed_slots, axis=1), w_out, NT).astype(BF)
    middle = residual + scatter_rows(product, rows)
    normed_two, factor_two = norm_forward(middle, gain_two)
    two_rows = gather_rows(normed_two.astype(BF))

    g_mine, g_other = parted(out_grad)
    g_got = swap(g_other, "seg", 1)
    grad_result = jnp.stack([g_mine, g_got]).astype(F32) * live
    grad_rows = gather_rows(grad_result.astype(BF))

    gates, ups, hidden = [], [], []
    for c in range(2):
        gate = mul(two_rows, w_gu[c][:, :ff], NN).astype(BF)
        upward = mul(two_rows, w_gu[c][:, ff:], NN).astype(BF)
        gate32 = gate.astype(F32)
        hid = (gate32 * jax.nn.sigmoid(gate32) * upward.astype(F32)).astype(BF)
        gate, upward, hid = lax.optimization_barrier((gate, upward, hid))
        gates.append(gate)
        ups.append(upward)
        hidden.append(hid)
    product = mul(jnp.concatenate(hidden, axis=1), jnp.concatenate(w_down, axis=1), NT)
    result = middle + after(scatter_rows(product.astype(BF), rows), grad_rows)
    grad_parts = []
    for c in range(2):
        grad_hidden = mul(grad_rows, w_down[c], NN)
        gate32, up32 = gates[c].astype(F32), ups[c].astype(F32)
        sig = jax.nn.sigmoid(gate32)
        grad_gate = (grad_hidden * up32 * sig * (1.0 + gate32 * (1.0 - sig))).astype(BF)
        grad_up = (grad_hidden * gate32 * sig).astype(BF)
        grad_parts.append(jnp.concatenate([grad_gate, grad_up], axis=1))

    def reduce_rows(full):
        return lax.psum_scatter(full.astype(BF), "fsdp", scatter_dimension=0, tiled=True)

    def reduce_parts(terms):
        sums = [reduce_rows(t) for t in terms]
        return sums[OWN].astype(F32) + swap(sums[OTHER], "seg", 1).astype(F32)

    grad_down = reduce_parts([mul(grad_rows, hidden[c], TN) for c in range(2)]).T
    grad_gu = reduce_parts([mul(two_rows, grad_parts[c], TN) for c in range(2)])
    grad_gu = grad_gu.reshape(depth, 2, ff)
    half = seq // 2
    grad_middle, gain_two_terms, mid_blocks = [None, None], [], [None, None]
    for h in (1, 0):
        terms = [mul(grad_parts[c][h * half : (h + 1) * half], w_gu[c], NT) for c in range(2)]
        grad_two = scatter_half((terms[0] + terms[1]).astype(BF), rows)
        if h == 0:
            grad_two = after(grad_two, mid_blocks[1][0])
        grad_resid, gain_term = norm_backward(middle[h], factor_two[h], gain_two, grad_two)
        gain_two_terms.append(gain_term)
        grad_middle[h] = grad_result[h] + grad_resid
        mid_blocks[h] = gather_slots(lax.optimization_barrier(grad_middle[h].astype(BF)), "tp")
    mid_rows = jnp.concatenate(mid_blocks[0] + mid_blocks[1], axis=0)
    raws, qkvo_terms = {}, {}
    for part in reversed(range(len(w_qkvo))):
        grad_mixed = mul(mid_rows, w_qkvo[part][:, cut:], NN).astype(BF)
        raw = attend_back(
            info, qkv[part], mixed[part], reorder(grad_mixed), lse[part], cos_t, sin_t, kernel_group
        )
        raws[part] = reorder(raw)
        term = mul(normed_rows, raws[part], TN).astype(BF)
        out_term = mul(mid_rows, mixed_slots[part], TN).astype(BF)
        qkvo_terms[part] = jnp.concatenate([term, out_term], axis=1)
    if whole_pairs:
        grad_qkv, grad_out = unpaired(reduce_parts([qkvo_terms[0], qkvo_terms[1]]))
    else:
        part_qkv, part_out = unpaired(reduce_rows(qkvo_terms[0]))
        part_qkv, part_out = part_qkv.reshape(depth, 3, SEG, head_cols), part_out.reshape(depth, SEG, head_cols)
        grad_qkv, grad_out = [
            p[..., 0, :].astype(F32) + swap(p[..., 1, :], "seg", 1).astype(F32) for p in (part_qkv, part_out)
        ]
    grad_out = grad_out.T
    weight = jnp.concatenate([w[:, :cut] for w in w_qkvo], axis=1)
    input_grads, gain_terms = [None, None], []
    for h in (1, 0):
        raw = jnp.concatenate([raws[part][h * half : (h + 1) * half] for part in range(len(w_qkvo))], axis=1)
        product = mul(raw, weight, NT).astype(BF)
        grad_one = scatter_half(product, rows)
        if h == 0:
            grad_one = after(grad_one, input_grads[1])
        grad_resid, gain_term = norm_backward(halves[h], factor_one[h], gain_one, grad_one)
        gain_terms.append(gain_term)
        input_grads[h] = (grad_middle[h] + grad_resid).astype(BF)
    input_grad = joined(input_grads[0], swap(input_grads[1], "seg", 1))
    result_live = (result * live).astype(BF)
    outputs = joined(result_live[0], swap(result_live[1], "seg", 1))
    gains = jnp.stack([gain_terms[0] + gain_terms[1], gain_two_terms[0] + gain_two_terms[1]])
    gains = sum_all(gains, ("fsdp", "tp", "seg"))
    gain_one_grad, gain_two_grad = lax.dynamic_slice_in_dim(gains, fsdp * depth, depth, axis=1)
    return (outputs, input_grad, gain_one_grad, grad_qkv, grad_out, gain_two_grad, grad_gu, grad_down)


def solution(mesh):
    fsdp, tp = mesh.devices.shape
    inner = Mesh(mesh.devices.reshape(fsdp, SEG, tp // SEG), ("fsdp", "seg", "tp"))
    act = P(None, "fsdp", ("seg", "tp"), None)
    col = P("fsdp", None, ("seg", "tp"))
    row = P(("seg", "tp"), "fsdp")
    return jax.shard_map(
        layer,
        mesh=inner,
        in_specs=(act, act, P(), P("fsdp"), col, row, P("fsdp"), col, row),
        out_specs=(act, act, P("fsdp"), col, row, P("fsdp"), col, row),
        check_vma=False,
    )
```

profile of v0, /device:TPU:0, one launch (start us, length us, event | category | flops | bytes accessed | tf_op | source)
XLA Modules:
  0.0 1489.6 jit_solution(9236279117069237047)
XLA Ops:
  14.5 45.8 %collective-permute-done.7 = bf16[512,1024]{1,0:T(8,128)(2,1)S(1)} collective-permute-done((bf16[512,1024]{1,0:T(8,128)(2,1)}, bf16[512,1024]{1,0:T(8,128)(2,1)S(1)}, u32[]{:S(2)}, u32[]{:S(2)}) %collective-permute-start.7) | collective-permute-done | bytes 1048608 | tf_op jit(solution)/shard_map/ppermute | solution.py:31
  65.3 92.9 %collective-permute-done.14 = bf16[512,2048]{1,0:T(8,128)(2,1)} collective-permute-done((bf16[512,2048]{1,0:T(8,128)(2,1)}, bf16[512,2048]{1,0:T(8,128)(2,1)}, u32[]{:S(2)}, u32[]{:S(2)}) %collective-permute-start.14) | collective-permute-done | bytes 2097184 | tf_op jit(solution)/shard_map/ppermute | solution.py:31
  158.4 7.9 all-gather.1
  172.5 38.1 %collective-permute-done.2 = bf16[256,2048]{1,0:T(8,128)(2,1)S(1)} collective-permute-done((bf16[256,2048]{1,0:T(8,128)(2,1)}, bf16[256,2048]{1,0:T(8,128)(2,1)S(1)}, u32[]{:S(2)}, u32[]{:S(2)}) %collective-permute-start.2) | collective-permute-done | bytes 1048608 | tf_op jit(solution)/shard_map/ppermute | solution.py:31
  225.3 19.0 %collective-permute-done.5 = bf16[256,2048]{1,0:T(8,128)(2,1)S(1)} collective-permute-done((bf16[256,2048]{1,0:T(8,128)(2,1)}, bf16[256,2048]{1,0:T(8,128)(2,1)S(1)}, u32[]{:S(2)}, u32[]{:S(2)}) %collective-permute-start.5) | collective-permute-done | bytes 1048608 | tf_op jit(solution)/shard_map/ppermute | solution.py:31
  245.6 6.3 fusion.127
  255.1 13.4 qkv_project.2.qkv_ref
  268.5 31.1 %attend.2 = (bf16[2048,256]{1,0:T(8,128)(2,1)}, f32[2,8,2,256]{3,2,1,0:T(2,128)}) custom-call(s32[3]{0:T(128)} %pad_add_fusion.info_ref, bf16[2048,768]{1,0:T(8,128)(2,1)} %qkv_project.2.qkv_ref), custom_call_target="tpu_custom_call" | custom-call | flops 8589934592 | bytes 4194304 | tf_op jit(solution)/shard_map/attend/pallas_call | solution.py:188
  299.6 13.8 qkv_project.3.qkv_ref
  313.4 31.3 %attend.3 = (bf16[2048,256]{1,0:T(8,128)(2,1)}, f32[2,8,2,256]{3,2,1,0:T(2,128)}) custom-call(s32[3]{0:T(128)} %pad_add_fusion.info_ref, bf16[2048,768]{1,0:T(8,128)(2,1)} %qkv_project.3.qkv_ref), custom_call_target="tpu_custom_call" | custom-call | flops 8589934592 | bytes 4194304 | tf_op jit(solution)/shard_map/attend/pallas_call | solution.py:188
  357.2 47.7 %collective-permute-done.19 = bf16[256,2048]{1,0:T(8,128)(2,1)S(1)} collective-permute-done((bf16[256,2048]{1,0:T(8,128)(2,1)S(1)}, bf16[256,2048]{1,0:T(8,128)(2,1)S(1)}, u32[]{:S(2)}, u32[]{:S(2)}) %collective-permute-start.19) | collective-permute-done | bytes 1048608 | tf_op jit(solution)/shard_map/ppermute | solution.py:31
  416.3 105.2 %collective-permute-done.15 = bf16[512,1024]{0,1:T(8,128)(2,1)} collective-permute-done((bf16[512,1024]{0,1:T(8,128)(2,1)S(1)}, bf16[512,1024]{0,1:T(8,128)(2,1)}, u32[]{:S(2)}, u32[]{:S(2)}) %collective-permute-start.15) | collective-permute-done | bytes 1048608 | tf_op jit(solution)/shard_map/ppermute | solution.py:31
  535.0 41.6 %collective-permute-done.12 = bf16[2,256,2048]{2,1,0:T(8,128)(2,1)S(1)} collective-permute-done((bf16[2,256,2048]{2,1,0:T(8,128)(2,1)S(1)}, bf16[2,256,2048]{2,1,0:T(8,128)(2,1)S(1)}, u32[]{:S(2)}, u32[]{:S(2)}) %collective-permute-start.12) | collective-permute-done | bytes 2097184 | tf_op jit(solution)/shard_map/ppermute | solution.py:31
  587.6 12.6 fusion.70
  602.2 14.3 fusion.34
  616.5 13.0 fusion.76
  629.6 15.8 %fusion.33 = (bf16[2048,1024]{1,0:T(8,128)(2,1)}, bf16[2048,1024]{1,0:T(8,128)(2,1)}) fusion(bf16[2048,1024]{1,0:T(8,128)(2,1)S(1)} %fusion.76, bf16[2048,2048]{1,0:T(8,128)(2,1)} %fusion.139, bf16[2048,2048]{1,0:T(8,128)(2,1)S(1)} %copy-done.48), kind=kOutput, calls=%fused_computation.55 | convolution fusion | flops 8608808960 | bytes 25165824 | tf_op jit(solution)/shard_map/dot_general | solution.py:329
  645.4 18.7 %fusion.17 = (bf16[2048,1024]{1,0:T(8,128)(2,1)S(1)}, bf16[2048,1024]{1,0:T(8,128)(2,1)S(1)}) fusion(bf16[2048,1024]{1,0:T(8,128)(2,1)} %copy-done.59, bf16[2048,1024]{1,0:T(8,128)(2,1)} %get-tuple-element.26, bf16[2048,2048]{1,0:T(8,128)(2,1)} %copy-done.28, bf16[2048,1024]{0,1:T(8,128)(2,1)} %all-gather.17.cloned.1.call-done), kind=kOutput, calls=%fused_computation.37 | convolution fusion | flops 8621391872 | bytes 29360128 | tf_op jit(solution)/shard_map/dot_general | solution.py:329
  667.3 13.6 fusion.52
  681.0 20.8 %fusion.25 = (bf16[2048,1024]{1,0:T(8,128)(2,1)}, bf16[2048,1024]{1,0:T(8,128)(2,1)}) fusion(bf16[2048,1024]{1,0:T(8,128)(2,1)} %copy-done.58, bf16[2048,1024]{1,0:T(8,128)(2,1)} %get-tuple-element.28, bf16[2048,2048]{1,0:T(8,128)(2,1)} %copy-done.28, bf16[2048,1024]{0,1:T(8,128)(2,1)} %all-gather.19.cloned.1.call-done), kind=kOutput, calls=%fused_computation.45 | convolution fusion | flops 8621391872 | bytes 29360128 | tf_op jit(solution)/shard_map/dot_general | solution.py:329
  701.8 14.3 add_convert_fusion
  718.7 14.5 fusion.49
  733.2 15.8 %add_convert_fusion.1 = bf16[1024,2048]{1,0:T(8,128)(2,1)} fusion(f32[1024,2048]{1,0:T(8,128)} %fusion.49, bf16[2048,2048]{1,0:T(8,128)(2,1)} %all-gather.15.cloned.1.call-done, bf16[2048,1024]{1,0:T(8,128)(2,1)} %get-tuple-element.85, bf16[2048,1024]{1,0:T(8,128)(2,1)} %get-tuple-element.84), kind=kOutput, calls=%fused_computation.54 | convolution fusion | flops 8602517504 | bytes 29360128 | tf_op jit(solution)/shard_map/dot_general | solution.py:329
  756.1 22.1 %collective-permute-done.29 = bf16[256,2048]{1,0:T(8,128)(2,1)S(1)} collective-permute-done((bf16[256,2048]{1,0:T(8,128)(2,1)S(1)}, bf16[256,2048]{1,0:T(8,128)(2,1)S(1)}, u32[]{:S(2)}, u32[]{:S(2)}) %collective-permute-start.29) | collective-permute-done | bytes 1048608 | tf_op jit(solution)/shard_map/ppermute | solution.py:31
  782.0 18.1 %collective-permute-done.26 = bf16[256,2048]{1,0:T(8,128)(2,1)S(1)} collective-permute-done((bf16[256,2048]{1,0:T(8,128)(2,1)S(1)}, bf16[256,2048]{1,0:T(8,128)(2,1)S(1)}, u32[]{:S(2)}, u32[]{:S(2)}) %collective-permute-start.26) | collective-permute-done | bytes 1048608 | tf_op jit(solution)/shard_map/ppermute | solution.py:31
  806.1 10.9 convolution_convert_fusion.1
  817.1 12.9 collective-permute-done.31
  832.5 19.5 %collective-permute-done.34 = bf16[256,2048]{1,0:T(8,128)(2,1)S(1)} collective-permute-done((bf16[256,2048]{1,0:T(8,128)(2,1)S(1)}, bf16[256,2048]{1,0:T(8,128)(2,1)S(1)}, u32[]{:S(2)}, u32[]{:S(2)}) %collective-permute-start.34) | collective-permute-done | bytes 1048608 | tf_op jit(solution)/shard_map/ppermute | solution.py:31
  864.5 44.2 %attend_back.3 = bf16[2048,768]{1,0:T(8,128)(2,1)} custom-call(s32[3]{0:T(128)} %pad_add_fusion.info_ref, bf16[2048,768]{1,0:T(8,128)(2,1)} %qkv_project.3.qkv_ref, bf16[2048,256]{1,0:T(8,128)(2,1)} %get-tuple-element.22.o_ref, bf16[2048,256]{1,0:T(8,128)(2,1)} %convolution_convert_fusion.7.do_ref, f32[2,8,2,256]{3,2,1,0:T(2,128)} %get-tuple-element.32.lse_ref, ...), custom_call_target="tpu_custom_call" | custom-call | flops 21474836480 | bytes 8388608 | tf_op jit(solution)/shard_map/attend_back/pallas_call | solution.py:287
  908.7 10.2 convolution_convert_fusion.3
  921.3 23.8 %fusion.36 = bf16[2048,2048]{1,0:T(8,128)(2,1)} fusion(bf16[2048,2048]{1,0:T(8,128)(2,1)} %fusion.139, bf16[2048,1024]{1,0:T(8,128)(2,1)} %get-tuple-element.84, bf16[2048,1024]{1,0:T(8,128)(2,1)} %get-tuple-element.85), kind=kOutput, calls=%fused_computation.58 | convolution fusion | flops 17200840704 | bytes 25165824 | tf_op jit(solution)/shard_map/dot_general | solution.py:329
  945.2 14.1 convolution_convert_fusion.2
  966.6 6.8 convolution_convert_fusion.8.do_ref
  973.4 44.2 %attend_back.2 = bf16[2048,768]{1,0:T(8,128)(2,1)} custom-call(s32[3]{0:T(128)} %pad_add_fusion.info_ref, bf16[2048,768]{1,0:T(8,128)(2,1)} %qkv_project.2.qkv_ref, bf16[2048,256]{1,0:T(8,128)(2,1)} %get-tuple-element.21.o_ref, bf16[2048,256]{1,0:T(8,128)(2,1)} %convolution_convert_fusion.8.do_ref, f32[2,8,2,256]{3,2,1,0:T(2,128)} %get-tuple-element.31.lse_ref, ...), custom_call_target="tpu_custom_call" | custom-call | flops 21474836480 | bytes 8388608 | tf_op jit(solution)/shard_map/attend_back/pallas_call | solution.py:287
  1017.6 10.4 convolution_convert_fusion.4
  1030.6 22.4 %fusion.37 = bf16[2048,2048]{1,0:T(8,128)(2,1)S(1)} fusion(bf16[2048,1024]{0,1:T(8,128)(2,1)} %all-gather.19.cloned.1.call-done, bf16[2048,1024]{0,1:T(8,128)(2,1)} %all-gather.17.cloned.1.call-done, bf16[2048,1024]{1,0:T(8,128)(2,1)} %get-tuple-element.24, bf16[2048,1024]{1,0:T(8,128)(2,1)} %get-tuple-element.23), kind=kOutput, calls=%fused_computation.59 | convolution fusion | flops 17217617920 | bytes 25165824 | tf_op jit(solution)/shard_map/dot_general | solution.py:329
  1061.0 22.2 %fusion.35 = bf16[2048,2048]{1,0:T(8,128)(2,1)} fusion(bf16[2048,2048]{1,0:T(8,128)(2,1)} %fusion.139, bf16[2048,1024]{1,0:T(8,128)(2,1)S(1)} %copy-done.54, bf16[2048,1024]{1,0:T(8,128)(2,1)S(1)} %copy-done.56), kind=kOutput, calls=%fused_computation.57 | convolution fusion | flops 17200840704 | bytes 25165824 | tf_op jit(solution)/shard_map/dot_general | solution.py:329
  1089.3 44.8 %collective-permute-done.18 = bf16[2,256,2048]{2,1,0:T(8,128)(2,1)S(1)} collective-permute-done((bf16[2,256,2048]{2,1,0:T(8,128)(2,1)S(1)}, bf16[2,256,2048]{2,1,0:T(8,128)(2,1)S(1)}, u32[]{:S(2)}, u32[]{:S(2)}) %collective-permute-start.18) | collective-permute-done | bytes 2097184 | tf_op jit(solution)/shard_map/ppermute | solution.py:31
  1139.0 7.1 fusion.69
  1147.4 6.9 fusion.68
  1161.0 31.5 %collective-permute-done.41 = bf16[256,2048]{1,0:T(8,128)(2,1)S(1)} collective-permute-done((bf16[256,2048]{1,0:T(8,128)(2,1)S(1)}, bf16[256,2048]{1,0:T(8,128)(2,1)S(1)}, u32[]{:S(2)}, u32[]{:S(2)}) %collective-permute-start.41) | collective-permute-done | bytes 1048608 | tf_op jit(solution)/shard_map/ppermute | solution.py:31
  1194.1 32.0 %collective-permute-done.38 = bf16[256,2048]{1,0:T(8,128)(2,1)S(1)} collective-permute-done((bf16[256,2048]{1,0:T(8,128)(2,1)S(1)}, bf16[256,2048]{1,0:T(8,128)(2,1)S(1)}, u32[]{:S(2)}, u32[]{:S(2)}) %collective-permute-start.38) | collective-permute-done | bytes 1048608 | tf_op jit(solution)/shard_map/ppermute | solution.py:31
  1246.1 20.9 %collective-permute-done.46 = f32[2,2048]{1,0:T(2,128)S(1)} collective-permute-done((f32[2,2048]{1,0:T(2,128)S(1)}, f32[2,2048]{1,0:T(2,128)S(1)}, u32[]{:S(2)}, u32[]{:S(2)}) %collective-permute-start.46) | collective-permute-done | bytes 16416 | tf_op jit(solution)/shard_map/ppermute | solution.py:31
  1276.5 104.7 %collective-permute-done.47 = f32[2,2048]{1,0:T(2,128)S(1)} collective-permute-done((f32[2,2048]{1,0:T(2,128)S(1)}, f32[2,2048]{1,0:T(2,128)S(1)}, u32[]{:S(2)}, u32[]{:S(2)}) %collective-permute-start.47) | collective-permute-done | bytes 16416 | tf_op jit(solution)/shard_map/ppermute | solution.py:31
  1383.5 20.3 %collective-permute-done.50 = bf16[512,1024]{1,0:T(8,128)(2,1)} collective-permute-done((bf16[512,1024]{1,0:T(8,128)(2,1)}, bf16[512,1024]{1,0:T(8,128)(2,1)}, u32[]{:S(2)}, u32[]{:S(2)}) %collective-permute-start.50) | collective-permute-done | bytes 1048608 | tf_op jit(solution)/shard_map/ppermute | solution.py:31
  1407.6 18.7 %collective-permute-done.48 = bf16[512,1024]{0,1:T(8,128)(2,1)} collective-permute-done((bf16[512,1024]{0,1:T(8,128)(2,1)}, bf16[512,1024]{0,1:T(8,128)(2,1)}, u32[]{:S(2)}, u32[]{:S(2)}) %collective-permute-start.48) | collective-permute-done | bytes 1048608 | tf_op jit(solution)/shard_map/ppermute | solution.py:31
  1437.2 33.6 %collective-permute-done.49 = bf16[512,2048]{1,0:T(8,128)(2,1)} collective-permute-done((bf16[512,2048]{1,0:T(8,128)(2,1)}, bf16[512,2048]{1,0:T(8,128)(2,1)}, u32[]{:S(2)}, u32[]{:S(2)}) %collective-permute-start.49) | collective-permute-done | bytes 2097184 | tf_op jit(solution)/shard_map/ppermute | solution.py:31
  1475.8 6.6 reshape.491
  (377 shorter events, 217.3 us)
Async XLA Ops:
  7.2 248.0 %all-gather.9.cloned.1.call-start = ((), (), s32[]{:S(2)}) async-start(), calls=%async_computation.6 | async-start | bytes 5242880 | tf_op jit(solution)/shard_map/all_gather | solution.py:359
  10.3 289.3 %all-gather.11.cloned.1.call-start = ((), (), s32[]{:S(2)}) async-start(), calls=%async_computation.7 | async-start | bytes 5242880 | tf_op jit(solution)/shard_map/all_gather | solution.py:359
  10.4 50.0 %collective-permute-start.7 = (bf16[512,1024]{1,0:T(8,128)(2,1)}, bf16[512,1024]{1,0:T(8,128)(2,1)S(1)}, u32[]{:S(2)}, u32[]{:S(2)}) collective-permute-start(bf16[512,1024]{1,0:T(8,128)(2,1)} %pad_maximum_fusion.17), channel_id=1, source_target_pairs={{0,4},{4,0},{1,5},{5,1},{2,6},{6,2},{3,7},{7,3},{8,12},{12,8},{9,1... | collective-permute-start | bytes 3145736 | tf_op jit(solution)/shard_map/ppermute | solution.py:31
  61.3 526.3 %all-gather.13.cloned.1.call-start = ((), (), s32[]{:S(2)}) async-start(), calls=%async_computation.8 | async-start | bytes 10485760 | tf_op jit(solution)/shard_map/all_gather | solution.py:359
  65.2 551.4 %all-gather.15.cloned.1.call-start = ((), (), s32[]{:S(2)}) async-start(), calls=%async_computation.9 | async-start | bytes 10485760 | tf_op jit(solution)/shard_map/all_gather | solution.py:359
  65.2 93.0 %collective-permute-start.14 = (bf16[512,2048]{1,0:T(8,128)(2,1)}, bf16[512,2048]{1,0:T(8,128)(2,1)}, u32[]{:S(2)}, u32[]{:S(2)}) collective-permute-start(bf16[512,2048]{1,0:T(8,128)(2,1)} %bitcast.261), channel_id=1, source_target_pairs={{0,4},{4,0},{1,5},{5,1},{2,6},{6,2},{3,7},{7,3},{8,12},{12,8},{9,1... | collective-permute-start | bytes 6291464 | tf_op jit(solution)/shard_map/ppermute | solution.py:31
  158.2 487.1 %all-gather.17.cloned.1.call-start = ((), (), s32[]{:S(2)}) async-start(), calls=%async_computation.10 | async-start | bytes 5242880 | tf_op jit(solution)/shard_map/all_gather | solution.py:359
  168.8 41.8 %collective-permute-start.2 = (bf16[256,2048]{1,0:T(8,128)(2,1)}, bf16[256,2048]{1,0:T(8,128)(2,1)S(1)}, u32[]{:S(2)}, u32[]{:S(2)}) collective-permute-start(bf16[256,2048]{1,0:T(8,128)(2,1)} %get-tuple-element.83), channel_id=1, source_target_pairs={{0,2},{1,3},{2,0},{3,1},{4,6},{5,7},{6,4},{7,5},{8,10},{9,11},{10,... | collective-permute-start | bytes 3145736 | tf_op jit(solution)/shard_map/ppermute | solution.py:31
  170.8 45.6 %collective-permute-start = (bf16[256,2048]{1,0:T(8,128)(2,1)}, bf16[256,2048]{1,0:T(8,128)(2,1)S(1)}, u32[]{:S(2)}, u32[]{:S(2)}) collective-permute-start(bf16[256,2048]{1,0:T(8,128)(2,1)} %get-tuple-element.111), channel_id=1, source_target_pairs={{0,4},{4,0},{1,5},{5,1},{2,6},{6,2},{3,7},{7,3},{8,12},{12,8},{9,1... | collective-permute-start | bytes 3145736 | tf_op jit(solution)/shard_map/ppermute | solution.py:31
  172.5 44.8 %collective-permute-start.1 = (bf16[256,2048]{1,0:T(8,128)(2,1)}, bf16[256,2048]{1,0:T(8,128)(2,1)}, u32[]{:S(2)}, u32[]{:S(2)}) collective-permute-start(bf16[256,2048]{1,0:T(8,128)(2,1)} %get-tuple-element.83), channel_id=1, source_target_pairs={{0,1},{1,0},{2,3},{3,2},{4,5},{5,4},{6,7},{7,6},{8,9},{9,8},{10,11... | collective-permute-start | bytes 3145736 | tf_op jit(solution)/shard_map/ppermute | solution.py:31
  210.6 470.3 %all-gather.19.cloned.1.call-start = ((), (), s32[]{:S(2)}) async-start(), calls=%async_computation.11 | async-start | bytes 5242880 | tf_op jit(solution)/shard_map/all_gather | solution.py:359
  225.1 26.8 %collective-permute-start.4 = (bf16[256,2048]{1,0:T(8,128)(2,1)}, bf16[256,2048]{1,0:T(8,128)(2,1)S(1)}, u32[]{:S(2)}, u32[]{:S(2)}) collective-permute-start(bf16[256,2048]{1,0:T(8,128)(2,1)} %get-tuple-element.81), channel_id=1, source_target_pairs={{0,1},{1,0},{2,3},{3,2},{4,5},{5,4},{6,7},{7,6},{8,9},{9,8},{10,11... | collective-permute-start | bytes 3145736 | tf_op jit(solution)/shard_map/ppermute | solution.py:31
  355.8 53.8 %collective-permute-start.9 = (bf16[2,256,2048]{2,1,0:T(8,128)(2,1)}, bf16[2,256,2048]{2,1,0:T(8,128)(2,1)}, u32[]{:S(2)}, u32[]{:S(2)}) collective-permute-start(bf16[2,256,2048]{2,1,0:T(8,128)(2,1)} %get-tuple-element.91), channel_id=1, source_target_pairs={{0,1},{1,0},{2,3},{3,2},{4,5},{5,4},{6,7},{7,6},{8,9},{9,8},{10,11... | collective-permute-start | bytes 6291464 | tf_op jit(solution)/shard_map/ppermute | solution.py:31
  356.4 48.5 %collective-permute-start.19 = (bf16[256,2048]{1,0:T(8,128)(2,1)S(1)}, bf16[256,2048]{1,0:T(8,128)(2,1)S(1)}, u32[]{:S(2)}, u32[]{:S(2)}) collective-permute-start(bf16[256,2048]{1,0:T(8,128)(2,1)S(1)} %get-tuple-element.109), channel_id=1, source_target_pairs={{0,4},{4,0},{1,5},{5,1},{2,6},{6,2},{3,7},{7,3},{8,12},{12,8},{9,1... | collective-permute-start | bytes 3145736 | tf_op jit(solution)/shard_map/ppermute | solution.py:31
  409.6 112.1 %collective-permute-start.21 = (bf16[2,256,2048]{2,1,0:T(8,128)(2,1)S(1)}, bf16[2,256,2048]{2,1,0:T(8,128)(2,1)}, u32[]{:S(2)}, u32[]{:S(2)}) collective-permute-start(bf16[2,256,2048]{2,1,0:T(8,128)(2,1)S(1)} %get-tuple-element.105), channel_id=1, source_target_pairs={{0,2},{1,3},{2,0},{3,1},{4,6},{5,7},{6,4},{7,5},{8,10},{9,11},{10,... | collective-permute-start | bytes 6291464 | tf_op jit(solution)/shard_map/ppermute | solution.py:31
  409.6 112.2 %collective-permute-start.8 = (bf16[2,256,2048]{2,1,0:T(8,128)(2,1)}, bf16[2,256,2048]{2,1,0:T(8,128)(2,1)}, u32[]{:S(2)}, u32[]{:S(2)}) collective-permute-start(bf16[2,256,2048]{2,1,0:T(8,128)(2,1)} %get-tuple-element.90), channel_id=1, source_target_pairs={{0,1},{1,0},{2,3},{3,2},{4,5},{5,4},{6,7},{7,6},{8,9},{9,8},{10,11... | collective-permute-start | bytes 6291464 | tf_op jit(solution)/shard_map/ppermute | solution.py:31
  414.1 109.6 %collective-permute-start.10 = (bf16[2,256,2048]{2,1,0:T(8,128)(2,1)}, bf16[2,256,2048]{2,1,0:T(8,128)(2,1)}, u32[]{:S(2)}, u32[]{:S(2)}) collective-permute-start(bf16[2,256,2048]{2,1,0:T(8,128)(2,1)} %fusion.64), channel_id=1, source_target_pairs={{0,2},{1,3},{2,0},{3,1},{4,6},{5,7},{6,4},{7,5},{8,10},{9,11},{10,... | collective-permute-start | bytes 6291464 | tf_op jit(solution)/shard_map/ppermute | solution.py:31
  416.1 105.4 %collective-permute-start.15 = (bf16[512,1024]{0,1:T(8,128)(2,1)S(1)}, bf16[512,1024]{0,1:T(8,128)(2,1)}, u32[]{:S(2)}, u32[]{:S(2)}) collective-permute-start(bf16[512,1024]{0,1:T(8,128)(2,1)S(1)} %bitcast.269), channel_id=1, source_target_pairs={{0,4},{4,0},{1,5},{5,1},{2,6},{6,2},{3,7},{7,3},{8,12},{12,8},{9,1... | collective-permute-start | bytes 3145736 | tf_op jit(solution)/shard_map/ppermute | solution.py:31
  416.1 114.2 %collective-permute-start.20 = (bf16[2,256,2048]{2,1,0:T(8,128)(2,1)S(1)}, bf16[2,256,2048]{2,1,0:T(8,128)(2,1)}, u32[]{:S(2)}, u32[]{:S(2)}) collective-permute-start(bf16[2,256,2048]{2,1,0:T(8,128)(2,1)S(1)} %get-tuple-element.105), channel_id=1, source_target_pairs={{0,1},{1,0},{2,3},{3,2},{4,5},{5,4},{6,7},{7,6},{8,9},{9,8},{10,11... | collective-permute-start | bytes 6291464 | tf_op jit(solution)/shard_map/ppermute | solution.py:31
  521.5 749.2 %reduce-scatter.17.cloned.1.call-start = ((), (), s32[]{:S(2)}) async-start(), calls=%async_computation.17 | async-start | bytes 5242880 | tf_op jit(solution)/shard_map/reduce_scatter | solution.py:476
  529.0 47.6 %collective-permute-start.12 = (bf16[2,256,2048]{2,1,0:T(8,128)(2,1)S(1)}, bf16[2,256,2048]{2,1,0:T(8,128)(2,1)S(1)}, u32[]{:S(2)}, u32[]{:S(2)}) collective-permute-start(bf16[2,256,2048]{2,1,0:T(8,128)(2,1)S(1)} %multiply_convert_fusion.1), channel_id=1, source_target_pairs={{0,2},{1,3},{2,0},{3,1},{4,6},{5,7},{6,4},{7,5},{8,10},{9,11},{10,... | collective-permute-start | bytes 6291464 | tf_op jit(solution)/shard_map/ppermute | solution.py:31
  533.3 45.8 %collective-permute-start.11 = (bf16[2,256,2048]{2,1,0:T(8,128)(2,1)S(1)}, bf16[2,256,2048]{2,1,0:T(8,128)(2,1)S(1)}, u32[]{:S(2)}, u32[]{:S(2)}) collective-permute-start(bf16[2,256,2048]{2,1,0:T(8,128)(2,1)S(1)} %multiply_convert_fusion.1), channel_id=1, source_target_pairs={{0,1},{1,0},{2,3},{3,2},{4,5},{5,4},{6,7},{7,6},{8,9},{9,8},{10,11... | collective-permute-start | bytes 6291464 | tf_op jit(solution)/shard_map/ppermute | solution.py:31
  717.3 34.3 %collective-permute-start.28 = (bf16[256,2048]{1,0:T(8,128)(2,1)}, bf16[256,2048]{1,0:T(8,128)(2,1)S(1)}, u32[]{:S(2)}, u32[]{:S(2)}) collective-permute-start(bf16[256,2048]{1,0:T(8,128)(2,1)} %get-tuple-element.99), channel_id=1, source_target_pairs={{0,1},{1,0},{2,3},{3,2},{4,5},{5,4},{6,7},{7,6},{8,9},{9,8},{10,11... | collective-permute-start | bytes 3145736 | tf_op jit(solution)/shard_map/ppermute | solution.py:31
  752.1 26.1 %collective-permute-start.29 = (bf16[256,2048]{1,0:T(8,128)(2,1)S(1)}, bf16[256,2048]{1,0:T(8,128)(2,1)S(1)}, u32[]{:S(2)}, u32[]{:S(2)}) collective-permute-start(bf16[256,2048]{1,0:T(8,128)(2,1)S(1)} %add_convert_fusion.6), channel_id=1, source_target_pairs={{0,2},{1,3},{2,0},{3,1},{4,6},{5,7},{6,4},{7,5},{8,10},{9,11},{10,... | collective-permute-start | bytes 3145736 | tf_op jit(solution)/shard_map/ppermute | solution.py:31
  753.9 28.1 %collective-permute-start.24 = (bf16[256,2048]{1,0:T(8,128)(2,1)S(1)}, bf16[256,2048]{1,0:T(8,128)(2,1)S(1)}, u32[]{:S(2)}, u32[]{:S(2)}) collective-permute-start(bf16[256,2048]{1,0:T(8,128)(2,1)S(1)} %get-tuple-element.96), channel_id=1, source_target_pairs={{0,1},{1,0},{2,3},{3,2},{4,5},{5,4},{6,7},{7,6},{8,9},{9,8},{10,11... | collective-permute-start | bytes 3145736 | tf_op jit(solution)/shard_map/ppermute | solution.py:31
  754.6 45.6 %collective-permute-start.26 = (bf16[256,2048]{1,0:T(8,128)(2,1)S(1)}, bf16[256,2048]{1,0:T(8,128)(2,1)S(1)}, u32[]{:S(2)}, u32[]{:S(2)}) collective-permute-start(bf16[256,2048]{1,0:T(8,128)(2,1)S(1)} %add_convert_fusion.8), channel_id=1, source_target_pairs={{0,2},{1,3},{2,0},{3,1},{4,6},{5,7},{6,4},{7,5},{8,10},{9,11},{10,... | collective-permute-start | bytes 3145736 | tf_op jit(solution)/shard_map/ppermute | solution.py:31
  803.9 48.1 %collective-permute-start.30 = (bf16[256,2048]{1,0:T(8,128)(2,1)S(1)}, bf16[256,2048]{1,0:T(8,128)(2,1)}, u32[]{:S(2)}, u32[]{:S(2)}) collective-permute-start(bf16[256,2048]{1,0:T(8,128)(2,1)S(1)} %get-tuple-element.74), channel_id=1, source_target_pairs={{0,1},{1,0},{2,3},{3,2},{4,5},{5,4},{6,7},{7,6},{8,9},{9,8},{10,11... | collective-permute-start | bytes 3145736 | tf_op jit(solution)/shard_map/ppermute | solution.py:31
  803.9 26.1 %collective-permute-start.31 = (bf16[256,2048]{1,0:T(8,128)(2,1)S(1)}, bf16[256,2048]{1,0:T(8,128)(2,1)}, u32[]{:S(2)}, u32[]{:S(2)}) collective-permute-start(bf16[256,2048]{1,0:T(8,128)(2,1)S(1)} %get-tuple-element.74), channel_id=1, source_target_pairs={{0,2},{1,3},{2,0},{3,1},{4,6},{5,7},{6,4},{7,5},{8,10},{9,11},{10,... | collective-permute-start | bytes 3145736 | tf_op jit(solution)/shard_map/ppermute | solution.py:31
  805.7 46.3 %collective-permute-start.34 = (bf16[256,2048]{1,0:T(8,128)(2,1)S(1)}, bf16[256,2048]{1,0:T(8,128)(2,1)S(1)}, u32[]{:S(2)}, u32[]{:S(2)}) collective-permute-start(bf16[256,2048]{1,0:T(8,128)(2,1)S(1)} %get-tuple-element.76), channel_id=1, source_target_pairs={{0,2},{1,3},{2,0},{3,1},{4,6},{5,7},{6,4},{7,5},{8,10},{9,11},{10,... | collective-permute-start | bytes 3145736 | tf_op jit(solution)/shard_map/ppermute | solution.py:31
  817.1 453.7 %reduce-scatter.9.cloned.1.call-start = ((), (), s32[]{:S(2)}) async-start(), calls=%async_computation.13 | async-start | bytes 5242880 | tf_op jit(solution)/shard_map/reduce_scatter | solution.py:476
  830.1 24.5 %collective-permute-start.32 = (bf16[256,2048]{1,0:T(8,128)(2,1)}, bf16[256,2048]{1,0:T(8,128)(2,1)S(1)}, u32[]{:S(2)}, u32[]{:S(2)}) collective-permute-start(bf16[256,2048]{1,0:T(8,128)(2,1)} %collective-permute-done.31), channel_id=1, source_target_pairs={{0,1},{1,0},{2,3},{3,2},{4,5},{5,4},{6,7},{7,6},{8,9},{9,8},{10,11... | collective-permute-start | bytes 3145736 | tf_op jit(solution)/shard_map/ppermute | solution.py:31
  831.9 22.9 %collective-permute-start.33 = (bf16[256,2048]{1,0:T(8,128)(2,1)S(1)}, bf16[256,2048]{1,0:T(8,128)(2,1)S(1)}, u32[]{:S(2)}, u32[]{:S(2)}) collective-permute-start(bf16[256,2048]{1,0:T(8,128)(2,1)S(1)} %get-tuple-element.76), channel_id=1, source_target_pairs={{0,1},{1,0},{2,3},{3,2},{4,5},{5,4},{6,7},{7,6},{8,9},{9,8},{10,11... | collective-permute-start | bytes 3145736 | tf_op jit(solution)/shard_map/ppermute | solution.py:31
  921.3 352.3 %reduce-scatter.13.cloned.1.call-start = ((), (), s32[]{:S(2)}) async-start(), calls=%async_computation.15 | async-start | bytes 10485760 | tf_op jit(solution)/shard_map/reduce_scatter | solution.py:476
  945.1 438.4 %reduce-scatter.15.cloned.1.call-start = ((), (), s32[]{:S(2)}) async-start(), calls=%async_computation.16 | async-start | bytes 5242880 | tf_op jit(solution)/shard_map/reduce_scatter | solution.py:476
  959.3 448.3 %reduce-scatter.7.cloned.1.call-start = ((), (), s32[]{:S(2)}) async-start(), calls=%async_computation.12 | async-start | bytes 5242880 | tf_op jit(solution)/shard_map/reduce_scatter | solution.py:476
  1030.6 406.6 %reduce-scatter.11.cloned.1.call-start = ((), (), s32[]{:S(2)}) async-start(), calls=%async_computation.14 | async-start | bytes 10485760 | tf_op jit(solution)/shard_map/reduce_scatter | solution.py:476
  1059.3 24.2 %collective-permute-start.17 = (bf16[2,256,2048]{2,1,0:T(8,128)(2,1)}, bf16[2,256,2048]{2,1,0:T(8,128)(2,1)S(1)}, u32[]{:S(2)}, u32[]{:S(2)}) collective-permute-start(bf16[2,256,2048]{2,1,0:T(8,128)(2,1)} %get-tuple-element.89), channel_id=1, source_target_pairs={{0,1},{1,0},{2,3},{3,2},{4,5},{5,4},{6,7},{7,6},{8,9},{9,8},{10,11... | collective-permute-start | bytes 6291464 | tf_op jit(solution)/shard_map/ppermute | solution.py:31
  1086.3 47.8 %collective-permute-start.18 = (bf16[2,256,2048]{2,1,0:T(8,128)(2,1)S(1)}, bf16[2,256,2048]{2,1,0:T(8,128)(2,1)S(1)}, u32[]{:S(2)}, u32[]{:S(2)}) collective-permute-start(bf16[2,256,2048]{2,1,0:T(8,128)(2,1)S(1)} %fusion.62), channel_id=1, source_target_pairs={{0,2},{1,3},{2,0},{3,1},{4,6},{5,7},{6,4},{7,5},{8,10},{9,11},{10,... | collective-permute-start | bytes 6291464 | tf_op jit(solution)/shard_map/ppermute | solution.py:31
  1155.6 36.9 %collective-permute-start.41 = (bf16[256,2048]{1,0:T(8,128)(2,1)S(1)}, bf16[256,2048]{1,0:T(8,128)(2,1)S(1)}, u32[]{:S(2)}, u32[]{:S(2)}) collective-permute-start(bf16[256,2048]{1,0:T(8,128)(2,1)S(1)} %add_convert_fusion.2), channel_id=1, source_target_pairs={{0,2},{1,3},{2,0},{3,1},{4,6},{5,7},{6,4},{7,5},{8,10},{9,11},{10,... | collective-permute-start | bytes 3145736 | tf_op jit(solution)/shard_map/ppermute | solution.py:31
  1157.9 36.1 %collective-permute-start.36 = (bf16[256,2048]{1,0:T(8,128)(2,1)S(1)}, bf16[256,2048]{1,0:T(8,128)(2,1)S(1)}, u32[]{:S(2)}, u32[]{:S(2)}) collective-permute-start(bf16[256,2048]{1,0:T(8,128)(2,1)S(1)} %get-tuple-element.92), channel_id=1, source_target_pairs={{0,1},{1,0},{2,3},{3,2},{4,5},{5,4},{6,7},{7,6},{8,9},{9,8},{10,11... | collective-permute-start | bytes 3145736 | tf_op jit(solution)/shard_map/ppermute | solution.py:31
  1158.5 67.6 %collective-permute-start.38 = (bf16[256,2048]{1,0:T(8,128)(2,1)S(1)}, bf16[256,2048]{1,0:T(8,128)(2,1)S(1)}, u32[]{:S(2)}, u32[]{:S(2)}) collective-permute-start(bf16[256,2048]{1,0:T(8,128)(2,1)S(1)} %add_convert_fusion.4), channel_id=1, source_target_pairs={{0,2},{1,3},{2,0},{3,1},{4,6},{5,7},{6,4},{7,5},{8,10},{9,11},{10,... | collective-permute-start | bytes 3145736 | tf_op jit(solution)/shard_map/ppermute | solution.py:31
  1161.0 76.8 %collective-permute-start.23 = (bf16[256,2048]{1,0:T(8,128)(2,1)}, bf16[256,2048]{1,0:T(8,128)(2,1)}, u32[]{:S(2)}, u32[]{:S(2)}) collective-permute-start(bf16[256,2048]{1,0:T(8,128)(2,1)} %get-tuple-element.107), channel_id=1, source_target_pairs={{0,4},{4,0},{1,5},{5,1},{2,6},{6,2},{3,7},{7,3},{8,12},{12,8},{9,1... | collective-permute-start | bytes 3145736 | tf_op jit(solution)/shard_map/ppermute | solution.py:31
  1241.0 140.8 %collective-permute-start.42 = (bf16[256,2048]{1,0:T(8,128)(2,1)}, bf16[256,2048]{1,0:T(8,128)(2,1)S(1)}, u32[]{:S(2)}, u32[]{:S(2)}) collective-permute-start(bf16[256,2048]{1,0:T(8,128)(2,1)} %fusion.113), channel_id=1, source_target_pairs={{0,4},{4,0},{1,5},{5,1},{2,6},{6,2},{3,7},{7,3},{8,12},{12,8},{9,1... | collective-permute-start | bytes 3145736 | tf_op jit(solution)/shard_map/ppermute | solution.py:31
  1243.4 23.7 %collective-permute-start.46 = (f32[2,2048]{1,0:T(2,128)S(1)}, f32[2,2048]{1,0:T(2,128)S(1)}, u32[]{:S(2)}, u32[]{:S(2)}) collective-permute-start(f32[2,2048]{1,0:T(2,128)S(1)} %add.348), channel_id=1, source_target_pairs={{0,2},{1,3},{2,0},{3,1},{4,6},{5,7},{6,4},{7,5},{8,10},{9,11},{10,... | collective-permute-start | bytes 49160 | tf_op jit(solution)/shard_map/ppermute | solution.py:31
  1267.1 114.2 %collective-permute-start.47 = (f32[2,2048]{1,0:T(2,128)S(1)}, f32[2,2048]{1,0:T(2,128)S(1)}, u32[]{:S(2)}, u32[]{:S(2)}) collective-permute-start(f32[2,2048]{1,0:T(2,128)S(1)} %add.349), channel_id=1, source_target_pairs={{0,4},{4,0},{1,5},{5,1},{2,6},{6,2},{3,7},{7,3},{8,12},{12,8},{9,1... | collective-permute-start | bytes 49160 | tf_op jit(solution)/shard_map/ppermute | solution.py:31
  1270.7 133.2 %collective-permute-start.50 = (bf16[512,1024]{1,0:T(8,128)(2,1)}, bf16[512,1024]{1,0:T(8,128)(2,1)}, u32[]{:S(2)}, u32[]{:S(2)}) collective-permute-start(bf16[512,1024]{1,0:T(8,128)(2,1)} %reduce-scatter.17.cloned.1.call-done), channel_id=1, source_target_pairs={{0,4},{4,0},{1,5},{5,1},{2,6},{6,2},{3,7},{7,3},{8,12},{12,8},{9,1... | collective-permute-start | bytes 3145736 | tf_op jit(solution)/shard_map/ppermute | solution.py:31
  1270.8 155.5 %collective-permute-start.48 = (bf16[512,1024]{0,1:T(8,128)(2,1)}, bf16[512,1024]{0,1:T(8,128)(2,1)}, u32[]{:S(2)}, u32[]{:S(2)}) collective-permute-start(bf16[512,1024]{0,1:T(8,128)(2,1)} %reduce-scatter.9.cloned.1.call-done), channel_id=1, source_target_pairs={{0,4},{4,0},{1,5},{5,1},{2,6},{6,2},{3,7},{7,3},{8,12},{12,8},{9,1... | collective-permute-start | bytes 3145736 | tf_op jit(solution)/shard_map/ppermute | solution.py:31
  1273.6 197.2 %collective-permute-start.49 = (bf16[512,2048]{1,0:T(8,128)(2,1)}, bf16[512,2048]{1,0:T(8,128)(2,1)}, u32[]{:S(2)}, u32[]{:S(2)}) collective-permute-start(bf16[512,2048]{1,0:T(8,128)(2,1)} %reduce-scatter.13.cloned.1.call-done), channel_id=1, source_target_pairs={{0,4},{4,0},{1,5},{5,1},{2,6},{6,2},{3,7},{7,3},{8,12},{12,8},{9,1... | collective-permute-start | bytes 6291464 | tf_op jit(solution)/shard_map/ppermute | solution.py:31
  (79 other events, 1733.2 us)
Sparse Core Ops, SparseCore 0:
  10.4 55.2 all-gather.8
  68.2 52.5 all-gather.10
  122.6 87.4 all-gather.12
  211.9 87.4 all-gather.14
  301.1 52.4 all-gather.16
  521.6 55.4 all-gather.18
  817.2 54.1 reduce-scatter.16
  921.4 54.1 reduce-scatter.8
  978.6 86.2 reduce-scatter.12
  1067.8 52.6 reduce-scatter.14
  1123.4 52.5 reduce-scatter.6
  1179.0 86.6 reduce-scatter.10
where the time goes:
time: 1500 us; the launch traced here: 1490 us
  waiting for transfers between devices  783 us (52%)
  matrix products  306 us (20%)
  Pallas kernels  178 us (12%)
  local copies, waits for them, and re-layouts  86.3 us (6%)
  other arithmetic  74.4 us (5%)
  starting transfers between devices  37.6 us (3%)
  between operations  15.8 us (1%)
    ppermute x51, waiting for transfers between devices, swap(): return lax.ppermute(x, axis, [(i, i ^ bit) for i in range(size)])  783 us
    dot_general x24, matrix products, mul(): return lax.dot_general(a, b, (dims, ((), ())), preferred_element_type=F32)  306 us
    pallas_call x2, Pallas kernels, attend_back(): pl.pallas_call(functools.partial(attend_back_kernel, group), grid_spec=pl...  88.4 us
    pallas_call x2, Pallas kernels, attend(): pl.pallas_call(functools.partial(attend_kernel, group), grid_spec=pltpu.P...  62.4 us
    unnamed x155, local copies, waits for them, and re-layouts  55.5 us
    ppermute x51, starting transfers between devices, swap(): return lax.ppermute(x, axis, [(i, i ^ bit) for i in range(size)])  37.1 us
  transfers between devices with their start and end apart: 63, of which 23 were waited for; matrix products, arithmetic and copies ran while one was open for 26% of the time, Pallas kernels for 12%

commit v1 on v0

--- a/solution.py
+++ b/solution.py
@@ -427,24 +427,34 @@
 
     halves = [x_mine.astype(F32), x_got.astype(F32)]
     blocks, factor_one = [], []
-    for x in halves:
+    for h, x in enumerate(halves):
+        if h == 1:
+            x = halves[1] = after(x_got, blocks[0][0]).astype(F32)
         normed, factor = norm_forward(x, gain_one)
-        blocks.append(gather_slots(normed.astype(BF), "tp"))
+        normed = lax.optimization_barrier(normed.astype(BF))
+        blocks.append(gather_slots(normed, "tp"))
         factor_one.append(factor)
     normed_rows = jnp.concatenate(blocks[0] + blocks[1], axis=0)
-    residual = jnp.stack(halves)
     qkv, mixed, lse = [], [], []
     for part, weight in enumerate(w_qkvo):
-        projected = qkv_project(normed_rows, weight, cos_tab, sin_a, sin_b)
-        qkv.append(reorder(projected))
+        qkv_rows = qkv_project(normed_rows, weight, cos_tab, sin_a, sin_b)
+        qkv.append(reorder(qkv_rows))
         outs = attend(info, qkv[part], kernel_group)
         mixed.append(outs[0])
         lse.append(outs[1])
     mixed_slots = [reorder(m) for m in mixed]
-    product = mul(jnp.concatenate(mixed_slots, axis=1), w_out, NT).astype(BF)
-    middle = residual + scatter_rows(product, rows)
-    normed_two, factor_two = norm_forward(middle, gain_two)
-    two_rows = gather_rows(normed_two.astype(BF))
+    half = seq // 2
+    middle, factor_two, two_blocks = [None, None], [None, None], [None, None]
+    for h in range(2):
+        rows_in = jnp.concatenate([m[h * half : (h + 1) * half] for m in mixed_slots], axis=1)
+        summed = scatter_half(mul(rows_in, w_out, NT).astype(BF), rows)
+        if h == 1:
+            summed = after(summed, two_blocks[0][0])
+        middle[h] = halves[h] + summed
+        normed, factor_two[h] = norm_forward(middle[h], gain_two)
+        normed = lax.optimization_barrier(normed.astype(BF))
+        two_blocks[h] = gather_slots(normed, "tp")
+    two_rows = jnp.concatenate(two_blocks[0] + two_blocks[1], axis=0)
 
     g_mine, g_other = parted(out_grad)
     g_got = swap(g_other, "seg", 1)
@@ -462,7 +472,7 @@
         ups.append(upward)
         hidden.append(hid)
     product = mul(jnp.concatenate(hidden, axis=1), jnp.concatenate(w_down, axis=1), NT)
-    result = middle + after(scatter_rows(product.astype(BF), rows), grad_rows)
+    projected = scatter_rows(product.astype(BF), rows)
     grad_parts = []
     for c in range(2):
         grad_hidden = mul(grad_rows, w_down[c], NN)
@@ -482,18 +492,21 @@
     grad_down = reduce_parts([mul(grad_rows, hidden[c], TN) for c in range(2)]).T
     grad_gu = reduce_parts([mul(two_rows, grad_parts[c], TN) for c in range(2)])
     grad_gu = grad_gu.reshape(depth, 2, ff)
-    half = seq // 2
     grad_middle, gain_two_terms, mid_blocks = [None, None], [], [None, None]
-    for h in (1, 0):
-        terms = [mul(grad_parts[c][h * half : (h + 1) * half], w_gu[c], NT) for c in range(2)]
-        grad_two = scatter_half((terms[0] + terms[1]).astype(BF), rows)
-        if h == 0:
-            grad_two = after(grad_two, mid_blocks[1][0])
+    for h in range(2):
+        weights = w_gu if h == 0 else lax.optimization_barrier(w_gu)
+        grads = jnp.concatenate([g[h * half : (h + 1) * half] for g in grad_parts], axis=1)
+        product = mul(grads, jnp.concatenate(weights, axis=1), NT)
+        grad_two = scatter_half(product.astype(BF), rows)
+        if h == 1:
+            grad_two = after(grad_two, mid_blocks[0][0])
         grad_resid, gain_term = norm_backward(middle[h], factor_two[h], gain_two, grad_two)
         gain_two_terms.append(gain_term)
         grad_middle[h] = grad_result[h] + grad_resid
         mid_blocks[h] = gather_slots(lax.optimization_barrier(grad_middle[h].astype(BF)), "tp")
     mid_rows = jnp.concatenate(mid_blocks[0] + mid_blocks[1], axis=0)
+    projected = after(projected, mid_blocks[1][0])
+    result_live = [((middle[h] + projected[h]) * live[h]).astype(BF) for h in range(2)]
     raws, qkvo_terms = {}, {}
     for part in reversed(range(len(w_qkvo))):
         grad_mixed = mul(mid_rows, w_qkvo[part][:, cut:], NN).astype(BF)
@@ -525,7 +538,6 @@
         gain_terms.append(gain_term)
         input_grads[h] = (grad_middle[h] + grad_resid).astype(BF)
     input_grad = joined(input_grads[0], swap(input_grads[1], "seg", 1))
-    result_live = (result * live).astype(BF)
     outputs = joined(result_live[0], swap(result_live[1], "seg", 1))
     gains = jnp.stack([gain_terms[0] + gain_terms[1], gain_two_terms[0] + gain_two_terms[1]])
     gains = sum_all(gains, ("fsdp", "tp", "seg"))

time: 1500 us -> 1490 us (level)
  waiting for transfers between devices: 783 us -> 755 us
  local copies, waits for them, and re-layouts: 86.3 us -> 108 us
    ppermute x51 -> x57, waiting for transfers between devices: 783 us -> 754 us  [swap(): return lax.ppermute(x, axis, [(i, i ^ bit) for i in range(size)])]
    unnamed x155 -> x167, local copies, waits for them, and re-layouts: 55.5 us -> 63.1 us
    ppermute x51 -> x57, starting transfers between devices: 37.1 us -> 34.8 us  [swap(): return lax.ppermute(x, axis, [(i, i ^ bit) for i in range(size)])]
    dot_general x24 -> x23, matrix products: 306 us -> 307 us  [mul(): return lax.dot_general(a, b, (dims, ((), ())), preferred_element_type=F32)]
  transfers between devices with their start and end apart: 63 -> 69, of which waited for: 23 -> 24; matrix products, arithmetic and copies ran while one was open for 26% -> 28% of each run, Pallas kernels for 12% -> 12%
where the time goes in v1:
time: 1490 us; the launch traced here: 1480 us
  waiting for transfers between devices  755 us (51%)
  matrix products  307 us (21%)
  Pallas kernels  178 us (12%)
  local copies, waits for them, and re-layouts  108 us (7%)
  other arithmetic  78.7 us (5%)
  starting transfers between devices  35.3 us (2%)
  between operations  15.8 us (1%)
    ppermute x57, waiting for transfers between devices, swap(): return lax.ppermute(x, axis, [(i, i ^ bit) for i in range(size)])  754 us
    dot_general x23, matrix products, mul(): return lax.dot_general(a, b, (dims, ((), ())), preferred_element_type=F32)  307 us
    pallas_call x2, Pallas kernels, attend_back(): pl.pallas_call(functools.partial(attend_back_kernel, group), grid_spec=pl...  88.3 us
    unnamed x167, local copies, waits for them, and re-layouts  63.1 us
    pallas_call x2, Pallas kernels, attend(): pl.pallas_call(functools.partial(attend_kernel, group), grid_spec=pltpu.P...  62.7 us
    ppermute x57, starting transfers between devices, swap(): return lax.ppermute(x, axis, [(i, i ^ bit) for i in range(size)])  34.8 us
  transfers between devices with their start and end apart: 69, of which 24 were waited for; matrix products, arithmetic and copies ran while one was open for 28% of the time, Pallas kernels for 12%

profile of v1, /device:TPU:0, one launch (start us, length us, event | category | flops | bytes accessed | tf_op | source)
XLA Modules:
  0.0 1484.9 jit_solution(13975520188446207090)
XLA Ops:
  14.5 45.8 %collective-permute-done.7 = bf16[512,1024]{1,0:T(8,128)(2,1)S(1)} collective-permute-done((bf16[512,1024]{1,0:T(8,128)(2,1)}, bf16[512,1024]{1,0:T(8,128)(2,1)S(1)}, u32[]{:S(2)}, u32[]{:S(2)}) %collective-permute-start.7) | collective-permute-done | bytes 1048608 | tf_op jit(solution)/shard_map/ppermute | solution.py:31
  65.8 92.9 %collective-permute-done.20 = bf16[512,2048]{1,0:T(8,128)(2,1)} collective-permute-done((bf16[512,2048]{1,0:T(8,128)(2,1)}, bf16[512,2048]{1,0:T(8,128)(2,1)}, u32[]{:S(2)}, u32[]{:S(2)}) %collective-permute-start.20) | collective-permute-done | bytes 2097184 | tf_op jit(solution)/shard_map/ppermute | solution.py:31
  158.9 7.9 all-gather.1
  181.9 5.9 fusion.130
  187.8 120.4 %collective-permute-done.25 = bf16[256,2048]{1,0:T(8,128)(2,1)} collective-permute-done((bf16[256,2048]{1,0:T(8,128)(2,1)}, bf16[256,2048]{1,0:T(8,128)(2,1)}, u32[]{:S(2)}, u32[]{:S(2)}) %collective-permute-start.25) | collective-permute-done | bytes 1048608 | tf_op jit(solution)/shard_map/ppermute | solution.py:31
  325.0 58.8 %collective-permute-done.5 = bf16[256,2048]{1,0:T(8,128)(2,1)} collective-permute-done((bf16[256,2048]{1,0:T(8,128)(2,1)}, bf16[256,2048]{1,0:T(8,128)(2,1)}, u32[]{:S(2)}, u32[]{:S(2)}) %collective-permute-start.5) | collective-permute-done | bytes 1048608 | tf_op jit(solution)/shard_map/ppermute | solution.py:31
  400.7 13.5 qkv_project.2.qkv_ref
  414.2 31.0 %attend.2 = (bf16[2048,256]{1,0:T(8,128)(2,1)}, f32[2,8,2,256]{3,2,1,0:T(2,128)}) custom-call(s32[3]{0:T(128)} %pad_add_fusion.info_ref, bf16[2048,768]{1,0:T(8,128)(2,1)} %qkv_project.2.qkv_ref), custom_call_target="tpu_custom_call" | custom-call | flops 8589934592 | bytes 4194304 | tf_op jit(solution)/shard_map/attend/pallas_call | solution.py:188
  449.8 13.4 qkv_project.3.qkv_ref
  465.4 31.7 %attend.3 = (bf16[2048,256]{1,0:T(8,128)(2,1)}, f32[2,8,2,256]{3,2,1,0:T(2,128)}) custom-call(s32[3]{0:T(128)} %pad_add_fusion.info_ref, bf16[2048,768]{1,0:T(8,128)(2,1)} %qkv_project.3.qkv_ref), custom_call_target="tpu_custom_call" | custom-call | flops 8589934592 | bytes 4194304 | tf_op jit(solution)/shard_map/attend/pallas_call | solution.py:188
  515.9 18.9 %collective-permute-done.10 = bf16[256,2048]{1,0:T(8,128)(2,1)S(1)} collective-permute-done((bf16[256,2048]{1,0:T(8,128)(2,1)S(1)}, bf16[256,2048]{1,0:T(8,128)(2,1)S(1)}, u32[]{:S(2)}, u32[]{:S(2)}) %collective-permute-start.10) | collective-permute-done | bytes 1048608 | tf_op jit(solution)/shard_map/ppermute | solution.py:31
  536.9 20.3 %collective-permute-done.16 = bf16[256,2048]{1,0:T(8,128)(2,1)S(1)} collective-permute-done((bf16[256,2048]{1,0:T(8,128)(2,1)S(1)}, bf16[256,2048]{1,0:T(8,128)(2,1)S(1)}, u32[]{:S(2)}, u32[]{:S(2)}) %collective-permute-start.16) | collective-permute-done | bytes 1048608 | tf_op jit(solution)/shard_map/ppermute | solution.py:31
  561.8 17.9 %collective-permute-done.12 = bf16[256,2048]{1,0:T(8,128)(2,1)S(1)} collective-permute-done((bf16[256,2048]{1,0:T(8,128)(2,1)S(1)}, bf16[256,2048]{1,0:T(8,128)(2,1)S(1)}, u32[]{:S(2)}, u32[]{:S(2)}) %collective-permute-start.12) | collective-permute-done | bytes 1048608 | tf_op jit(solution)/shard_map/ppermute | solution.py:31
  583.6 17.9 %collective-permute-done.18 = bf16[256,2048]{1,0:T(8,128)(2,1)S(1)} collective-permute-done((bf16[256,2048]{1,0:T(8,128)(2,1)S(1)}, bf16[256,2048]{1,0:T(8,128)(2,1)S(1)}, u32[]{:S(2)}, u32[]{:S(2)}) %collective-permute-start.18) | collective-permute-done | bytes 1048608 | tf_op jit(solution)/shard_map/ppermute | solution.py:31
  609.0 12.6 fusion.84
  621.7 15.8 %fusion.48 = (bf16[2048,1024]{1,0:T(8,128)(2,1)}, bf16[2048,1024]{1,0:T(8,128)(2,1)}) fusion(bf16[2048,1024]{1,0:T(8,128)(2,1)S(1)} %fusion.84, bf16[2048,2048]{1,0:T(8,128)(2,1)} %constant_dynamic-update-slice_fusion.8, bf16[2048,2048]{1,0:T(8,128)(2,1)S(1)} %copy-done.60), kind=kOutput, calls=%fused_computation.68 | convolution fusion | flops 8608808960 | bytes 25165824 | tf_op jit(solution)/shard_map/dot_general | solution.py:329
  637.5 18.5 %fusion.25 = (bf16[2048,1024]{1,0:T(8,128)(2,1)S(1)}, bf16[2048,1024]{1,0:T(8,128)(2,1)S(1)}) fusion(bf16[2048,1024]{1,0:T(8,128)(2,1)} %copy-done.64, bf16[2048,1024]{1,0:T(8,128)(2,1)} %get-tuple-element.31, bf16[2048,2048]{1,0:T(8,128)(2,1)} %fusion.135, bf16[2048,1024]{0,1:T(8,128)(2,1)} %all-gather.17.cloned.1.call-done), kind=kOutput, calls=%fused_computation.45 | convolution fusion | flops 8621391872 | bytes 29360128 | tf_op jit(solution)/shard_map/dot_general | solution.py:329
  663.0 12.8 fusion.90
  675.8 15.8 %fusion.47 = (bf16[2048,1024]{1,0:T(8,128)(2,1)}, bf16[2048,1024]{1,0:T(8,128)(2,1)}) fusion(bf16[2048,1024]{1,0:T(8,128)(2,1)S(1)} %fusion.90, bf16[2048,2048]{1,0:T(8,128)(2,1)} %constant_dynamic-update-slice_fusion.8, bf16[2048,2048]{1,0:T(8,128)(2,1)S(1)} %copy-done.61), kind=kOutput, calls=%fused_computation.67 | convolution fusion | flops 8608808960 | bytes 25165824 | tf_op jit(solution)/shard_map/dot_general | solution.py:329
  691.7 18.5 %fusion.33 = (bf16[2048,1024]{1,0:T(8,128)(2,1)S(1)}, bf16[2048,1024]{1,0:T(8,128)(2,1)S(1)}) fusion(bf16[2048,1024]{1,0:T(8,128)(2,1)} %copy-done.63, bf16[2048,1024]{1,0:T(8,128)(2,1)} %get-tuple-element.33, bf16[2048,2048]{1,0:T(8,128)(2,1)} %fusion.135, bf16[2048,1024]{0,1:T(8,128)(2,1)} %all-gather.19.cloned.1.call-done), kind=kOutput, calls=%fused_computation.53 | convolution fusion | flops 8621391872 | bytes 29360128 | tf_op jit(solution)/shard_map/dot_general | solution.py:329
  716.0 26.9 %fusion.72 = bf16[1024,2048]{1,0:T(8,128)(2,1)} fusion(bf16[2048,2048]{1,0:T(8,128)(2,1)} %all-gather.15.cloned.1.call-done, bf16[2048,2048]{1,0:T(8,128)(2,1)} %all-gather.13.cloned.1.call-done, bf16[1024,2048]{1,0:T(8,128)(2,1)} %get-tuple-element.96, bf16[1024,2048]{1,0:T(8,128)(2,1)} %get-tuple-element.94), kind=kOutput, calls=%fused_computation.108 | convolution fusion | flops 17232297984 | bytes 29360128 | tf_op jit(solution)/shard_map/dot_general | solution.py:329
  745.2 26.7 %fusion.77 = bf16[1024,2048]{1,0:T(8,128)(2,1)} fusion(bf16[2048,2048]{1,0:T(8,128)(2,1)} %all-gather.15.cloned.1.call-done, bf16[2048,2048]{1,0:T(8,128)(2,1)} %all-gather.13.cloned.1.call-done, bf16[1024,2048]{1,0:T(8,128)(2,1)} %get-tuple-element.97, bf16[1024,2048]{1,0:T(8,128)(2,1)} %get-tuple-element.95), kind=kOutput, calls=%fused_computation.109 | convolution fusion | flops 17232297984 | bytes 29360128 | tf_op jit(solution)/shard_map/dot_general | solution.py:329
  779.1 22.2 %collective-permute-done.34 = bf16[256,2048]{1,0:T(8,128)(2,1)S(1)} collective-permute-done((bf16[256,2048]{1,0:T(8,128)(2,1)S(1)}, bf16[256,2048]{1,0:T(8,128)(2,1)S(1)}, u32[]{:S(2)}, u32[]{:S(2)}) %collective-permute-start.34) | collective-permute-done | bytes 1048608 | tf_op jit(solution)/shard_map/ppermute | solution.py:31
  805.4 18.3 %collective-permute-done.31 = bf16[256,2048]{1,0:T(8,128)(2,1)S(1)} collective-permute-done((bf16[256,2048]{1,0:T(8,128)(2,1)S(1)}, bf16[256,2048]{1,0:T(8,128)(2,1)S(1)}, u32[]{:S(2)}, u32[]{:S(2)}) %collective-permute-start.31) | collective-permute-done | bytes 1048608 | tf_op jit(solution)/shard_map/ppermute | solution.py:31
  831.0 10.9 convolution_convert_fusion.2
  848.7 19.1 %collective-permute-done.40 = bf16[256,2048]{1,0:T(8,128)(2,1)} collective-permute-done((bf16[256,2048]{1,0:T(8,128)(2,1)S(1)}, bf16[256,2048]{1,0:T(8,128)(2,1)}, u32[]{:S(2)}, u32[]{:S(2)}) %collective-permute-start.40) | collective-permute-done | bytes 1048608 | tf_op jit(solution)/shard_map/ppermute | solution.py:31
  879.0 44.2 %attend_back.3 = bf16[2048,768]{1,0:T(8,128)(2,1)} custom-call(s32[3]{0:T(128)} %pad_add_fusion.info_ref, bf16[2048,768]{1,0:T(8,128)(2,1)} %qkv_project.3.qkv_ref, bf16[2048,256]{1,0:T(8,128)(2,1)} %get-tuple-element.27.o_ref, bf16[2048,256]{1,0:T(8,128)(2,1)} %convolution_convert_fusion.8.do_ref, f32[2,8,2,256]{3,2,1,0:T(2,128)} %get-tuple-element.40.lse_ref, ...), custom_call_target="tpu_custom_call" | custom-call | flops 21474836480 | bytes 8388608 | tf_op jit(solution)/shard_map/attend_back/pallas_call | solution.py:287
  923.2 10.2 convolution_convert_fusion.4
  936.0 23.8 %fusion.50 = bf16[2048,2048]{1,0:T(8,128)(2,1)} fusion(bf16[2048,2048]{1,0:T(8,128)(2,1)} %constant_dynamic-update-slice_fusion.8, bf16[2048,1024]{1,0:T(8,128)(2,1)} %copy-done.18, bf16[2048,1024]{1,0:T(8,128)(2,1)} %copy-done.19), kind=kOutput, calls=%fused_computation.70 | convolution fusion | flops 17200840704 | bytes 25165824 | tf_op jit(solution)/shard_map/dot_general | solution.py:329
  959.8 14.1 convolution_convert_fusion.3
  975.2 5.7 convolution_convert_fusion.7
  980.9 7.0 convolution_convert_fusion.9.do_ref
  988.0 44.1 %attend_back.2 = bf16[2048,768]{1,0:T(8,128)(2,1)} custom-call(s32[3]{0:T(128)} %pad_add_fusion.info_ref, bf16[2048,768]{1,0:T(8,128)(2,1)} %qkv_project.2.qkv_ref, bf16[2048,256]{1,0:T(8,128)(2,1)} %get-tuple-element.26.o_ref, bf16[2048,256]{1,0:T(8,128)(2,1)} %convolution_convert_fusion.9.do_ref, f32[2,8,2,256]{3,2,1,0:T(2,128)} %get-tuple-element.39.lse_ref, ...), custom_call_target="tpu_custom_call" | custom-call | flops 21474836480 | bytes 8388608 | tf_op jit(solution)/shard_map/attend_back/pallas_call | solution.py:287
  1032.1 10.4 convolution_convert_fusion.5
  1044.9 23.7 %fusion.49 = bf16[2048,2048]{1,0:T(8,128)(2,1)} fusion(bf16[2048,2048]{1,0:T(8,128)(2,1)} %constant_dynamic-update-slice_fusion.8, bf16[2048,1024]{1,0:T(8,128)(2,1)} %copy-done.16, bf16[2048,1024]{1,0:T(8,128)(2,1)} %copy-done.17), kind=kOutput, calls=%fused_computation.69 | convolution fusion | flops 17200840704 | bytes 25165824 | tf_op jit(solution)/shard_map/dot_general | solution.py:329
  1068.7 22.4 %fusion.51 = bf16[2048,2048]{1,0:T(8,128)(2,1)S(1)} fusion(bf16[2048,1024]{0,1:T(8,128)(2,1)} %all-gather.19.cloned.1.call-done, bf16[2048,1024]{0,1:T(8,128)(2,1)} %all-gather.17.cloned.1.call-done, bf16[2048,1024]{1,0:T(8,128)(2,1)} %get-tuple-element.30, bf16[2048,1024]{1,0:T(8,128)(2,1)} %get-tuple-element.29), kind=kOutput, calls=%fused_computation.71 | convolution fusion | flops 17217617920 | bytes 25165824 | tf_op jit(solution)/shard_map/dot_general | solution.py:329
  1103.7 9.0 fusion.83
  1115.4 8.8 fusion.82
  1124.8 22.7 %collective-permute-done.24 = bf16[2,256,2048]{2,1,0:T(8,128)(2,1)} collective-permute-done((bf16[2,256,2048]{2,1,0:T(8,128)(2,1)}, bf16[2,256,2048]{2,1,0:T(8,128)(2,1)}, u32[]{:S(2)}, u32[]{:S(2)}) %collective-permute-start.24) | collective-permute-done | bytes 2097184 | tf_op jit(solution)/shard_map/ppermute | solution.py:31
  1156.2 22.3 %collective-permute-done.47 = bf16[256,2048]{1,0:T(8,128)(2,1)S(1)} collective-permute-done((bf16[256,2048]{1,0:T(8,128)(2,1)S(1)}, bf16[256,2048]{1,0:T(8,128)(2,1)S(1)}, u32[]{:S(2)}, u32[]{:S(2)}) %collective-permute-start.47) | collective-permute-done | bytes 1048608 | tf_op jit(solution)/shard_map/ppermute | solution.py:31
  1180.0 42.4 %collective-permute-done.44 = bf16[256,2048]{1,0:T(8,128)(2,1)S(1)} collective-permute-done((bf16[256,2048]{1,0:T(8,128)(2,1)S(1)}, bf16[256,2048]{1,0:T(8,128)(2,1)S(1)}, u32[]{:S(2)}, u32[]{:S(2)}) %collective-permute-start.44) | collective-permute-done | bytes 1048608 | tf_op jit(solution)/shard_map/ppermute | solution.py:31
  1239.2 22.1 %collective-permute-done.52 = f32[2,2048]{1,0:T(2,128)S(1)} collective-permute-done((f32[2,2048]{1,0:T(2,128)S(1)}, f32[2,2048]{1,0:T(2,128)S(1)}, u32[]{:S(2)}, u32[]{:S(2)}) %collective-permute-start.52) | collective-permute-done | bytes 16416 | tf_op jit(solution)/shard_map/ppermute | solution.py:31
  1269.7 106.4 %collective-permute-done.53 = f32[2,2048]{1,0:T(2,128)S(1)} collective-permute-done((f32[2,2048]{1,0:T(2,128)S(1)}, f32[2,2048]{1,0:T(2,128)S(1)}, u32[]{:S(2)}, u32[]{:S(2)}) %collective-permute-start.53) | collective-permute-done | bytes 16416 | tf_op jit(solution)/shard_map/ppermute | solution.py:31
  1378.4 20.3 %collective-permute-done.56 = bf16[512,1024]{1,0:T(8,128)(2,1)} collective-permute-done((bf16[512,1024]{1,0:T(8,128)(2,1)}, bf16[512,1024]{1,0:T(8,128)(2,1)}, u32[]{:S(2)}, u32[]{:S(2)}) %collective-permute-start.56) | collective-permute-done | bytes 1048608 | tf_op jit(solution)/shard_map/ppermute | solution.py:31
  1402.5 18.7 %collective-permute-done.54 = bf16[512,1024]{0,1:T(8,128)(2,1)} collective-permute-done((bf16[512,1024]{0,1:T(8,128)(2,1)}, bf16[512,1024]{0,1:T(8,128)(2,1)}, u32[]{:S(2)}, u32[]{:S(2)}) %collective-permute-start.54) | collective-permute-done | bytes 1048608 | tf_op jit(solution)/shard_map/ppermute | solution.py:31
  1432.1 34.0 %collective-permute-done.55 = bf16[512,2048]{1,0:T(8,128)(2,1)} collective-permute-done((bf16[512,2048]{1,0:T(8,128)(2,1)}, bf16[512,2048]{1,0:T(8,128)(2,1)}, u32[]{:S(2)}, u32[]{:S(2)}) %collective-permute-start.55) | collective-permute-done | bytes 2097184 | tf_op jit(solution)/shard_map/ppermute | solution.py:31
  1466.1 5.1 convert_add_fusion.4
  1471.1 6.6 reshape.484
  (406 shorter events, 230.4 us)
Async XLA Ops:
  7.2 393.5 %all-gather.9.cloned.1.call-start = ((), (), s32[]{:S(2)}) async-start(), calls=%async_computation.6 | async-start | bytes 5242880 | tf_op jit(solution)/shard_map/all_gather | solution.py:359
  10.3 439.4 %all-gather.11.cloned.1.call-start = ((), (), s32[]{:S(2)}) async-start(), calls=%async_computation.7 | async-start | bytes 5242880 | tf_op jit(solution)/shard_map/all_gather | solution.py:359
  10.4 50.0 %collective-permute-start.7 = (bf16[512,1024]{1,0:T(8,128)(2,1)}, bf16[512,1024]{1,0:T(8,128)(2,1)S(1)}, u32[]{:S(2)}, u32[]{:S(2)}) collective-permute-start(bf16[512,1024]{1,0:T(8,128)(2,1)} %pad_maximum_fusion.20), channel_id=1, source_target_pairs={{0,4},{4,0},{1,5},{5,1},{2,6},{6,2},{3,7},{7,3},{8,12},{12,8},{9,1... | collective-permute-start | bytes 3145736 | tf_op jit(solution)/shard_map/ppermute | solution.py:31
  61.3 547.7 %all-gather.13.cloned.1.call-start = ((), (), s32[]{:S(2)}) async-start(), calls=%async_computation.8 | async-start | bytes 10485760 | tf_op jit(solution)/shard_map/all_gather | solution.py:359
  65.1 572.4 %all-gather.17.cloned.1.call-start = ((), (), s32[]{:S(2)}) async-start(), calls=%async_computation.10 | async-start | bytes 5242880 | tf_op jit(solution)/shard_map/all_gather | solution.py:359
  65.7 597.3 %all-gather.15.cloned.1.call-start = ((), (), s32[]{:S(2)}) async-start(), calls=%async_computation.9 | async-start | bytes 10485760 | tf_op jit(solution)/shard_map/all_gather | solution.py:359
  65.7 93.0 %collective-permute-start.20 = (bf16[512,2048]{1,0:T(8,128)(2,1)}, bf16[512,2048]{1,0:T(8,128)(2,1)}, u32[]{:S(2)}, u32[]{:S(2)}) collective-permute-start(bf16[512,2048]{1,0:T(8,128)(2,1)} %bitcast.162), channel_id=1, source_target_pairs={{0,4},{4,0},{1,5},{5,1},{2,6},{6,2},{3,7},{7,3},{8,12},{12,8},{9,1... | collective-permute-start | bytes 6291464 | tf_op jit(solution)/shard_map/ppermute | solution.py:31
  158.8 532.9 %all-gather.19.cloned.1.call-start = ((), (), s32[]{:S(2)}) async-start(), calls=%async_computation.11 | async-start | bytes 5242880 | tf_op jit(solution)/shard_map/all_gather | solution.py:359
  169.0 146.2 %collective-permute-start = (bf16[256,2048]{1,0:T(8,128)(2,1)}, bf16[256,2048]{1,0:T(8,128)(2,1)}, u32[]{:S(2)}, u32[]{:S(2)}) collective-permute-start(bf16[256,2048]{1,0:T(8,128)(2,1)} %fusion.114), channel_id=1, source_target_pairs={{0,1},{1,0},{2,3},{3,2},{4,5},{5,4},{6,7},{7,6},{8,9},{9,8},{10,11... | collective-permute-start | bytes 3145736 | tf_op jit(solution)/shard_map/ppermute | solution.py:31
  169.0 148.2 %collective-permute-start.1 = (bf16[256,2048]{1,0:T(8,128)(2,1)}, bf16[256,2048]{1,0:T(8,128)(2,1)}, u32[]{:S(2)}, u32[]{:S(2)}) collective-permute-start(bf16[256,2048]{1,0:T(8,128)(2,1)} %fusion.114), channel_id=1, source_target_pairs={{0,2},{1,3},{2,0},{3,1},{4,6},{5,7},{6,4},{7,5},{8,10},{9,11},{10,... | collective-permute-start | bytes 3145736 | tf_op jit(solution)/shard_map/ppermute | solution.py:31
  169.0 151.8 %collective-permute-start.21 = (bf16[512,1024]{0,1:T(8,128)(2,1)}, bf16[512,1024]{0,1:T(8,128)(2,1)}, u32[]{:S(2)}, u32[]{:S(2)}) collective-permute-start(bf16[512,1024]{0,1:T(8,128)(2,1)} %bitcast.13), channel_id=1, source_target_pairs={{0,4},{4,0},{1,5},{5,1},{2,6},{6,2},{3,7},{7,3},{8,12},{12,8},{9,1... | collective-permute-start | bytes 3145736 | tf_op jit(solution)/shard_map/ppermute | solution.py:31
  171.8 141.1 %collective-permute-start.3 = (bf16[256,2048]{1,0:T(8,128)(2,1)}, bf16[256,2048]{1,0:T(8,128)(2,1)S(1)}, u32[]{:S(2)}, u32[]{:S(2)}) collective-permute-start(bf16[256,2048]{1,0:T(8,128)(2,1)} %dynamic-slice_bitcast_fusion.2), channel_id=1, source_target_pairs={{0,4},{4,0},{1,5},{5,1},{2,6},{6,2},{3,7},{7,3},{8,12},{12,8},{9,1... | collective-permute-start | bytes 3145736 | tf_op jit(solution)/shard_map/ppermute | solution.py:31
  176.1 132.1 %collective-permute-start.25 = (bf16[256,2048]{1,0:T(8,128)(2,1)}, bf16[256,2048]{1,0:T(8,128)(2,1)}, u32[]{:S(2)}, u32[]{:S(2)}) collective-permute-start(bf16[256,2048]{1,0:T(8,128)(2,1)} %get-tuple-element.121), channel_id=1, source_target_pairs={{0,4},{4,0},{1,5},{5,1},{2,6},{6,2},{3,7},{7,3},{8,12},{12,8},{9,1... | collective-permute-start | bytes 3145736 | tf_op jit(solution)/shard_map/ppermute | solution.py:31
  312.9 80.9 %collective-permute-start.26 = (bf16[2,256,2048]{2,1,0:T(8,128)(2,1)}, bf16[2,256,2048]{2,1,0:T(8,128)(2,1)}, u32[]{:S(2)}, u32[]{:S(2)}) collective-permute-start(bf16[2,256,2048]{2,1,0:T(8,128)(2,1)} %get-tuple-element.119), channel_id=1, source_target_pairs={{0,1},{1,0},{2,3},{3,2},{4,5},{5,4},{6,7},{7,6},{8,9},{9,8},{10,11... | collective-permute-start | bytes 6291464 | tf_op jit(solution)/shard_map/ppermute | solution.py:31
  312.9 80.4 %collective-permute-start.27 = (bf16[2,256,2048]{2,1,0:T(8,128)(2,1)}, bf16[2,256,2048]{2,1,0:T(8,128)(2,1)}, u32[]{:S(2)}, u32[]{:S(2)}) collective-permute-start(bf16[2,256,2048]{2,1,0:T(8,128)(2,1)} %get-tuple-element.119), channel_id=1, source_target_pairs={{0,2},{1,3},{2,0},{3,1},{4,6},{5,7},{6,4},{7,5},{8,10},{9,11},{10,... | collective-permute-start | bytes 6291464 | tf_op jit(solution)/shard_map/ppermute | solution.py:31
  315.2 68.5 %collective-permute-start.5 = (bf16[256,2048]{1,0:T(8,128)(2,1)}, bf16[256,2048]{1,0:T(8,128)(2,1)}, u32[]{:S(2)}, u32[]{:S(2)}) collective-permute-start(bf16[256,2048]{1,0:T(8,128)(2,1)} %fusion.104), channel_id=1, source_target_pairs={{0,2},{1,3},{2,0},{3,1},{4,6},{5,7},{6,4},{7,5},{8,10},{9,11},{10,... | collective-permute-start | bytes 3145736 | tf_op jit(solution)/shard_map/ppermute | solution.py:31
  317.2 66.5 %collective-permute-start.2 = (bf16[256,2048]{1,0:T(8,128)(2,1)}, bf16[256,2048]{1,0:T(8,128)(2,1)}, u32[]{:S(2)}, u32[]{:S(2)}) collective-permute-start(bf16[256,2048]{1,0:T(8,128)(2,1)} %collective-permute-done.1), channel_id=1, source_target_pairs={{0,1},{1,0},{2,3},{3,2},{4,5},{5,4},{6,7},{7,6},{8,9},{9,8},{10,11... | collective-permute-start | bytes 3145736 | tf_op jit(solution)/shard_map/ppermute | solution.py:31
  320.8 67.7 %collective-permute-start.4 = (bf16[256,2048]{1,0:T(8,128)(2,1)}, bf16[256,2048]{1,0:T(8,128)(2,1)}, u32[]{:S(2)}, u32[]{:S(2)}) collective-permute-start(bf16[256,2048]{1,0:T(8,128)(2,1)} %fusion.104), channel_id=1, source_target_pairs={{0,1},{1,0},{2,3},{3,2},{4,5},{5,4},{6,7},{7,6},{8,9},{9,8},{10,11... | collective-permute-start | bytes 3145736 | tf_op jit(solution)/shard_map/ppermute | solution.py:31
  323.6 940.4 %reduce-scatter.17.cloned.1.call-start = ((), (), s32[]{:S(2)}) async-start(), calls=%async_computation.17 | async-start | bytes 5242880 | tf_op jit(solution)/shard_map/reduce_scatter | solution.py:486
  393.3 109.4 %collective-permute-start.28 = (bf16[2,256,2048]{2,1,0:T(8,128)(2,1)}, bf16[2,256,2048]{2,1,0:T(8,128)(2,1)}, u32[]{:S(2)}, u32[]{:S(2)}) collective-permute-start(bf16[2,256,2048]{2,1,0:T(8,128)(2,1)} %collective-permute-done.27), channel_id=1, source_target_pairs={{0,1},{1,0},{2,3},{3,2},{4,5},{5,4},{6,7},{7,6},{8,9},{9,8},{10,11... | collective-permute-start | bytes 6291464 | tf_op jit(solution)/shard_map/ppermute | solution.py:31
  514.1 43.1 %collective-permute-start.16 = (bf16[256,2048]{1,0:T(8,128)(2,1)S(1)}, bf16[256,2048]{1,0:T(8,128)(2,1)S(1)}, u32[]{:S(2)}, u32[]{:S(2)}) collective-permute-start(bf16[256,2048]{1,0:T(8,128)(2,1)S(1)} %add_convert_fusion.8), channel_id=1, source_target_pairs={{0,2},{1,3},{2,0},{3,1},{4,6},{5,7},{6,4},{7,5},{8,10},{9,11},{10,... | collective-permute-start | bytes 3145736 | tf_op jit(solution)/shard_map/ppermute | solution.py:31
  536.4 65.1 %collective-permute-start.11 = (bf16[256,2048]{1,0:T(8,128)(2,1)S(1)}, bf16[256,2048]{1,0:T(8,128)(2,1)S(1)}, u32[]{:S(2)}, u32[]{:S(2)}) collective-permute-start(bf16[256,2048]{1,0:T(8,128)(2,1)S(1)} %multiply_convert_fusion.1), channel_id=1, source_target_pairs={{0,1},{1,0},{2,3},{3,2},{4,5},{5,4},{6,7},{7,6},{8,9},{9,8},{10,11... | collective-permute-start | bytes 3145736 | tf_op jit(solution)/shard_map/ppermute | solution.py:31
  536.5 43.2 %collective-permute-start.12 = (bf16[256,2048]{1,0:T(8,128)(2,1)S(1)}, bf16[256,2048]{1,0:T(8,128)(2,1)S(1)}, u32[]{:S(2)}, u32[]{:S(2)}) collective-permute-start(bf16[256,2048]{1,0:T(8,128)(2,1)S(1)} %multiply_convert_fusion.1), channel_id=1, source_target_pairs={{0,2},{1,3},{2,0},{3,1},{4,6},{5,7},{6,4},{7,5},{8,10},{9,11},{10,... | collective-permute-start | bytes 3145736 | tf_op jit(solution)/shard_map/ppermute | solution.py:31
  559.1 42.5 %collective-permute-start.18 = (bf16[256,2048]{1,0:T(8,128)(2,1)S(1)}, bf16[256,2048]{1,0:T(8,128)(2,1)S(1)}, u32[]{:S(2)}, u32[]{:S(2)}) collective-permute-start(bf16[256,2048]{1,0:T(8,128)(2,1)S(1)} %multiply_convert_fusion), channel_id=1, source_target_pairs={{0,2},{1,3},{2,0},{3,1},{4,6},{5,7},{6,4},{7,5},{8,10},{9,11},{10,... | collective-permute-start | bytes 3145736 | tf_op jit(solution)/shard_map/ppermute | solution.py:31
  744.6 29.8 %collective-permute-start.33 = (bf16[256,2048]{1,0:T(8,128)(2,1)S(1)}, bf16[256,2048]{1,0:T(8,128)(2,1)S(1)}, u32[]{:S(2)}, u32[]{:S(2)}) collective-permute-start(bf16[256,2048]{1,0:T(8,128)(2,1)S(1)} %get-tuple-element.107), channel_id=1, source_target_pairs={{0,1},{1,0},{2,3},{3,2},{4,5},{5,4},{6,7},{7,6},{8,9},{9,8},{10,11... | collective-permute-start | bytes 3145736 | tf_op jit(solution)/shard_map/ppermute | solution.py:31
  775.5 29.9 %collective-permute-start.29 = (bf16[256,2048]{1,0:T(8,128)(2,1)S(1)}, bf16[256,2048]{1,0:T(8,128)(2,1)S(1)}, u32[]{:S(2)}, u32[]{:S(2)}) collective-permute-start(bf16[256,2048]{1,0:T(8,128)(2,1)S(1)} %get-tuple-element.108), channel_id=1, source_target_pairs={{0,1},{1,0},{2,3},{3,2},{4,5},{5,4},{6,7},{7,6},{8,9},{9,8},{10,11... | collective-permute-start | bytes 3145736 | tf_op jit(solution)/shard_map/ppermute | solution.py:31
  778.4 45.3 %collective-permute-start.31 = (bf16[256,2048]{1,0:T(8,128)(2,1)S(1)}, bf16[256,2048]{1,0:T(8,128)(2,1)S(1)}, u32[]{:S(2)}, u32[]{:S(2)}) collective-permute-start(bf16[256,2048]{1,0:T(8,128)(2,1)S(1)} %add_convert_fusion.6), channel_id=1, source_target_pairs={{0,2},{1,3},{2,0},{3,1},{4,6},{5,7},{6,4},{7,5},{8,10},{9,11},{10,... | collective-permute-start | bytes 3145736 | tf_op jit(solution)/shard_map/ppermute | solution.py:31
  805.0 62.8 %collective-permute-start.36 = (bf16[256,2048]{1,0:T(8,128)(2,1)S(1)}, bf16[256,2048]{1,0:T(8,128)(2,1)S(1)}, u32[]{:S(2)}, u32[]{:S(2)}) collective-permute-start(bf16[256,2048]{1,0:T(8,128)(2,1)S(1)} %get-tuple-element.84), channel_id=1, source_target_pairs={{0,1},{1,0},{2,3},{3,2},{4,5},{5,4},{6,7},{7,6},{8,9},{9,8},{10,11... | collective-permute-start | bytes 3145736 | tf_op jit(solution)/shard_map/ppermute | solution.py:31
  805.0 41.2 %collective-permute-start.37 = (bf16[256,2048]{1,0:T(8,128)(2,1)S(1)}, bf16[256,2048]{1,0:T(8,128)(2,1)}, u32[]{:S(2)}, u32[]{:S(2)}) collective-permute-start(bf16[256,2048]{1,0:T(8,128)(2,1)S(1)} %get-tuple-element.84), channel_id=1, source_target_pairs={{0,2},{1,3},{2,0},{3,1},{4,6},{5,7},{6,4},{7,5},{8,10},{9,11},{10,... | collective-permute-start | bytes 3145736 | tf_op jit(solution)/shard_map/ppermute | solution.py:31
  828.9 39.0 %collective-permute-start.40 = (bf16[256,2048]{1,0:T(8,128)(2,1)S(1)}, bf16[256,2048]{1,0:T(8,128)(2,1)}, u32[]{:S(2)}, u32[]{:S(2)}) collective-permute-start(bf16[256,2048]{1,0:T(8,128)(2,1)S(1)} %get-tuple-element.82), channel_id=1, source_target_pairs={{0,2},{1,3},{2,0},{3,1},{4,6},{5,7},{6,4},{7,5},{8,10},{9,11},{10,... | collective-permute-start | bytes 3145736 | tf_op jit(solution)/shard_map/ppermute | solution.py:31
  842.0 422.3 %reduce-scatter.9.cloned.1.call-start = ((), (), s32[]{:S(2)}) async-start(), calls=%async_computation.13 | async-start | bytes 5242880 | tf_op jit(solution)/shard_map/reduce_scatter | solution.py:486
  936.0 331.0 %reduce-scatter.13.cloned.1.call-start = ((), (), s32[]{:S(2)}) async-start(), calls=%async_computation.15 | async-start | bytes 10485760 | tf_op jit(solution)/shard_map/reduce_scatter | solution.py:486
  959.8 418.6 %reduce-scatter.15.cloned.1.call-start = ((), (), s32[]{:S(2)}) async-start(), calls=%async_computation.16 | async-start | bytes 5242880 | tf_op jit(solution)/shard_map/reduce_scatter | solution.py:486
  974.0 428.5 %reduce-scatter.7.cloned.1.call-start = ((), (), s32[]{:S(2)}) async-start(), calls=%async_computation.12 | async-start | bytes 5242880 | tf_op jit(solution)/shard_map/reduce_scatter | solution.py:486
  1044.9 387.2 %reduce-scatter.11.cloned.1.call-start = ((), (), s32[]{:S(2)}) async-start(), calls=%async_computation.14 | async-start | bytes 10485760 | tf_op jit(solution)/shard_map/reduce_scatter | solution.py:486
  1096.0 28.8 %collective-permute-start.22 = (bf16[2,256,2048]{2,1,0:T(8,128)(2,1)}, bf16[2,256,2048]{2,1,0:T(8,128)(2,1)}, u32[]{:S(2)}, u32[]{:S(2)}) collective-permute-start(bf16[2,256,2048]{2,1,0:T(8,128)(2,1)} %get-tuple-element.98), channel_id=1, source_target_pairs={{0,1},{1,0},{2,3},{3,2},{4,5},{5,4},{6,7},{7,6},{8,9},{9,8},{10,11... | collective-permute-start | bytes 6291464 | tf_op jit(solution)/shard_map/ppermute | solution.py:31
  1099.3 48.2 %collective-permute-start.24 = (bf16[2,256,2048]{2,1,0:T(8,128)(2,1)}, bf16[2,256,2048]{2,1,0:T(8,128)(2,1)}, u32[]{:S(2)}, u32[]{:S(2)}) collective-permute-start(bf16[2,256,2048]{2,1,0:T(8,128)(2,1)} %fusion.68), channel_id=1, source_target_pairs={{0,2},{1,3},{2,0},{3,1},{4,6},{5,7},{6,4},{7,5},{8,10},{9,11},{10,... | collective-permute-start | bytes 6291464 | tf_op jit(solution)/shard_map/ppermute | solution.py:31
  1114.4 37.5 %collective-permute-start.46 = (bf16[256,2048]{1,0:T(8,128)(2,1)}, bf16[256,2048]{1,0:T(8,128)(2,1)S(1)}, u32[]{:S(2)}, u32[]{:S(2)}) collective-permute-start(bf16[256,2048]{1,0:T(8,128)(2,1)} %get-tuple-element.103), channel_id=1, source_target_pairs={{0,1},{1,0},{2,3},{3,2},{4,5},{5,4},{6,7},{7,6},{8,9},{9,8},{10,11... | collective-permute-start | bytes 3145736 | tf_op jit(solution)/shard_map/ppermute | solution.py:31
  1124.5 28.1 %collective-permute-start.43 = (bf16[256,2048]{1,0:T(8,128)(2,1)S(1)}, bf16[256,2048]{1,0:T(8,128)(2,1)S(1)}, u32[]{:S(2)}, u32[]{:S(2)}) collective-permute-start(bf16[256,2048]{1,0:T(8,128)(2,1)S(1)} %get-tuple-element.101), channel_id=1, source_target_pairs={{0,1},{1,0},{2,3},{3,2},{4,5},{5,4},{6,7},{7,6},{8,9},{9,8},{10,11... | collective-permute-start | bytes 3145736 | tf_op jit(solution)/shard_map/ppermute | solution.py:31
  1151.3 28.7 %collective-permute-start.42 = (bf16[256,2048]{1,0:T(8,128)(2,1)S(1)}, bf16[256,2048]{1,0:T(8,128)(2,1)S(1)}, u32[]{:S(2)}, u32[]{:S(2)}) collective-permute-start(bf16[256,2048]{1,0:T(8,128)(2,1)S(1)} %get-tuple-element.100), channel_id=1, source_target_pairs={{0,1},{1,0},{2,3},{3,2},{4,5},{5,4},{6,7},{7,6},{8,9},{9,8},{10,11... | collective-permute-start | bytes 3145736 | tf_op jit(solution)/shard_map/ppermute | solution.py:31
  1152.2 26.2 %collective-permute-start.47 = (bf16[256,2048]{1,0:T(8,128)(2,1)S(1)}, bf16[256,2048]{1,0:T(8,128)(2,1)S(1)}, u32[]{:S(2)}, u32[]{:S(2)}) collective-permute-start(bf16[256,2048]{1,0:T(8,128)(2,1)S(1)} %add_convert_fusion), channel_id=1, source_target_pairs={{0,2},{1,3},{2,0},{3,1},{4,6},{5,7},{6,4},{7,5},{8,10},{9,11},{10,... | collective-permute-start | bytes 3145736 | tf_op jit(solution)/shard_map/ppermute | solution.py:31
  1153.0 69.4 %collective-permute-start.44 = (bf16[256,2048]{1,0:T(8,128)(2,1)S(1)}, bf16[256,2048]{1,0:T(8,128)(2,1)S(1)}, u32[]{:S(2)}, u32[]{:S(2)}) collective-permute-start(bf16[256,2048]{1,0:T(8,128)(2,1)S(1)} %add_convert_fusion.2), channel_id=1, source_target_pairs={{0,2},{1,3},{2,0},{3,1},{4,6},{5,7},{6,4},{7,5},{8,10},{9,11},{10,... | collective-permute-start | bytes 3145736 | tf_op jit(solution)/shard_map/ppermute | solution.py:31
  1156.2 78.0 %collective-permute-start.35 = (bf16[256,2048]{1,0:T(8,128)(2,1)}, bf16[256,2048]{1,0:T(8,128)(2,1)}, u32[]{:S(2)}, u32[]{:S(2)}) collective-permute-start(bf16[256,2048]{1,0:T(8,128)(2,1)} %get-tuple-element.105), channel_id=1, source_target_pairs={{0,4},{4,0},{1,5},{5,1},{2,6},{6,2},{3,7},{7,3},{8,12},{12,8},{9,1... | collective-permute-start | bytes 3145736 | tf_op jit(solution)/shard_map/ppermute | solution.py:31
  1237.6 139.1 %collective-permute-start.48 = (bf16[256,2048]{1,0:T(8,128)(2,1)}, bf16[256,2048]{1,0:T(8,128)(2,1)S(1)}, u32[]{:S(2)}, u32[]{:S(2)}) collective-permute-start(bf16[256,2048]{1,0:T(8,128)(2,1)} %fusion.108), channel_id=1, source_target_pairs={{0,4},{4,0},{1,5},{5,1},{2,6},{6,2},{3,7},{7,3},{8,12},{12,8},{9,1... | collective-permute-start | bytes 3145736 | tf_op jit(solution)/shard_map/ppermute | solution.py:31
  1261.3 114.8 %collective-permute-start.53 = (f32[2,2048]{1,0:T(2,128)S(1)}, f32[2,2048]{1,0:T(2,128)S(1)}, u32[]{:S(2)}, u32[]{:S(2)}) collective-permute-start(f32[2,2048]{1,0:T(2,128)S(1)} %add.380), channel_id=1, source_target_pairs={{0,4},{4,0},{1,5},{5,1},{2,6},{6,2},{3,7},{7,3},{8,12},{12,8},{9,1... | collective-permute-start | bytes 49160 | tf_op jit(solution)/shard_map/ppermute | solution.py:31
  1264.1 134.7 %collective-permute-start.56 = (bf16[512,1024]{1,0:T(8,128)(2,1)}, bf16[512,1024]{1,0:T(8,128)(2,1)}, u32[]{:S(2)}, u32[]{:S(2)}) collective-permute-start(bf16[512,1024]{1,0:T(8,128)(2,1)} %reduce-scatter.17.cloned.1.call-done), channel_id=1, source_target_pairs={{0,4},{4,0},{1,5},{5,1},{2,6},{6,2},{3,7},{7,3},{8,12},{12,8},{9,1... | collective-permute-start | bytes 3145736 | tf_op jit(solution)/shard_map/ppermute | solution.py:31
  1264.3 156.8 %collective-permute-start.54 = (bf16[512,1024]{0,1:T(8,128)(2,1)}, bf16[512,1024]{0,1:T(8,128)(2,1)}, u32[]{:S(2)}, u32[]{:S(2)}) collective-permute-start(bf16[512,1024]{0,1:T(8,128)(2,1)} %reduce-scatter.9.cloned.1.call-done), channel_id=1, source_target_pairs={{0,4},{4,0},{1,5},{5,1},{2,6},{6,2},{3,7},{7,3},{8,12},{12,8},{9,1... | collective-permute-start | bytes 3145736 | tf_op jit(solution)/shard_map/ppermute | solution.py:31
  1267.0 199.1 %collective-permute-start.55 = (bf16[512,2048]{1,0:T(8,128)(2,1)}, bf16[512,2048]{1,0:T(8,128)(2,1)}, u32[]{:S(2)}, u32[]{:S(2)}) collective-permute-start(bf16[512,2048]{1,0:T(8,128)(2,1)} %reduce-scatter.13.cloned.1.call-done), channel_id=1, source_target_pairs={{0,4},{4,0},{1,5},{5,1},{2,6},{6,2},{3,7},{7,3},{8,12},{12,8},{9,1... | collective-permute-start | bytes 6291464 | tf_op jit(solution)/shard_map/ppermute | solution.py:31
  (88 other events, 2384.0 us)
Sparse Core Ops, SparseCore 0:
  10.4 55.2 all-gather.8
  68.2 52.5 all-gather.10
  123.2 87.4 all-gather.12
  212.4 52.4 all-gather.16
  266.6 87.4 all-gather.14
  355.8 52.4 all-gather.18
  842.1 50.9 reduce-scatter.16
  936.1 51.1 reduce-scatter.8
  990.3 86.3 reduce-scatter.12
  1079.5 52.5 reduce-scatter.14
  1135.1 52.5 reduce-scatter.6
  1190.6 86.6 reduce-scatter.10

commit v2 on v1

--- a/solution.py
+++ b/solution.py
@@ -54,9 +54,30 @@
     return slots[0]
 
 
+def join_kernel(*refs):
+    rows = refs[0].shape[0]
+    for k, block in enumerate(refs[:-1]):
+        refs[-1][k * rows : (k + 1) * rows, :] = block[...]
+
+
+def join(blocks):
+    rows, dim = blocks[0].shape
+    cols = dim // 4
+    total = rows * len(blocks)
+    return pl.pallas_call(
+        join_kernel,
+        grid=(4,),
+        in_specs=[pl.BlockSpec((rows, cols), lambda i: (0, i))] * len(blocks),
+        out_specs=pl.BlockSpec((total, cols), lambda i: (0, i)),
+        out_shape=jax.ShapeDtypeStruct((total, dim), blocks[0].dtype),
+        compiler_params=pltpu.CompilerParams(vmem_limit_bytes=24 * 1024 * 1024),
+        cost_estimate=pl.CostEstimate(flops=0, bytes_accessed=4 * total * dim, transcendentals=0),
+    )(*blocks)
+
+
 def gather_rows(local):
     blocks = gather_slots(local, "tp")
-    return jnp.concatenate([b[h] for h in range(2) for b in blocks], axis=0)
+    return join([b[h] for h in range(2) for b in blocks])
 
 
 def scatter_rows(full, rows):
@@ -434,7 +455,7 @@
         normed = lax.optimization_barrier(normed.astype(BF))
         blocks.append(gather_slots(normed, "tp"))
         factor_one.append(factor)
-    normed_rows = jnp.concatenate(blocks[0] + blocks[1], axis=0)
+    normed_rows = join(blocks[0] + blocks[1])
     qkv, mixed, lse = [], [], []
     for part, weight in enumerate(w_qkvo):
         qkv_rows = qkv_project(normed_rows, weight, cos_tab, sin_a, sin_b)
@@ -454,7 +475,7 @@
         normed, factor_two[h] = norm_forward(middle[h], gain_two)
         normed = lax.optimization_barrier(normed.astype(BF))
         two_blocks[h] = gather_slots(normed, "tp")
-    two_rows = jnp.concatenate(two_blocks[0] + two_blocks[1], axis=0)
+    two_rows = join(two_blocks[0] + two_blocks[1])
 
     g_mine, g_other = parted(out_grad)
     g_got = swap(g_other, "seg", 1)
@@ -480,7 +501,7 @@
         sig = jax.nn.sigmoid(gate32)
         grad_gate = (grad_hidden * up32 * sig * (1.0 + gate32 * (1.0 - sig))).astype(BF)
         grad_up = (grad_hidden * gate32 * sig).astype(BF)
-        grad_parts.append(jnp.concatenate([grad_gate, grad_up], axis=1))
+        grad_parts += [grad_gate, grad_up]
 
     def reduce_rows(full):
         return lax.psum_scatter(full.astype(BF), "fsdp", scatter_dimension=0, tiled=True)
@@ -490,12 +511,15 @@
         return sums[OWN].astype(F32) + swap(sums[OTHER], "seg", 1).astype(F32)
 
     grad_down = reduce_parts([mul(grad_rows, hidden[c], TN) for c in range(2)]).T
-    grad_gu = reduce_parts([mul(two_rows, grad_parts[c], TN) for c in range(2)])
+    copies = lax.optimization_barrier(grad_parts)
+    terms = [mul(two_rows, jnp.concatenate(copies[2 * c : 2 * c + 2], axis=1), TN) for c in range(2)]
+    grad_gu = reduce_parts(terms)
     grad_gu = grad_gu.reshape(depth, 2, ff)
     grad_middle, gain_two_terms, mid_blocks = [None, None], [], [None, None]
     for h in range(2):
         weights = w_gu if h == 0 else lax.optimization_barrier(w_gu)
-        grads = jnp.concatenate([g[h * half : (h + 1) * half] for g in grad_parts], axis=1)
+        grads = grad_parts if h == 0 else lax.optimization_barrier(grad_parts)
+        grads = jnp.concatenate([g[h * half : (h + 1) * half] for g in grads], axis=1)
         product = mul(grads, jnp.concatenate(weights, axis=1), NT)
         grad_two = scatter_half(product.astype(BF), rows)
         if h == 1:
@@ -504,7 +528,7 @@
         gain_two_terms.append(gain_term)
         grad_middle[h] = grad_result[h] + grad_resid
         mid_blocks[h] = gather_slots(lax.optimization_barrier(grad_middle[h].astype(BF)), "tp")
-    mid_rows = jnp.concatenate(mid_blocks[0] + mid_blocks[1], axis=0)
+    mid_rows = join(mid_blocks[0] + mid_blocks[1])
     projected = after(projected, mid_blocks[1][0])
     result_live = [((middle[h] + projected[h]) * live[h]).astype(BF) for h in range(2)]
     raws, qkvo_terms = {}, {}

time: 1490 us -> 1340 us (0.90)
  waiting for transfers between devices: 755 us -> 612 us
  local copies, waits for them, and re-layouts: 108 us -> 92.8 us
    ppermute x57, waiting for transfers between devices: 754 us -> 611 us  [swap(): return lax.ppermute(x, axis, [(i, i ^ bit) for i in range(size)])]
    unnamed x167 -> x143, local copies, waits for them, and re-layouts: 63.1 us -> 30.8 us
  transfers between devices with their start and end apart: 69 -> 69, of which waited for: 24 -> 25; matrix products, arithmetic and copies ran while one was open for 28% -> 28% of each run, Pallas kernels for 12% -> 14%
where the time goes in v2:
time: 1340 us
  waiting for transfers between devices  612 us (46%)
  matrix products  306 us (23%)
  Pallas kernels  190 us (14%)
  local copies, waits for them, and re-layouts  92.8 us (7%)
  other arithmetic  83 us (6%)
  starting transfers between devices  30.6 us (2%)
  between operations  15.8 us (1%)
    ppermute x57, waiting for transfers between devices, swap(): return lax.ppermute(x, axis, [(i, i ^ bit) for i in range(size)])  611 us
    dot_general x23, matrix products, mul(): return lax.dot_general(a, b, (dims, ((), ())), preferred_element_type=F32)  306 us
    pallas_call x2, Pallas kernels, attend_back(): pl.pallas_call(functools.partial(attend_back_kernel, group), grid_spec=pl...  88.2 us
    pallas_call x2, Pallas kernels, attend(): pl.pallas_call(functools.partial(attend_kernel, group), grid_spec=pltpu.P...  62.9 us
    unnamed x143, local copies, waits for them, and re-layouts  30.8 us
    ppermute x57, starting transfers between devices, swap(): return lax.ppermute(x, axis, [(i, i ^ bit) for i in range(size)])  30.1 us
    pallas_call x2, Pallas kernels, qkv_project(): pl.pallas_call(qkv_kernel, grid=(seq // row_block,), in_specs=[pl.BlockSp...  27.3 us
  transfers between devices with their start and end apart: 69, of which 25 were waited for; matrix products, arithmetic and copies ran while one was open for 28% of the time, Pallas kernels for 14%

profile of v2, /device:TPU:0, one launch (start us, length us, event | category | flops | bytes accessed | tf_op | source)
XLA Modules:
  0.0 1337.2 jit_solution(3286364220025422593)
XLA Ops:
  15.5 45.9 %collective-permute-done.7 = bf16[512,1024]{1,0:T(8,128)(2,1)} collective-permute-done((bf16[512,1024]{1,0:T(8,128)(2,1)}, bf16[512,1024]{1,0:T(8,128)(2,1)}, u32[]{:S(2)}, u32[]{:S(2)}) %collective-permute-start.7) | collective-permute-done | bytes 1048608 | tf_op jit(solution)/shard_map/ppermute | solution.py:31
  61.6 47.8 %collective-permute-done.21 = bf16[512,1024]{0,1:T(8,128)(2,1)} collective-permute-done((bf16[512,1024]{0,1:T(8,128)(2,1)S(1)}, bf16[512,1024]{0,1:T(8,128)(2,1)}, u32[]{:S(2)}, u32[]{:S(2)}) %collective-permute-start.21) | collective-permute-done | bytes 1048608 | tf_op jit(solution)/shard_map/ppermute | solution.py:31
  114.2 7.9 all-gather.1
  132.8 29.4 %collective-permute-done.3 = bf16[256,2048]{1,0:T(8,128)(2,1)S(1)} collective-permute-done((bf16[256,2048]{1,0:T(8,128)(2,1)}, bf16[256,2048]{1,0:T(8,128)(2,1)S(1)}, u32[]{:S(2)}, u32[]{:S(2)}) %collective-permute-start.3) | collective-permute-done | bytes 1048608 | tf_op jit(solution)/shard_map/ppermute | solution.py:31
  167.9 7.2 collective-permute-done.1.refs_2_
  175.1 44.2 %collective-permute-done.5.refs_6_ = bf16[256,2048]{1,0:T(8,128)(2,1)} collective-permute-done((bf16[256,2048]{1,0:T(8,128)(2,1)S(1)}, bf16[256,2048]{1,0:T(8,128)(2,1)}, u32[]{:S(2)}, u32[]{:S(2)}) %collective-permute-start.5) | collective-permute-done | bytes 1048608 | tf_op jit(solution)/shard_map/ppermute | solution.py:31
  241.2 13.4 %qkv_project.2.qkv_ref = bf16[2048,768]{1,0:T(8,128)(2,1)} custom-call(bf16[2048,2048]{1,0:T(8,128)(2,1)} %copy-done, bf16[2048,1024]{1,0:T(8,128)(2,1)} %all-gather.9.cloned.1.call-done.w_ref, f32[2048,128]{1,0:T(8,128)} %get-tuple-element.142.cos_ref, f32[2048,128]{1,0:T(8,128)} %get-tuple-element.139.sa_ref, f32[2048,128]{1,0:T(8,128)} %get-tuple-element.138.sb_ref), custom_call_target="tpu_custom_call" | custom-call | flops 6442450944 | bytes 14680064 | tf_op jit(solution)/shard_map/qkv_project/pallas_call | solution.py:118
  254.6 31.6 %attend.2 = (bf16[2048,256]{1,0:T(8,128)(2,1)}, f32[2,8,2,256]{3,2,1,0:T(2,128)}) custom-call(s32[3]{0:T(128)} %pad_add_fusion.info_ref, bf16[2048,768]{1,0:T(8,128)(2,1)} %qkv_project.2.qkv_ref), custom_call_target="tpu_custom_call" | custom-call | flops 8589934592 | bytes 4194304 | tf_op jit(solution)/shard_map/attend/pallas_call | solution.py:209
  289.6 13.9 %qkv_project.3.qkv_ref = bf16[2048,768]{1,0:T(8,128)(2,1)} custom-call(bf16[2048,2048]{1,0:T(8,128)(2,1)} %copy-done, bf16[2048,1024]{1,0:T(8,128)(2,1)} %all-gather.11.cloned.1.call-done.w_ref, f32[2048,128]{1,0:T(8,128)} %get-tuple-element.142.cos_ref, f32[2048,128]{1,0:T(8,128)} %get-tuple-element.139.sa_ref, f32[2048,128]{1,0:T(8,128)} %get-tuple-element.138.sb_ref), custom_call_target="tpu_custom_call" | custom-call | flops 6442450944 | bytes 14680064 | tf_op jit(solution)/shard_map/qkv_project/pallas_call | solution.py:118
  303.5 31.3 %attend.3 = (bf16[2048,256]{1,0:T(8,128)(2,1)}, f32[2,8,2,256]{3,2,1,0:T(2,128)}) custom-call(s32[3]{0:T(128)} %pad_add_fusion.info_ref, bf16[2048,768]{1,0:T(8,128)(2,1)} %qkv_project.3.qkv_ref), custom_call_target="tpu_custom_call" | custom-call | flops 8589934592 | bytes 4194304 | tf_op jit(solution)/shard_map/attend/pallas_call | solution.py:209
  357.1 21.1 %collective-permute-done.10 = bf16[256,2048]{1,0:T(8,128)(2,1)S(1)} collective-permute-done((bf16[256,2048]{1,0:T(8,128)(2,1)S(1)}, bf16[256,2048]{1,0:T(8,128)(2,1)S(1)}, u32[]{:S(2)}, u32[]{:S(2)}) %collective-permute-start.10) | collective-permute-done | bytes 1048608 | tf_op jit(solution)/shard_map/ppermute | solution.py:31
  379.9 20.7 %collective-permute-done.16 = bf16[256,2048]{1,0:T(8,128)(2,1)S(1)} collective-permute-done((bf16[256,2048]{1,0:T(8,128)(2,1)S(1)}, bf16[256,2048]{1,0:T(8,128)(2,1)S(1)}, u32[]{:S(2)}, u32[]{:S(2)}) %collective-permute-start.16) | collective-permute-done | bytes 1048608 | tf_op jit(solution)/shard_map/ppermute | solution.py:31
  410.7 12.4 collective-permute-done.12.refs_2_
  423.2 21.9 %collective-permute-done.18.refs_6_ = bf16[256,2048]{1,0:T(8,128)(2,1)} collective-permute-done((bf16[256,2048]{1,0:T(8,128)(2,1)S(1)}, bf16[256,2048]{1,0:T(8,128)(2,1)}, u32[]{:S(2)}, u32[]{:S(2)}) %collective-permute-start.18) | collective-permute-done | bytes 1048608 | tf_op jit(solution)/shard_map/ppermute | solution.py:31
  445.1 14.6 %fusion.187 = f32[2048,1024]{1,0:T(8,128)} fusion(bf16[2048,2048]{1,0:T(8,128)(2,1)} %copy-done.1, bf16[2048,1024]{0,1:T(8,128)(2,1)} %all-gather.19.cloned.1.call-done), kind=kOutput, calls=%fused_computation.285 | convolution fusion | flops 8589934592 | bytes 20971520 | tf_op jit(solution)/shard_map/dot_general | solution.py:350
  466.8 12.6 fusion.98
  479.4 11.9 fusion.62
  491.3 18.7 %fusion.23 = (bf16[2048,1024]{1,0:T(8,128)(2,1)S(1)}, bf16[2048,1024]{1,0:T(8,128)(2,1)S(1)}) fusion(bf16[2048,1024]{1,0:T(8,128)(2,1)} %copy-done.66, bf16[2048,1024]{1,0:T(8,128)(2,1)} %get-tuple-element.35, bf16[2048,2048]{1,0:T(8,128)(2,1)} %copy-done.1, bf16[2048,1024]{0,1:T(8,128)(2,1)} %all-gather.17.cloned.1.call-done), kind=kOutput, calls=%fused_computation.33 | convolution fusion | flops 8621391872 | bytes 29360128 | tf_op jit(solution)/shard_map/dot_general | solution.py:350
  514.8 12.6 fusion.104
  527.4 15.1 %fusion.61 = (bf16[2048,1024]{1,0:T(8,128)(2,1)}, bf16[2048,1024]{1,0:T(8,128)(2,1)S(1)}) fusion(bf16[2048,1024]{1,0:T(8,128)(2,1)S(1)} %fusion.104, bf16[2048,2048]{1,0:T(8,128)(2,1)} %copy-done.2, bf16[2048,2048]{1,0:T(8,128)(2,1)} %all-gather.15.cloned.1.call-done), kind=kOutput, calls=%fused_computation.71 | convolution fusion | flops 8608808960 | bytes 25165824 | tf_op jit(solution)/shard_map/dot_general | solution.py:350
  557.5 29.3 %fusion.86 = bf16[1024,2048]{1,0:T(8,128)(2,1)} fusion(bf16[2048,2048]{1,0:T(8,128)(2,1)} %all-gather.15.cloned.1.call-done, bf16[2048,2048]{1,0:T(8,128)(2,1)} %all-gather.13.cloned.1.call-done, bf16[1024,1024]{1,0:T(8,128)(2,1)} %slice.343, bf16[1024,1024]{1,0:T(8,128)(2,1)} %slice.342, bf16[1024,1024]{1,0:T(8,128)(2,1)S(1)} %slice.341, ...), kind=kOutput, calls=%fused_computation.108 | convolution fusion | flops 17249075200 | bytes 29360128 | tf_op jit(solution)/shard_map/dot_general | solution.py:350
  590.5 28.9 %fusion.91 = bf16[1024,2048]{1,0:T(8,128)(2,1)} fusion(bf16[2048,2048]{1,0:T(8,128)(2,1)} %all-gather.15.cloned.1.call-done, bf16[2048,2048]{1,0:T(8,128)(2,1)} %all-gather.13.cloned.1.call-done, bf16[1024,1024]{1,0:T(8,128)(2,1)S(1)} %copy-done.33, bf16[1024,1024]{1,0:T(8,128)(2,1)} %slice.271, bf16[1024,1024]{1,0:T(8,128)(2,1)} %slice.270, ...), kind=kOutput, calls=%fused_computation.109 | convolution fusion | flops 17249075200 | bytes 29360128 | tf_op jit(solution)/shard_map/dot_general | solution.py:350
  626.5 13.0 convolution_convert_fusion.2
  643.4 9.1 collective-permute-done.34
  659.6 15.3 %collective-permute-done.31 = bf16[256,2048]{1,0:T(8,128)(2,1)S(1)} collective-permute-done((bf16[256,2048]{1,0:T(8,128)(2,1)S(1)}, bf16[256,2048]{1,0:T(8,128)(2,1)S(1)}, u32[]{:S(2)}, u32[]{:S(2)}) %collective-permute-start.31) | collective-permute-done | bytes 1048608 | tf_op jit(solution)/shard_map/ppermute | solution.py:31
  681.2 16.1 %collective-permute-done.37.refs_2_ = bf16[256,2048]{1,0:T(8,128)(2,1)S(1)} collective-permute-done((bf16[256,2048]{1,0:T(8,128)(2,1)S(1)}, bf16[256,2048]{1,0:T(8,128)(2,1)S(1)}, u32[]{:S(2)}, u32[]{:S(2)}) %collective-permute-start.37) | collective-permute-done | bytes 1048608 | tf_op jit(solution)/shard_map/ppermute | solution.py:31
  697.4 22.0 %collective-permute-done.40.refs_6_ = bf16[256,2048]{1,0:T(8,128)(2,1)S(1)} collective-permute-done((bf16[256,2048]{1,0:T(8,128)(2,1)S(1)}, bf16[256,2048]{1,0:T(8,128)(2,1)S(1)}, u32[]{:S(2)}, u32[]{:S(2)}) %collective-permute-start.40) | collective-permute-done | bytes 1048608 | tf_op jit(solution)/shard_map/ppermute | solution.py:31
  731.8 44.1 %attend_back.3 = bf16[2048,768]{1,0:T(8,128)(2,1)} custom-call(s32[3]{0:T(128)} %pad_add_fusion.info_ref, bf16[2048,768]{1,0:T(8,128)(2,1)} %qkv_project.3.qkv_ref, bf16[2048,256]{1,0:T(8,128)(2,1)} %get-tuple-element.31.o_ref, bf16[2048,256]{1,0:T(8,128)(2,1)} %convolution_convert_fusion.8.do_ref, f32[2,8,2,256]{3,2,1,0:T(2,128)} %get-tuple-element.48.lse_ref, ...), custom_call_target="tpu_custom_call" | custom-call | flops 21474836480 | bytes 8388608 | tf_op jit(solution)/shard_map/attend_back/pallas_call | solution.py:308
  775.9 10.2 convolution_convert_fusion.4
  788.5 23.8 %fusion.63 = bf16[2048,2048]{1,0:T(8,128)(2,1)} fusion(bf16[2048,2048]{1,0:T(8,128)(2,1)} %copy-done.2, bf16[2048,1024]{1,0:T(8,128)(2,1)} %copy-done.19, bf16[2048,1024]{1,0:T(8,128)(2,1)} %copy-done.20), kind=kOutput, calls=%fused_computation.73 | convolution fusion | flops 17200840704 | bytes 25165824 | tf_op jit(solution)/shard_map/dot_general | solution.py:350
  812.4 14.0 %convolution_convert_fusion.3 = bf16[2048,1024]{1,0:T(8,128)(2,1)} fusion(bf16[2048,2048]{1,0:T(8,128)(2,1)} %copy-done.1, bf16[2048,1024]{1,0:T(8,128)(2,1)} %get-tuple-element.33), kind=kOutput, calls=%fused_computation.119 | convolution fusion | flops 8592031744 | bytes 16777216 | tf_op jit(solution)/shard_map/dot_general | solution.py:350
  827.7 5.8 convolution_convert_fusion.7
  833.5 7.0 convolution_convert_fusion.9.do_ref
  840.5 44.2 %attend_back.2 = bf16[2048,768]{1,0:T(8,128)(2,1)} custom-call(s32[3]{0:T(128)} %pad_add_fusion.info_ref, bf16[2048,768]{1,0:T(8,128)(2,1)} %qkv_project.2.qkv_ref, bf16[2048,256]{1,0:T(8,128)(2,1)} %get-tuple-element.30.o_ref, bf16[2048,256]{1,0:T(8,128)(2,1)} %convolution_convert_fusion.9.do_ref, f32[2,8,2,256]{3,2,1,0:T(2,128)} %get-tuple-element.47.lse_ref, ...), custom_call_target="tpu_custom_call" | custom-call | flops 21474836480 | bytes 8388608 | tf_op jit(solution)/shard_map/attend_back/pallas_call | solution.py:308
  884.7 10.4 convolution_convert_fusion.5
  897.6 23.7 %fusion.66 = bf16[2048,2048]{1,0:T(8,128)(2,1)} fusion(bf16[2048,2048]{1,0:T(8,128)(2,1)} %copy-done.2, bf16[2048,1024]{1,0:T(8,128)(2,1)} %copy-done.24, bf16[2048,1024]{1,0:T(8,128)(2,1)} %copy-done.26), kind=kOutput, calls=%fused_computation.74 | convolution fusion | flops 17200840704 | bytes 25165824 | tf_op jit(solution)/shard_map/dot_general | solution.py:350
  921.3 22.4 %fusion.69 = bf16[2048,2048]{1,0:T(8,128)(2,1)S(1)} fusion(bf16[2048,1024]{0,1:T(8,128)(2,1)} %all-gather.19.cloned.1.call-done, bf16[2048,1024]{0,1:T(8,128)(2,1)} %all-gather.17.cloned.1.call-done, bf16[2048,1024]{1,0:T(8,128)(2,1)} %get-tuple-element.34, bf16[2048,1024]{1,0:T(8,128)(2,1)} %get-tuple-element.33), kind=kOutput, calls=%fused_computation.75 | convolution fusion | flops 17217617920 | bytes 25165824 | tf_op jit(solution)/shard_map/dot_general | solution.py:350
  956.8 9.1 fusion.97
  967.8 9.5 fusion.96
  977.8 22.1 %collective-permute-done.24 = bf16[2,256,2048]{2,1,0:T(8,128)(2,1)} collective-permute-done((bf16[2,256,2048]{2,1,0:T(8,128)(2,1)}, bf16[2,256,2048]{2,1,0:T(8,128)(2,1)}, u32[]{:S(2)}, u32[]{:S(2)}) %collective-permute-start.24) | collective-permute-done | bytes 2097184 | tf_op jit(solution)/shard_map/ppermute | solution.py:31
  1008.3 22.2 %collective-permute-done.47 = bf16[256,2048]{1,0:T(8,128)(2,1)S(1)} collective-permute-done((bf16[256,2048]{1,0:T(8,128)(2,1)S(1)}, bf16[256,2048]{1,0:T(8,128)(2,1)S(1)}, u32[]{:S(2)}, u32[]{:S(2)}) %collective-permute-start.47) | collective-permute-done | bytes 1048608 | tf_op jit(solution)/shard_map/ppermute | solution.py:31
  1032.1 42.4 %collective-permute-done.44 = bf16[256,2048]{1,0:T(8,128)(2,1)S(1)} collective-permute-done((bf16[256,2048]{1,0:T(8,128)(2,1)S(1)}, bf16[256,2048]{1,0:T(8,128)(2,1)S(1)}, u32[]{:S(2)}, u32[]{:S(2)}) %collective-permute-start.44) | collective-permute-done | bytes 1048608 | tf_op jit(solution)/shard_map/ppermute | solution.py:31
  1090.2 23.3 %collective-permute-done.52 = f32[2,2048]{1,0:T(2,128)S(1)} collective-permute-done((f32[2,2048]{1,0:T(2,128)S(1)}, f32[2,2048]{1,0:T(2,128)S(1)}, u32[]{:S(2)}, u32[]{:S(2)}) %collective-permute-start.52) | collective-permute-done | bytes 16416 | tf_op jit(solution)/shard_map/ppermute | solution.py:31
  1122.0 106.5 %collective-permute-done.53 = f32[2,2048]{1,0:T(2,128)S(1)} collective-permute-done((f32[2,2048]{1,0:T(2,128)S(1)}, f32[2,2048]{1,0:T(2,128)S(1)}, u32[]{:S(2)}, u32[]{:S(2)}) %collective-permute-start.53) | collective-permute-done | bytes 16416 | tf_op jit(solution)/shard_map/ppermute | solution.py:31
  1230.7 20.3 %collective-permute-done.56 = bf16[512,1024]{1,0:T(8,128)(2,1)} collective-permute-done((bf16[512,1024]{1,0:T(8,128)(2,1)}, bf16[512,1024]{1,0:T(8,128)(2,1)}, u32[]{:S(2)}, u32[]{:S(2)}) %collective-permute-start.56) | collective-permute-done | bytes 1048608 | tf_op jit(solution)/shard_map/ppermute | solution.py:31
  1254.8 18.7 %collective-permute-done.54 = bf16[512,1024]{0,1:T(8,128)(2,1)} collective-permute-done((bf16[512,1024]{0,1:T(8,128)(2,1)}, bf16[512,1024]{0,1:T(8,128)(2,1)}, u32[]{:S(2)}, u32[]{:S(2)}) %collective-permute-start.54) | collective-permute-done | bytes 1048608 | tf_op jit(solution)/shard_map/ppermute | solution.py:31
  1284.4 34.0 %collective-permute-done.55 = bf16[512,2048]{1,0:T(8,128)(2,1)} collective-permute-done((bf16[512,2048]{1,0:T(8,128)(2,1)}, bf16[512,2048]{1,0:T(8,128)(2,1)}, u32[]{:S(2)}, u32[]{:S(2)}) %collective-permute-start.55) | collective-permute-done | bytes 2097184 | tf_op jit(solution)/shard_map/ppermute | solution.py:31
  1323.4 6.6 reshape.484
  (393 shorter events, 233.2 us)
Async XLA Ops:
  7.2 232.8 %all-gather.9.cloned.1.call-start = ((), (), s32[]{:S(2)}) async-start(), calls=%async_computation.6 | async-start | bytes 5242880 | tf_op jit(solution)/shard_map/all_gather | solution.py:380
  11.3 276.9 %all-gather.11.cloned.1.call-start = ((), (), s32[]{:S(2)}) async-start(), calls=%async_computation.7 | async-start | bytes 5242880 | tf_op jit(solution)/shard_map/all_gather | solution.py:380
  11.4 50.1 %collective-permute-start.7 = (bf16[512,1024]{1,0:T(8,128)(2,1)}, bf16[512,1024]{1,0:T(8,128)(2,1)}, u32[]{:S(2)}, u32[]{:S(2)}) collective-permute-start(bf16[512,1024]{1,0:T(8,128)(2,1)} %pad_maximum_fusion.12), channel_id=1, source_target_pairs={{0,4},{4,0},{1,5},{5,1},{2,6},{6,2},{3,7},{7,3},{8,12},{12,8},{9,1... | collective-permute-start | bytes 3145736 | tf_op jit(solution)/shard_map/ppermute | solution.py:31
  61.5 383.7 %all-gather.19.cloned.1.call-start = ((), (), s32[]{:S(2)}) async-start(), calls=%async_computation.11 | async-start | bytes 5242880 | tf_op jit(solution)/shard_map/all_gather | solution.py:380
  61.5 47.9 %collective-permute-start.21 = (bf16[512,1024]{0,1:T(8,128)(2,1)S(1)}, bf16[512,1024]{0,1:T(8,128)(2,1)}, u32[]{:S(2)}, u32[]{:S(2)}) collective-permute-start(bf16[512,1024]{0,1:T(8,128)(2,1)S(1)} %bitcast.155), channel_id=1, source_target_pairs={{0,4},{4,0},{1,5},{5,1},{2,6},{6,2},{3,7},{7,3},{8,12},{12,8},{9,1... | collective-permute-start | bytes 3145736 | tf_op jit(solution)/shard_map/ppermute | solution.py:31
  109.4 357.4 %all-gather.13.cloned.1.call-start = ((), (), s32[]{:S(2)}) async-start(), calls=%async_computation.8 | async-start | bytes 10485760 | tf_op jit(solution)/shard_map/all_gather | solution.py:380
  113.0 378.3 %all-gather.17.cloned.1.call-start = ((), (), s32[]{:S(2)}) async-start(), calls=%async_computation.10 | async-start | bytes 5242880 | tf_op jit(solution)/shard_map/all_gather | solution.py:380
  114.1 48.0 %collective-permute-start.3 = (bf16[256,2048]{1,0:T(8,128)(2,1)}, bf16[256,2048]{1,0:T(8,128)(2,1)S(1)}, u32[]{:S(2)}, u32[]{:S(2)}) collective-permute-start(bf16[256,2048]{1,0:T(8,128)(2,1)} %dynamic-slice_bitcast_fusion.2), channel_id=1, source_target_pairs={{0,4},{4,0},{1,5},{5,1},{2,6},{6,2},{3,7},{7,3},{8,12},{12,8},{9,1... | collective-permute-start | bytes 3145736 | tf_op jit(solution)/shard_map/ppermute | solution.py:31
  126.3 104.3 %collective-permute-start = (bf16[256,2048]{1,0:T(8,128)(2,1)S(1)}, bf16[256,2048]{1,0:T(8,128)(2,1)S(1)}, u32[]{:S(2)}, u32[]{:S(2)}) collective-permute-start(bf16[256,2048]{1,0:T(8,128)(2,1)S(1)} %fusion.128.refs_0_), channel_id=1, source_target_pairs={{0,1},{1,0},{2,3},{3,2},{4,5},{5,4},{6,7},{7,6},{8,9},{9,8},{10,11... | collective-permute-start | bytes 3145736 | tf_op jit(solution)/shard_map/ppermute | solution.py:31
  126.4 48.7 %collective-permute-start.1 = (bf16[256,2048]{1,0:T(8,128)(2,1)S(1)}, bf16[256,2048]{1,0:T(8,128)(2,1)}, u32[]{:S(2)}, u32[]{:S(2)}) collective-permute-start(bf16[256,2048]{1,0:T(8,128)(2,1)S(1)} %fusion.128.refs_0_), channel_id=1, source_target_pairs={{0,2},{1,3},{2,0},{3,1},{4,6},{5,7},{6,4},{7,5},{8,10},{9,11},{10,... | collective-permute-start | bytes 3145736 | tf_op jit(solution)/shard_map/ppermute | solution.py:31
  128.3 386.4 %all-gather.15.cloned.1.call-start = ((), (), s32[]{:S(2)}) async-start(), calls=%async_computation.9 | async-start | bytes 10485760 | tf_op jit(solution)/shard_map/all_gather | solution.py:380
  131.7 93.4 %collective-permute-start.25 = (bf16[256,2048]{1,0:T(8,128)(2,1)}, bf16[256,2048]{1,0:T(8,128)(2,1)}, u32[]{:S(2)}, u32[]{:S(2)}) collective-permute-start(bf16[256,2048]{1,0:T(8,128)(2,1)} %get-tuple-element.133), channel_id=1, source_target_pairs={{0,4},{4,0},{1,5},{5,1},{2,6},{6,2},{3,7},{7,3},{8,12},{12,8},{9,1... | collective-permute-start | bytes 3145736 | tf_op jit(solution)/shard_map/ppermute | solution.py:31
  164.7 54.6 %collective-permute-start.5 = (bf16[256,2048]{1,0:T(8,128)(2,1)S(1)}, bf16[256,2048]{1,0:T(8,128)(2,1)}, u32[]{:S(2)}, u32[]{:S(2)}) collective-permute-start(bf16[256,2048]{1,0:T(8,128)(2,1)S(1)} %fusion.118.refs_4_), channel_id=1, source_target_pairs={{0,2},{1,3},{2,0},{3,1},{4,6},{5,7},{6,4},{7,5},{8,10},{9,11},{10,... | collective-permute-start | bytes 3145736 | tf_op jit(solution)/shard_map/ppermute | solution.py:31
  167.8 65.4 %collective-permute-start.4 = (bf16[256,2048]{1,0:T(8,128)(2,1)S(1)}, bf16[256,2048]{1,0:T(8,128)(2,1)S(1)}, u32[]{:S(2)}, u32[]{:S(2)}) collective-permute-start(bf16[256,2048]{1,0:T(8,128)(2,1)S(1)} %fusion.118.refs_4_), channel_id=1, source_target_pairs={{0,1},{1,0},{2,3},{3,2},{4,5},{5,4},{6,7},{7,6},{8,9},{9,8},{10,11... | collective-permute-start | bytes 3145736 | tf_op jit(solution)/shard_map/ppermute | solution.py:31
  175.1 58.2 %collective-permute-start.2 = (bf16[256,2048]{1,0:T(8,128)(2,1)}, bf16[256,2048]{1,0:T(8,128)(2,1)S(1)}, u32[]{:S(2)}, u32[]{:S(2)}) collective-permute-start(bf16[256,2048]{1,0:T(8,128)(2,1)} %collective-permute-done.1.refs_2_), channel_id=1, source_target_pairs={{0,1},{1,0},{2,3},{3,2},{4,5},{5,4},{6,7},{7,6},{8,9},{9,8},{10,11... | collective-permute-start | bytes 3145736 | tf_op jit(solution)/shard_map/ppermute | solution.py:31
  225.1 119.0 %collective-permute-start.20 = (bf16[512,2048]{1,0:T(8,128)(2,1)}, bf16[512,2048]{1,0:T(8,128)(2,1)}, u32[]{:S(2)}, u32[]{:S(2)}) collective-permute-start(bf16[512,2048]{1,0:T(8,128)(2,1)} %bitcast.148), channel_id=1, source_target_pairs={{0,4},{4,0},{1,5},{5,1},{2,6},{6,2},{3,7},{7,3},{8,12},{12,8},{9,1... | collective-permute-start | bytes 6291464 | tf_op jit(solution)/shard_map/ppermute | solution.py:31
  230.6 113.6 %collective-permute-start.27 = (bf16[2,256,2048]{2,1,0:T(8,128)(2,1)}, bf16[2,256,2048]{2,1,0:T(8,128)(2,1)}, u32[]{:S(2)}, u32[]{:S(2)}) collective-permute-start(bf16[2,256,2048]{2,1,0:T(8,128)(2,1)} %get-tuple-element.123), channel_id=1, source_target_pairs={{0,2},{1,3},{2,0},{3,1},{4,6},{5,7},{6,4},{7,5},{8,10},{9,11},{10,... | collective-permute-start | bytes 6291464 | tf_op jit(solution)/shard_map/ppermute | solution.py:31
  344.0 58.5 %collective-permute-start.26 = (bf16[2,256,2048]{2,1,0:T(8,128)(2,1)}, bf16[2,256,2048]{2,1,0:T(8,128)(2,1)}, u32[]{:S(2)}, u32[]{:S(2)}) collective-permute-start(bf16[2,256,2048]{2,1,0:T(8,128)(2,1)} %get-tuple-element.123), channel_id=1, source_target_pairs={{0,1},{1,0},{2,3},{3,2},{4,5},{5,4},{6,7},{7,6},{8,9},{9,8},{10,11... | collective-permute-start | bytes 6291464 | tf_op jit(solution)/shard_map/ppermute | solution.py:31
  344.1 772.3 %reduce-scatter.17.cloned.1.call-start = ((), (), s32[]{:S(2)}) async-start(), calls=%async_computation.17 | async-start | bytes 5242880 | tf_op jit(solution)/shard_map/reduce_scatter | solution.py:507
  344.2 60.2 %collective-permute-start.28 = (bf16[2,256,2048]{2,1,0:T(8,128)(2,1)}, bf16[2,256,2048]{2,1,0:T(8,128)(2,1)S(1)}, u32[]{:S(2)}, u32[]{:S(2)}) collective-permute-start(bf16[2,256,2048]{2,1,0:T(8,128)(2,1)} %collective-permute-done.27), channel_id=1, source_target_pairs={{0,1},{1,0},{2,3},{3,2},{4,5},{5,4},{6,7},{7,6},{8,9},{9,8},{10,11... | collective-permute-start | bytes 6291464 | tf_op jit(solution)/shard_map/ppermute | solution.py:31
  355.4 45.2 %collective-permute-start.16 = (bf16[256,2048]{1,0:T(8,128)(2,1)S(1)}, bf16[256,2048]{1,0:T(8,128)(2,1)S(1)}, u32[]{:S(2)}, u32[]{:S(2)}) collective-permute-start(bf16[256,2048]{1,0:T(8,128)(2,1)S(1)} %add_convert_fusion.8), channel_id=1, source_target_pairs={{0,2},{1,3},{2,0},{3,1},{4,6},{5,7},{6,4},{7,5},{8,10},{9,11},{10,... | collective-permute-start | bytes 3145736 | tf_op jit(solution)/shard_map/ppermute | solution.py:31
  379.8 43.4 %collective-permute-start.12 = (bf16[256,2048]{1,0:T(8,128)(2,1)S(1)}, bf16[256,2048]{1,0:T(8,128)(2,1)}, u32[]{:S(2)}, u32[]{:S(2)}) collective-permute-start(bf16[256,2048]{1,0:T(8,128)(2,1)S(1)} %multiply_convert_fusion.1.refs_0_), channel_id=1, source_target_pairs={{0,2},{1,3},{2,0},{3,1},{4,6},{5,7},{6,4},{7,5},{8,10},{9,11},{10,... | collective-permute-start | bytes 3145736 | tf_op jit(solution)/shard_map/ppermute | solution.py:31
  402.4 42.7 %collective-permute-start.18 = (bf16[256,2048]{1,0:T(8,128)(2,1)S(1)}, bf16[256,2048]{1,0:T(8,128)(2,1)}, u32[]{:S(2)}, u32[]{:S(2)}) collective-permute-start(bf16[256,2048]{1,0:T(8,128)(2,1)S(1)} %multiply_convert_fusion.refs_4_), channel_id=1, source_target_pairs={{0,2},{1,3},{2,0},{3,1},{4,6},{5,7},{6,4},{7,5},{8,10},{9,11},{10,... | collective-permute-start | bytes 3145736 | tf_op jit(solution)/shard_map/ppermute | solution.py:31
  410.2 49.5 %collective-permute-start.11 = (bf16[256,2048]{1,0:T(8,128)(2,1)S(1)}, bf16[256,2048]{1,0:T(8,128)(2,1)S(1)}, u32[]{:S(2)}, u32[]{:S(2)}) collective-permute-start(bf16[256,2048]{1,0:T(8,128)(2,1)S(1)} %multiply_convert_fusion.1.refs_0_), channel_id=1, source_target_pairs={{0,1},{1,0},{2,3},{3,2},{4,5},{5,4},{6,7},{7,6},{8,9},{9,8},{10,11... | collective-permute-start | bytes 3145736 | tf_op jit(solution)/shard_map/ppermute | solution.py:31
  410.2 49.5 %collective-permute-start.17 = (bf16[256,2048]{1,0:T(8,128)(2,1)S(1)}, bf16[256,2048]{1,0:T(8,128)(2,1)}, u32[]{:S(2)}, u32[]{:S(2)}) collective-permute-start(bf16[256,2048]{1,0:T(8,128)(2,1)S(1)} %multiply_convert_fusion.refs_4_), channel_id=1, source_target_pairs={{0,1},{1,0},{2,3},{3,2},{4,5},{5,4},{6,7},{7,6},{8,9},{9,8},{10,11... | collective-permute-start | bytes 3145736 | tf_op jit(solution)/shard_map/ppermute | solution.py:31
  423.2 36.5 %collective-permute-start.13 = (bf16[256,2048]{1,0:T(8,128)(2,1)}, bf16[256,2048]{1,0:T(8,128)(2,1)}, u32[]{:S(2)}, u32[]{:S(2)}) collective-permute-start(bf16[256,2048]{1,0:T(8,128)(2,1)} %collective-permute-done.12.refs_2_), channel_id=1, source_target_pairs={{0,1},{1,0},{2,3},{3,2},{4,5},{5,4},{6,7},{7,6},{8,9},{9,8},{10,11... | collective-permute-start | bytes 3145736 | tf_op jit(solution)/shard_map/ppermute | solution.py:31
  590.0 33.2 %collective-permute-start.33 = (bf16[256,2048]{1,0:T(8,128)(2,1)}, bf16[256,2048]{1,0:T(8,128)(2,1)}, u32[]{:S(2)}, u32[]{:S(2)}) collective-permute-start(bf16[256,2048]{1,0:T(8,128)(2,1)} %get-tuple-element.111), channel_id=1, source_target_pairs={{0,1},{1,0},{2,3},{3,2},{4,5},{5,4},{6,7},{7,6},{8,9},{9,8},{10,11... | collective-permute-start | bytes 3145736 | tf_op jit(solution)/shard_map/ppermute | solution.py:31
  622.7 37.0 %collective-permute-start.29 = (bf16[256,2048]{1,0:T(8,128)(2,1)}, bf16[256,2048]{1,0:T(8,128)(2,1)}, u32[]{:S(2)}, u32[]{:S(2)}) collective-permute-start(bf16[256,2048]{1,0:T(8,128)(2,1)} %get-tuple-element.112), channel_id=1, source_target_pairs={{0,1},{1,0},{2,3},{3,2},{4,5},{5,4},{6,7},{7,6},{8,9},{9,8},{10,11... | collective-permute-start | bytes 3145736 | tf_op jit(solution)/shard_map/ppermute | solution.py:31
  639.5 477.0 %reduce-scatter.9.cloned.1.call-start = ((), (), s32[]{:S(2)}) async-start(), calls=%async_computation.13 | async-start | bytes 5242880 | tf_op jit(solution)/shard_map/reduce_scatter | solution.py:507
  641.6 33.3 %collective-permute-start.31 = (bf16[256,2048]{1,0:T(8,128)(2,1)S(1)}, bf16[256,2048]{1,0:T(8,128)(2,1)S(1)}, u32[]{:S(2)}, u32[]{:S(2)}) collective-permute-start(bf16[256,2048]{1,0:T(8,128)(2,1)S(1)} %add_convert_fusion.6), channel_id=1, source_target_pairs={{0,2},{1,3},{2,0},{3,1},{4,6},{5,7},{6,4},{7,5},{8,10},{9,11},{10,... | collective-permute-start | bytes 3145736 | tf_op jit(solution)/shard_map/ppermute | solution.py:31
  659.4 37.9 %collective-permute-start.37 = (bf16[256,2048]{1,0:T(8,128)(2,1)S(1)}, bf16[256,2048]{1,0:T(8,128)(2,1)S(1)}, u32[]{:S(2)}, u32[]{:S(2)}) collective-permute-start(bf16[256,2048]{1,0:T(8,128)(2,1)S(1)} %get-tuple-element.92.refs_0_), channel_id=1, source_target_pairs={{0,2},{1,3},{2,0},{3,1},{4,6},{5,7},{6,4},{7,5},{8,10},{9,11},{10,... | collective-permute-start | bytes 3145736 | tf_op jit(solution)/shard_map/ppermute | solution.py:31
  680.7 38.6 %collective-permute-start.40 = (bf16[256,2048]{1,0:T(8,128)(2,1)S(1)}, bf16[256,2048]{1,0:T(8,128)(2,1)S(1)}, u32[]{:S(2)}, u32[]{:S(2)}) collective-permute-start(bf16[256,2048]{1,0:T(8,128)(2,1)S(1)} %get-tuple-element.90.refs_4_), channel_id=1, source_target_pairs={{0,2},{1,3},{2,0},{3,1},{4,6},{5,7},{6,4},{7,5},{8,10},{9,11},{10,... | collective-permute-start | bytes 3145736 | tf_op jit(solution)/shard_map/ppermute | solution.py:31
  680.7 40.4 %collective-permute-start.36 = (bf16[256,2048]{1,0:T(8,128)(2,1)S(1)}, bf16[256,2048]{1,0:T(8,128)(2,1)S(1)}, u32[]{:S(2)}, u32[]{:S(2)}) collective-permute-start(bf16[256,2048]{1,0:T(8,128)(2,1)S(1)} %get-tuple-element.92.refs_0_), channel_id=1, source_target_pairs={{0,1},{1,0},{2,3},{3,2},{4,5},{5,4},{6,7},{7,6},{8,9},{9,8},{10,11... | collective-permute-start | bytes 3145736 | tf_op jit(solution)/shard_map/ppermute | solution.py:31
  680.7 40.4 %collective-permute-start.39 = (bf16[256,2048]{1,0:T(8,128)(2,1)S(1)}, bf16[256,2048]{1,0:T(8,128)(2,1)S(1)}, u32[]{:S(2)}, u32[]{:S(2)}) collective-permute-start(bf16[256,2048]{1,0:T(8,128)(2,1)S(1)} %get-tuple-element.90.refs_4_), channel_id=1, source_target_pairs={{0,1},{1,0},{2,3},{3,2},{4,5},{5,4},{6,7},{7,6},{8,9},{9,8},{10,11... | collective-permute-start | bytes 3145736 | tf_op jit(solution)/shard_map/ppermute | solution.py:31
  788.5 330.8 %reduce-scatter.13.cloned.1.call-start = ((), (), s32[]{:S(2)}) async-start(), calls=%async_computation.15 | async-start | bytes 10485760 | tf_op jit(solution)/shard_map/reduce_scatter | solution.py:507
  812.4 418.3 %reduce-scatter.15.cloned.1.call-start = ((), (), s32[]{:S(2)}) async-start(), calls=%async_computation.16 | async-start | bytes 5242880 | tf_op jit(solution)/shard_map/reduce_scatter | solution.py:507
  826.5 428.3 %reduce-scatter.7.cloned.1.call-start = ((), (), s32[]{:S(2)}) async-start(), calls=%async_computation.12 | async-start | bytes 5242880 | tf_op jit(solution)/shard_map/reduce_scatter | solution.py:507
  897.5 386.9 %reduce-scatter.11.cloned.1.call-start = ((), (), s32[]{:S(2)}) async-start(), calls=%async_computation.14 | async-start | bytes 10485760 | tf_op jit(solution)/shard_map/reduce_scatter | solution.py:507
  948.9 28.9 %collective-permute-start.22 = (bf16[2,256,2048]{2,1,0:T(8,128)(2,1)}, bf16[2,256,2048]{2,1,0:T(8,128)(2,1)}, u32[]{:S(2)}, u32[]{:S(2)}) collective-permute-start(bf16[2,256,2048]{2,1,0:T(8,128)(2,1)} %get-tuple-element.102), channel_id=1, source_target_pairs={{0,1},{1,0},{2,3},{3,2},{4,5},{5,4},{6,7},{7,6},{8,9},{9,8},{10,11... | collective-permute-start | bytes 6291464 | tf_op jit(solution)/shard_map/ppermute | solution.py:31
  951.9 48.0 %collective-permute-start.24 = (bf16[2,256,2048]{2,1,0:T(8,128)(2,1)}, bf16[2,256,2048]{2,1,0:T(8,128)(2,1)}, u32[]{:S(2)}, u32[]{:S(2)}) collective-permute-start(bf16[2,256,2048]{2,1,0:T(8,128)(2,1)} %fusion.82), channel_id=1, source_target_pairs={{0,2},{1,3},{2,0},{3,1},{4,6},{5,7},{6,4},{7,5},{8,10},{9,11},{10,... | collective-permute-start | bytes 6291464 | tf_op jit(solution)/shard_map/ppermute | solution.py:31
  967.5 36.4 %collective-permute-start.46 = (bf16[256,2048]{1,0:T(8,128)(2,1)}, bf16[256,2048]{1,0:T(8,128)(2,1)S(1)}, u32[]{:S(2)}, u32[]{:S(2)}) collective-permute-start(bf16[256,2048]{1,0:T(8,128)(2,1)} %get-tuple-element.107), channel_id=1, source_target_pairs={{0,1},{1,0},{2,3},{3,2},{4,5},{5,4},{6,7},{7,6},{8,9},{9,8},{10,11... | collective-permute-start | bytes 3145736 | tf_op jit(solution)/shard_map/ppermute | solution.py:31
  1005.3 69.1 %collective-permute-start.44 = (bf16[256,2048]{1,0:T(8,128)(2,1)S(1)}, bf16[256,2048]{1,0:T(8,128)(2,1)S(1)}, u32[]{:S(2)}, u32[]{:S(2)}) collective-permute-start(bf16[256,2048]{1,0:T(8,128)(2,1)S(1)} %add_convert_fusion.2), channel_id=1, source_target_pairs={{0,2},{1,3},{2,0},{3,1},{4,6},{5,7},{6,4},{7,5},{8,10},{9,11},{10,... | collective-permute-start | bytes 3145736 | tf_op jit(solution)/shard_map/ppermute | solution.py:31
  1008.3 78.0 %collective-permute-start.35 = (bf16[256,2048]{1,0:T(8,128)(2,1)}, bf16[256,2048]{1,0:T(8,128)(2,1)}, u32[]{:S(2)}, u32[]{:S(2)}) collective-permute-start(bf16[256,2048]{1,0:T(8,128)(2,1)} %get-tuple-element.109), channel_id=1, source_target_pairs={{0,4},{4,0},{1,5},{5,1},{2,6},{6,2},{3,7},{7,3},{8,12},{12,8},{9,1... | collective-permute-start | bytes 3145736 | tf_op jit(solution)/shard_map/ppermute | solution.py:31
  1089.5 139.5 %collective-permute-start.48 = (bf16[256,2048]{1,0:T(8,128)(2,1)}, bf16[256,2048]{1,0:T(8,128)(2,1)S(1)}, u32[]{:S(2)}, u32[]{:S(2)}) collective-permute-start(bf16[256,2048]{1,0:T(8,128)(2,1)} %fusion.122), channel_id=1, source_target_pairs={{0,4},{4,0},{1,5},{5,1},{2,6},{6,2},{3,7},{7,3},{8,12},{12,8},{9,1... | collective-permute-start | bytes 3145736 | tf_op jit(solution)/shard_map/ppermute | solution.py:31
  1113.4 115.0 %collective-permute-start.53 = (f32[2,2048]{1,0:T(2,128)S(1)}, f32[2,2048]{1,0:T(2,128)S(1)}, u32[]{:S(2)}, u32[]{:S(2)}) collective-permute-start(f32[2,2048]{1,0:T(2,128)S(1)} %add.380), channel_id=1, source_target_pairs={{0,4},{4,0},{1,5},{5,1},{2,6},{6,2},{3,7},{7,3},{8,12},{12,8},{9,1... | collective-permute-start | bytes 49160 | tf_op jit(solution)/shard_map/ppermute | solution.py:31
  1116.4 134.6 %collective-permute-start.56 = (bf16[512,1024]{1,0:T(8,128)(2,1)}, bf16[512,1024]{1,0:T(8,128)(2,1)}, u32[]{:S(2)}, u32[]{:S(2)}) collective-permute-start(bf16[512,1024]{1,0:T(8,128)(2,1)} %reduce-scatter.17.cloned.1.call-done), channel_id=1, source_target_pairs={{0,4},{4,0},{1,5},{5,1},{2,6},{6,2},{3,7},{7,3},{8,12},{12,8},{9,1... | collective-permute-start | bytes 3145736 | tf_op jit(solution)/shard_map/ppermute | solution.py:31
  1116.5 157.0 %collective-permute-start.54 = (bf16[512,1024]{0,1:T(8,128)(2,1)}, bf16[512,1024]{0,1:T(8,128)(2,1)}, u32[]{:S(2)}, u32[]{:S(2)}) collective-permute-start(bf16[512,1024]{0,1:T(8,128)(2,1)} %reduce-scatter.9.cloned.1.call-done), channel_id=1, source_target_pairs={{0,4},{4,0},{1,5},{5,1},{2,6},{6,2},{3,7},{7,3},{8,12},{12,8},{9,1... | collective-permute-start | bytes 3145736 | tf_op jit(solution)/shard_map/ppermute | solution.py:31
  1119.3 199.1 %collective-permute-start.55 = (bf16[512,2048]{1,0:T(8,128)(2,1)}, bf16[512,2048]{1,0:T(8,128)(2,1)}, u32[]{:S(2)}, u32[]{:S(2)}) collective-permute-start(bf16[512,2048]{1,0:T(8,128)(2,1)} %reduce-scatter.13.cloned.1.call-done), channel_id=1, source_target_pairs={{0,4},{4,0},{1,5},{5,1},{2,6},{6,2},{3,7},{7,3},{8,12},{12,8},{9,1... | collective-permute-start | bytes 6291464 | tf_op jit(solution)/shard_map/ppermute | solution.py:31
  (90 other events, 1701.9 us)
Sparse Core Ops, SparseCore 0:
  11.4 55.2 all-gather.8
  68.6 52.6 all-gather.10
  123.1 52.4 all-gather.18
  177.9 87.4 all-gather.12
  267.0 52.4 all-gather.16
  344.3 85.0 all-gather.14
  639.6 51.0 reduce-scatter.16
  788.6 49.8 reduce-scatter.8
  841.6 86.3 reduce-scatter.12
  930.8 52.5 reduce-scatter.14
  986.4 52.5 reduce-scatter.6
  1042.0 86.6 reduce-scatter.10

commit v3 on v2

--- a/solution.py
+++ b/solution.py
@@ -14,6 +14,7 @@
 NORM_EPS = 1e-05
 ROPE_THETA = 130000.0
 BLK = 256
+KEY_STEP = 4
 SEG = 2
 BF = jnp.bfloat16
 F32 = jnp.float32
@@ -163,38 +164,36 @@
             where_q = rows_of(i)
             vt_ref[i] = qkv_ref[where_q, 256:384].T
             q = qkv_ref[where_q, 0:128]
-            outs = []
-            for h in range(2):
-                qt = jnp.where(masks[h], q, jnp.zeros_like(q)).T
-                top = total = acc = None
-                step = 2
-                first = 0
-                while first <= i:
-                    blocks = list(range(first, min(first + step, i + 1)))
-                    scores = []
+            q_t = [jnp.where(masks[h], q, jnp.zeros_like(q)).T for h in range(2)]
+            state = [None, None]
+            for first in range(0, i + 1, KEY_STEP):
+                blocks = range(first, min(first + KEY_STEP, i + 1))
+                scores = [[], []]
+                for h in range(2):
                     for b in blocks:
-                        s = jnp.dot(qkv_ref[rows_of(b), 128:256], qt, preferred_element_type=F32) * (SCALE * LOG2E)
+                        s = jnp.dot(qkv_ref[rows_of(b), 128:256], q_t[h], preferred_element_type=F32) * (SCALE * LOG2E)
                         if b == i:
                             s = jnp.where(diagonal_mask(i, length), s, NEG)
-                        scores.append(s)
-                    new_top = functools.reduce(jnp.maximum, [jnp.max(s, axis=0, keepdims=True) for s in scores])
-                    if top is not None:
-                        new_top = jnp.maximum(top, new_top)
-                        fade = jnp.exp2(top - new_top)
+                        scores[h].append(s)
+                for h in range(2):
+                    top = functools.reduce(jnp.maximum, [jnp.max(s, axis=0, keepdims=True) for s in scores[h]])
+                    total = acc = None
+                    if state[h] is not None:
+                        old_top, total, acc = state[h]
+                        top = jnp.maximum(old_top, top)
+                        fade = jnp.exp2(old_top - top)
                         total, acc = total * fade, acc * fade
-                    for b, s in zip(blocks, scores):
-                        p = jnp.exp2(s - new_top)
+                    for b, s in zip(blocks, scores[h]):
+                        p = jnp.exp2(s - top)
                         p_sum = jnp.sum(p, axis=0, keepdims=True)
-                        mixed = jnp.dot(
-                            vt_ref[b, h * HD : h * HD + HD, :], p.astype(BF), preferred_element_type=F32
-                        )
+                        mixed = jnp.dot(vt_ref[b, h * HD : h * HD + HD, :], p.astype(BF), preferred_element_type=F32)
                         total = p_sum if total is None else total + p_sum
                         acc = mixed if acc is None else acc + mixed
-                    top = new_top
-                    first += step
-                outs.append(acc / total)
+                    state[h] = (top, total, acc)
+            for h in range(2):
+                top, total, _ = state[h]
                 lse_ref[i, h : h + 1, :] = top + jnp.log2(total)
-            o_ref[where_q, :] = jnp.concatenate(outs, axis=0).T.astype(BF)
+            o_ref[where_q, :] = jnp.concatenate([acc / total for _, total, acc in state], axis=0).T.astype(BF)
 
         @pl.when(i * BLK >= length)
         def _():
@@ -256,34 +255,37 @@
             do = do_ref[where_q, :]
             product = (o_ref[where_q, :].astype(F32) * do.astype(F32)).T
             zero = jnp.zeros_like(q)
-            dq_t = []
-            for h in range(2):
-                q_h = jnp.where(masks[h], q, zero)
-                do_h = jnp.where(masks[h], do, zero)
-                qt, dot_t = q_h.T, do_h.T
-                lse = lse_ref[i, h : h + 1, :]
-                delta = jnp.sum(product[h * HD : h * HD + HD], axis=0, keepdims=True)
-                dq = None
-                for b in range(i + 1):
-                    rows_b = rows_of(b)
-                    s = jnp.dot(qkv_ref[rows_b, 128:256], qt, preferred_element_type=F32)
-                    s = s * (SCALE * LOG2E) - lse
+            q_h = [jnp.where(masks[h], q, zero) for h in range(2)]
+            do_h = [jnp.where(masks[h], do, zero) for h in range(2)]
+            q_t, do_t = [x.T for x in q_h], [x.T for x in do_h]
+            q_both, do_both = jnp.concatenate(q_h, axis=0), jnp.concatenate(do_h, axis=0)
+            lse = [lse_ref[i, h : h + 1, :] for h in range(2)]
+            delta = [jnp.sum(product[h * HD : h * HD + HD], axis=0, keepdims=True) for h in range(2)]
+            dq = [None, None]
+            for b in range(i + 1):
+                rows_b = rows_of(b)
+                probs, ds = [], []
+                for h in range(2):
+                    s = jnp.dot(qkv_ref[rows_b, 128:256], q_t[h], preferred_element_type=F32)
+                    s = s * (SCALE * LOG2E) - lse[h]
                     if b == i:
                         s = jnp.where(diagonal_mask(i, length), s, NEG)
                     p = jnp.exp2(s)
-                    dp = jnp.dot(qkv_ref[rows_b, 256:384], dot_t, preferred_element_type=F32)
-                    ds = (p * (dp - delta)).astype(BF)
-                    dv = jnp.dot(p.astype(BF), do_h, preferred_element_type=F32)
-                    dk = jnp.dot(ds, q_h, preferred_element_type=F32)
-                    if b == i and h == 0:
-                        dv_ref[b] = dv
-                        dk_ref[b] = dk
-                    else:
-                        dv_ref[b] += dv
-                        dk_ref[b] += dk
-                    part = jnp.dot(kt_ref[b, h * HD : h * HD + HD, :], ds, preferred_element_type=F32)
-                    dq = part if dq is None else dq + part
-                dq_t.append(rope_back(dq * SCALE, cos_ref[i], sin_ref[i]))
+                    dp = jnp.dot(qkv_ref[rows_b, 256:384], do_t[h], preferred_element_type=F32)
+                    ds.append((p * (dp - delta[h])).astype(BF))
+                    probs.append(p.astype(BF))
+                dv = jnp.dot(jnp.concatenate(probs, axis=1), do_both, preferred_element_type=F32)
+                dk = jnp.dot(jnp.concatenate(ds, axis=1), q_both, preferred_element_type=F32)
+                if b == i:
+                    dv_ref[b] = dv
+                    dk_ref[b] = dk
+                else:
+                    dv_ref[b] += dv
+                    dk_ref[b] += dk
+                for h in range(2):
+                    part = jnp.dot(kt_ref[b, h * HD : h * HD + HD, :], ds[h], preferred_element_type=F32)
+                    dq[h] = part if dq[h] is None else dq[h] + part
+            dq_t = [rope_back(dq[h] * SCALE, cos_ref[i], sin_ref[i]) for h in range(2)]
             d_ref[where_q, 0:128] = jnp.concatenate(dq_t, axis=0).T.astype(BF)
 
         @pl.when(i * BLK >= length)

time: 1340 us -> 1310 us (0.978)
  Pallas kernels: 190 us -> 153 us
    pallas_call x2, Pallas kernels: 88.2 us -> 69.6 us  [attend_back(): pl.pallas_call(functools.partial(attend_back_kernel, group), grid_spec=pl...]
    pallas_call x2, Pallas kernels: 62.9 us -> 44.7 us  [attend(): pl.pallas_call(functools.partial(attend_kernel, group), grid_spec=pltpu.P...]
  transfers between devices with their start and end apart: 69 -> 69, of which waited for: 25 -> 25; matrix products, arithmetic and copies ran while one was open for 28% -> 28% of each run, Pallas kernels for 14% -> 12%
where the time goes in v3:
time: 1310 us; the launch traced here: 1300 us
  waiting for transfers between devices  612 us (47%)
  matrix products  306 us (23%)
  Pallas kernels  153 us (12%)
  local copies, waits for them, and re-layouts  92.6 us (7%)
  other arithmetic  84 us (6%)
  starting transfers between devices  30.8 us (2%)
  between operations  15.6 us (1%)
    ppermute x57, waiting for transfers between devices, swap(): return lax.ppermute(x, axis, [(i, i ^ bit) for i in range(size)])  611 us
    dot_general x23, matrix products, mul(): return lax.dot_general(a, b, (dims, ((), ())), preferred_element_type=F32)  306 us
    pallas_call x2, Pallas kernels, attend_back(): pl.pallas_call(functools.partial(attend_back_kernel, group), grid_spec=pl...  69.6 us
    pallas_call x2, Pallas kernels, attend(): pl.pallas_call(functools.partial(attend_kernel, group), grid_spec=pltpu.P...  44.7 us
    unnamed x143, local copies, waits for them, and re-layouts  30.5 us
    ppermute x57, starting transfers between devices, swap(): return lax.ppermute(x, axis, [(i, i ^ bit) for i in range(size)])  30.3 us
    pallas_call x2, Pallas kernels, qkv_project(): pl.pallas_call(qkv_kernel, grid=(seq // row_block,), in_specs=[pl.BlockSp...  27.2 us
  transfers between devices with their start and end apart: 69, of which 25 were waited for; matrix products, arithmetic and copies ran while one was open for 28% of the time, Pallas kernels for 12%

profile of v3, /device:TPU:0, one launch (start us, length us, event | category | flops | bytes accessed | tf_op | source)
XLA Modules:
  0.0 1300.9 jit_solution(4411686346724403930)
XLA Ops:
  15.5 45.9 %collective-permute-done.7 = bf16[512,1024]{1,0:T(8,128)(2,1)} collective-permute-done((bf16[512,1024]{1,0:T(8,128)(2,1)}, bf16[512,1024]{1,0:T(8,128)(2,1)}, u32[]{:S(2)}, u32[]{:S(2)}) %collective-permute-start.7) | collective-permute-done | bytes 1048608 | tf_op jit(solution)/shard_map/ppermute | solution.py:32
  61.6 47.8 %collective-permute-done.21 = bf16[512,1024]{0,1:T(8,128)(2,1)} collective-permute-done((bf16[512,1024]{0,1:T(8,128)(2,1)S(1)}, bf16[512,1024]{0,1:T(8,128)(2,1)}, u32[]{:S(2)}, u32[]{:S(2)}) %collective-permute-start.21) | collective-permute-done | bytes 1048608 | tf_op jit(solution)/shard_map/ppermute | solution.py:32
  114.2 7.9 all-gather.1
  132.8 29.4 %collective-permute-done.3 = bf16[256,2048]{1,0:T(8,128)(2,1)S(1)} collective-permute-done((bf16[256,2048]{1,0:T(8,128)(2,1)}, bf16[256,2048]{1,0:T(8,128)(2,1)S(1)}, u32[]{:S(2)}, u32[]{:S(2)}) %collective-permute-start.3) | collective-permute-done | bytes 1048608 | tf_op jit(solution)/shard_map/ppermute | solution.py:32
  167.9 7.2 collective-permute-done.1.refs_2_
  175.1 44.2 %collective-permute-done.5.refs_6_ = bf16[256,2048]{1,0:T(8,128)(2,1)} collective-permute-done((bf16[256,2048]{1,0:T(8,128)(2,1)S(1)}, bf16[256,2048]{1,0:T(8,128)(2,1)}, u32[]{:S(2)}, u32[]{:S(2)}) %collective-permute-start.5) | collective-permute-done | bytes 1048608 | tf_op jit(solution)/shard_map/ppermute | solution.py:32
  219.3 6.2 fusion.144
  241.7 13.4 %qkv_project.2.qkv_ref = bf16[2048,768]{1,0:T(8,128)(2,1)} custom-call(bf16[2048,2048]{1,0:T(8,128)(2,1)} %copy-done, bf16[2048,1024]{1,0:T(8,128)(2,1)} %all-gather.9.cloned.1.call-done.w_ref, f32[2048,128]{1,0:T(8,128)} %get-tuple-element.142.cos_ref, f32[2048,128]{1,0:T(8,128)} %get-tuple-element.139.sa_ref, f32[2048,128]{1,0:T(8,128)} %get-tuple-element.138.sb_ref), custom_call_target="tpu_custom_call" | custom-call | flops 6442450944 | bytes 14680064 | tf_op jit(solution)/shard_map/qkv_project/pallas_call | solution.py:119
  255.1 22.3 %attend.2 = (bf16[2048,256]{1,0:T(8,128)(2,1)}, f32[2,8,2,256]{3,2,1,0:T(2,128)}) custom-call(s32[3]{0:T(128)} %pad_add_fusion.info_ref, bf16[2048,768]{1,0:T(8,128)(2,1)} %qkv_project.2.qkv_ref), custom_call_target="tpu_custom_call" | custom-call | flops 8589934592 | bytes 4194304 | tf_op jit(solution)/shard_map/attend/pallas_call | solution.py:208
  280.8 13.8 %qkv_project.3.qkv_ref = bf16[2048,768]{1,0:T(8,128)(2,1)} custom-call(bf16[2048,2048]{1,0:T(8,128)(2,1)} %copy-done, bf16[2048,1024]{1,0:T(8,128)(2,1)} %all-gather.11.cloned.1.call-done.w_ref, f32[2048,128]{1,0:T(8,128)} %get-tuple-element.142.cos_ref, f32[2048,128]{1,0:T(8,128)} %get-tuple-element.139.sa_ref, f32[2048,128]{1,0:T(8,128)} %get-tuple-element.138.sb_ref), custom_call_target="tpu_custom_call" | custom-call | flops 6442450944 | bytes 14680064 | tf_op jit(solution)/shard_map/qkv_project/pallas_call | solution.py:119
  294.6 22.4 %attend.3 = (bf16[2048,256]{1,0:T(8,128)(2,1)}, f32[2,8,2,256]{3,2,1,0:T(2,128)}) custom-call(s32[3]{0:T(128)} %pad_add_fusion.info_ref, bf16[2048,768]{1,0:T(8,128)(2,1)} %qkv_project.3.qkv_ref), custom_call_target="tpu_custom_call" | custom-call | flops 8589934592 | bytes 4194304 | tf_op jit(solution)/shard_map/attend/pallas_call | solution.py:208
  339.2 21.1 %collective-permute-done.10 = bf16[256,2048]{1,0:T(8,128)(2,1)S(1)} collective-permute-done((bf16[256,2048]{1,0:T(8,128)(2,1)S(1)}, bf16[256,2048]{1,0:T(8,128)(2,1)S(1)}, u32[]{:S(2)}, u32[]{:S(2)}) %collective-permute-start.10) | collective-permute-done | bytes 1048608 | tf_op jit(solution)/shard_map/ppermute | solution.py:32
  362.1 20.7 %collective-permute-done.16 = bf16[256,2048]{1,0:T(8,128)(2,1)S(1)} collective-permute-done((bf16[256,2048]{1,0:T(8,128)(2,1)S(1)}, bf16[256,2048]{1,0:T(8,128)(2,1)S(1)}, u32[]{:S(2)}, u32[]{:S(2)}) %collective-permute-start.16) | collective-permute-done | bytes 1048608 | tf_op jit(solution)/shard_map/ppermute | solution.py:32
  392.7 12.6 collective-permute-done.12.refs_2_
  405.4 21.9 %collective-permute-done.18.refs_6_ = bf16[256,2048]{1,0:T(8,128)(2,1)} collective-permute-done((bf16[256,2048]{1,0:T(8,128)(2,1)S(1)}, bf16[256,2048]{1,0:T(8,128)(2,1)}, u32[]{:S(2)}, u32[]{:S(2)}) %collective-permute-start.18) | collective-permute-done | bytes 1048608 | tf_op jit(solution)/shard_map/ppermute | solution.py:32
  427.3 14.6 %fusion.187 = f32[2048,1024]{1,0:T(8,128)} fusion(bf16[2048,2048]{1,0:T(8,128)(2,1)} %copy-done.1, bf16[2048,1024]{0,1:T(8,128)(2,1)} %all-gather.19.cloned.1.call-done), kind=kOutput, calls=%fused_computation.285 | convolution fusion | flops 8589934592 | bytes 20971520 | tf_op jit(solution)/shard_map/dot_general | solution.py:352
  449.0 12.6 fusion.98
  461.6 11.9 fusion.62
  473.5 18.9 %fusion.23 = (bf16[2048,1024]{1,0:T(8,128)(2,1)S(1)}, bf16[2048,1024]{1,0:T(8,128)(2,1)S(1)}) fusion(bf16[2048,1024]{1,0:T(8,128)(2,1)} %copy-done.66, bf16[2048,1024]{1,0:T(8,128)(2,1)} %get-tuple-element.35, bf16[2048,2048]{1,0:T(8,128)(2,1)} %copy-done.1, bf16[2048,1024]{0,1:T(8,128)(2,1)} %all-gather.17.cloned.1.call-done), kind=kOutput, calls=%fused_computation.33 | convolution fusion | flops 8621391872 | bytes 29360128 | tf_op jit(solution)/shard_map/dot_general | solution.py:352
  497.2 12.6 fusion.104
  509.8 15.1 %fusion.61 = (bf16[2048,1024]{1,0:T(8,128)(2,1)}, bf16[2048,1024]{1,0:T(8,128)(2,1)S(1)}) fusion(bf16[2048,1024]{1,0:T(8,128)(2,1)S(1)} %fusion.104, bf16[2048,2048]{1,0:T(8,128)(2,1)} %copy-done.2, bf16[2048,2048]{1,0:T(8,128)(2,1)} %all-gather.15.cloned.1.call-done), kind=kOutput, calls=%fused_computation.71 | convolution fusion | flops 8608808960 | bytes 25165824 | tf_op jit(solution)/shard_map/dot_general | solution.py:352
  539.8 29.1 %fusion.86 = bf16[1024,2048]{1,0:T(8,128)(2,1)} fusion(bf16[2048,2048]{1,0:T(8,128)(2,1)} %all-gather.15.cloned.1.call-done, bf16[2048,2048]{1,0:T(8,128)(2,1)} %all-gather.13.cloned.1.call-done, bf16[1024,1024]{1,0:T(8,128)(2,1)} %slice.343, bf16[1024,1024]{1,0:T(8,128)(2,1)} %slice.342, bf16[1024,1024]{1,0:T(8,128)(2,1)S(1)} %slice.341, ...), kind=kOutput, calls=%fused_computation.108 | convolution fusion | flops 17249075200 | bytes 29360128 | tf_op jit(solution)/shard_map/dot_general | solution.py:352
  572.7 28.9 %fusion.91 = bf16[1024,2048]{1,0:T(8,128)(2,1)} fusion(bf16[2048,2048]{1,0:T(8,128)(2,1)} %all-gather.15.cloned.1.call-done, bf16[2048,2048]{1,0:T(8,128)(2,1)} %all-gather.13.cloned.1.call-done, bf16[1024,1024]{1,0:T(8,128)(2,1)S(1)} %copy-done.33, bf16[1024,1024]{1,0:T(8,128)(2,1)} %slice.271, bf16[1024,1024]{1,0:T(8,128)(2,1)} %slice.270, ...), kind=kOutput, calls=%fused_computation.109 | convolution fusion | flops 17249075200 | bytes 29360128 | tf_op jit(solution)/shard_map/dot_general | solution.py:352
  608.6 13.3 %convolution_convert_fusion.2 = bf16[2048,1024]{1,0:T(8,128)(2,1)} fusion(bf16[2048,2048]{1,0:T(8,128)(2,1)} %copy-done.1, bf16[2048,1024]{1,0:T(8,128)(2,1)S(1)} %copy-done.65), kind=kOutput, calls=%fused_computation.118 | convolution fusion | flops 8592031744 | bytes 16777216 | tf_op jit(solution)/shard_map/dot_general | solution.py:352
  625.9 8.8 collective-permute-done.34
  641.9 15.2 %collective-permute-done.31 = bf16[256,2048]{1,0:T(8,128)(2,1)S(1)} collective-permute-done((bf16[256,2048]{1,0:T(8,128)(2,1)S(1)}, bf16[256,2048]{1,0:T(8,128)(2,1)S(1)}, u32[]{:S(2)}, u32[]{:S(2)}) %collective-permute-start.31) | collective-permute-done | bytes 1048608 | tf_op jit(solution)/shard_map/ppermute | solution.py:32
  663.2 16.4 %collective-permute-done.37.refs_2_ = bf16[256,2048]{1,0:T(8,128)(2,1)S(1)} collective-permute-done((bf16[256,2048]{1,0:T(8,128)(2,1)S(1)}, bf16[256,2048]{1,0:T(8,128)(2,1)S(1)}, u32[]{:S(2)}, u32[]{:S(2)}) %collective-permute-start.37) | collective-permute-done | bytes 1048608 | tf_op jit(solution)/shard_map/ppermute | solution.py:32
  679.5 22.0 %collective-permute-done.40.refs_6_ = bf16[256,2048]{1,0:T(8,128)(2,1)S(1)} collective-permute-done((bf16[256,2048]{1,0:T(8,128)(2,1)S(1)}, bf16[256,2048]{1,0:T(8,128)(2,1)S(1)}, u32[]{:S(2)}, u32[]{:S(2)}) %collective-permute-start.40) | collective-permute-done | bytes 1048608 | tf_op jit(solution)/shard_map/ppermute | solution.py:32
  714.0 34.8 %attend_back.3 = bf16[2048,768]{1,0:T(8,128)(2,1)} custom-call(s32[3]{0:T(128)} %pad_add_fusion.info_ref, bf16[2048,768]{1,0:T(8,128)(2,1)} %qkv_project.3.qkv_ref, bf16[2048,256]{1,0:T(8,128)(2,1)} %get-tuple-element.31.o_ref, bf16[2048,256]{1,0:T(8,128)(2,1)} %convolution_convert_fusion.8.do_ref, f32[2,8,2,256]{3,2,1,0:T(2,128)} %get-tuple-element.48.lse_ref, ...), custom_call_target="tpu_custom_call" | custom-call | flops 21474836480 | bytes 8388608 | tf_op jit(solution)/shard_map/attend_back/pallas_call | solution.py:310
  748.8 10.2 convolution_convert_fusion.4
  761.4 23.8 %fusion.63 = bf16[2048,2048]{1,0:T(8,128)(2,1)} fusion(bf16[2048,2048]{1,0:T(8,128)(2,1)} %copy-done.2, bf16[2048,1024]{1,0:T(8,128)(2,1)} %copy-done.19, bf16[2048,1024]{1,0:T(8,128)(2,1)} %copy-done.20), kind=kOutput, calls=%fused_computation.73 | convolution fusion | flops 17200840704 | bytes 25165824 | tf_op jit(solution)/shard_map/dot_general | solution.py:352
  785.3 14.0 %convolution_convert_fusion.3 = bf16[2048,1024]{1,0:T(8,128)(2,1)} fusion(bf16[2048,2048]{1,0:T(8,128)(2,1)} %copy-done.1, bf16[2048,1024]{1,0:T(8,128)(2,1)} %get-tuple-element.33), kind=kOutput, calls=%fused_computation.119 | convolution fusion | flops 8592031744 | bytes 16777216 | tf_op jit(solution)/shard_map/dot_general | solution.py:352
  806.4 7.0 convolution_convert_fusion.9.do_ref
  813.4 34.9 %attend_back.2 = bf16[2048,768]{1,0:T(8,128)(2,1)} custom-call(s32[3]{0:T(128)} %pad_add_fusion.info_ref, bf16[2048,768]{1,0:T(8,128)(2,1)} %qkv_project.2.qkv_ref, bf16[2048,256]{1,0:T(8,128)(2,1)} %get-tuple-element.30.o_ref, bf16[2048,256]{1,0:T(8,128)(2,1)} %convolution_convert_fusion.9.do_ref, f32[2,8,2,256]{3,2,1,0:T(2,128)} %get-tuple-element.47.lse_ref, ...), custom_call_target="tpu_custom_call" | custom-call | flops 21474836480 | bytes 8388608 | tf_op jit(solution)/shard_map/attend_back/pallas_call | solution.py:310
  848.3 10.4 convolution_convert_fusion.5
  861.2 23.8 %fusion.66 = bf16[2048,2048]{1,0:T(8,128)(2,1)} fusion(bf16[2048,2048]{1,0:T(8,128)(2,1)} %copy-done.2, bf16[2048,1024]{1,0:T(8,128)(2,1)} %copy-done.24, bf16[2048,1024]{1,0:T(8,128)(2,1)} %copy-done.26), kind=kOutput, calls=%fused_computation.74 | convolution fusion | flops 17200840704 | bytes 25165824 | tf_op jit(solution)/shard_map/dot_general | solution.py:352
  885.0 22.5 %fusion.69 = bf16[2048,2048]{1,0:T(8,128)(2,1)S(1)} fusion(bf16[2048,1024]{0,1:T(8,128)(2,1)} %all-gather.19.cloned.1.call-done, bf16[2048,1024]{0,1:T(8,128)(2,1)} %all-gather.17.cloned.1.call-done, bf16[2048,1024]{1,0:T(8,128)(2,1)} %get-tuple-element.34, bf16[2048,1024]{1,0:T(8,128)(2,1)} %get-tuple-element.33), kind=kOutput, calls=%fused_computation.75 | convolution fusion | flops 17217617920 | bytes 25165824 | tf_op jit(solution)/shard_map/dot_general | solution.py:352
  920.9 9.1 fusion.97
  932.0 8.8 fusion.96
  941.4 22.4 %collective-permute-done.24 = bf16[2,256,2048]{2,1,0:T(8,128)(2,1)} collective-permute-done((bf16[2,256,2048]{2,1,0:T(8,128)(2,1)}, bf16[2,256,2048]{2,1,0:T(8,128)(2,1)}, u32[]{:S(2)}, u32[]{:S(2)}) %collective-permute-start.24) | collective-permute-done | bytes 2097184 | tf_op jit(solution)/shard_map/ppermute | solution.py:32
  972.3 37.3 %collective-permute-done.47 = bf16[256,2048]{1,0:T(8,128)(2,1)S(1)} collective-permute-done((bf16[256,2048]{1,0:T(8,128)(2,1)S(1)}, bf16[256,2048]{1,0:T(8,128)(2,1)S(1)}, u32[]{:S(2)}, u32[]{:S(2)}) %collective-permute-start.47) | collective-permute-done | bytes 1048608 | tf_op jit(solution)/shard_map/ppermute | solution.py:32
  1011.2 27.3 %collective-permute-done.44 = bf16[256,2048]{1,0:T(8,128)(2,1)S(1)} collective-permute-done((bf16[256,2048]{1,0:T(8,128)(2,1)S(1)}, bf16[256,2048]{1,0:T(8,128)(2,1)S(1)}, u32[]{:S(2)}, u32[]{:S(2)}) %collective-permute-start.44) | collective-permute-done | bytes 1048608 | tf_op jit(solution)/shard_map/ppermute | solution.py:32
  1053.9 23.6 %collective-permute-done.52 = f32[2,2048]{1,0:T(2,128)S(1)} collective-permute-done((f32[2,2048]{1,0:T(2,128)S(1)}, f32[2,2048]{1,0:T(2,128)S(1)}, u32[]{:S(2)}, u32[]{:S(2)}) %collective-permute-start.52) | collective-permute-done | bytes 16416 | tf_op jit(solution)/shard_map/ppermute | solution.py:32
  1086.0 106.4 %collective-permute-done.53 = f32[2,2048]{1,0:T(2,128)S(1)} collective-permute-done((f32[2,2048]{1,0:T(2,128)S(1)}, f32[2,2048]{1,0:T(2,128)S(1)}, u32[]{:S(2)}, u32[]{:S(2)}) %collective-permute-start.53) | collective-permute-done | bytes 16416 | tf_op jit(solution)/shard_map/ppermute | solution.py:32
  1194.6 20.3 %collective-permute-done.56 = bf16[512,1024]{1,0:T(8,128)(2,1)} collective-permute-done((bf16[512,1024]{1,0:T(8,128)(2,1)}, bf16[512,1024]{1,0:T(8,128)(2,1)}, u32[]{:S(2)}, u32[]{:S(2)}) %collective-permute-start.56) | collective-permute-done | bytes 1048608 | tf_op jit(solution)/shard_map/ppermute | solution.py:32
  1218.7 18.7 %collective-permute-done.54 = bf16[512,1024]{0,1:T(8,128)(2,1)} collective-permute-done((bf16[512,1024]{0,1:T(8,128)(2,1)}, bf16[512,1024]{0,1:T(8,128)(2,1)}, u32[]{:S(2)}, u32[]{:S(2)}) %collective-permute-start.54) | collective-permute-done | bytes 1048608 | tf_op jit(solution)/shard_map/ppermute | solution.py:32
  1248.3 34.0 %collective-permute-done.55 = bf16[512,2048]{1,0:T(8,128)(2,1)} collective-permute-done((bf16[512,2048]{1,0:T(8,128)(2,1)}, bf16[512,2048]{1,0:T(8,128)(2,1)}, u32[]{:S(2)}, u32[]{:S(2)}) %collective-permute-start.55) | collective-permute-done | bytes 2097184 | tf_op jit(solution)/shard_map/ppermute | solution.py:32
  1287.3 6.6 reshape.484
  (393 shorter events, 232.9 us)
Async XLA Ops:
  7.2 233.2 %all-gather.9.cloned.1.call-start = ((), (), s32[]{:S(2)}) async-start(), calls=%async_computation.6 | async-start | bytes 5242880 | tf_op jit(solution)/shard_map/all_gather | solution.py:382
  11.3 268.2 %all-gather.11.cloned.1.call-start = ((), (), s32[]{:S(2)}) async-start(), calls=%async_computation.7 | async-start | bytes 5242880 | tf_op jit(solution)/shard_map/all_gather | solution.py:382
  11.4 50.1 %collective-permute-start.7 = (bf16[512,1024]{1,0:T(8,128)(2,1)}, bf16[512,1024]{1,0:T(8,128)(2,1)}, u32[]{:S(2)}, u32[]{:S(2)}) collective-permute-start(bf16[512,1024]{1,0:T(8,128)(2,1)} %pad_maximum_fusion.12), channel_id=1, source_target_pairs={{0,4},{4,0},{1,5},{5,1},{2,6},{6,2},{3,7},{7,3},{8,12},{12,8},{9,1... | collective-permute-start | bytes 3145736 | tf_op jit(solution)/shard_map/ppermute | solution.py:32
  61.5 365.8 %all-gather.19.cloned.1.call-start = ((), (), s32[]{:S(2)}) async-start(), calls=%async_computation.11 | async-start | bytes 5242880 | tf_op jit(solution)/shard_map/all_gather | solution.py:382
  61.5 47.9 %collective-permute-start.21 = (bf16[512,1024]{0,1:T(8,128)(2,1)S(1)}, bf16[512,1024]{0,1:T(8,128)(2,1)}, u32[]{:S(2)}, u32[]{:S(2)}) collective-permute-start(bf16[512,1024]{0,1:T(8,128)(2,1)S(1)} %bitcast.155), channel_id=1, source_target_pairs={{0,4},{4,0},{1,5},{5,1},{2,6},{6,2},{3,7},{7,3},{8,12},{12,8},{9,1... | collective-permute-start | bytes 3145736 | tf_op jit(solution)/shard_map/ppermute | solution.py:32
  109.4 339.5 %all-gather.13.cloned.1.call-start = ((), (), s32[]{:S(2)}) async-start(), calls=%async_computation.8 | async-start | bytes 10485760 | tf_op jit(solution)/shard_map/all_gather | solution.py:382
  113.0 360.5 %all-gather.17.cloned.1.call-start = ((), (), s32[]{:S(2)}) async-start(), calls=%async_computation.10 | async-start | bytes 5242880 | tf_op jit(solution)/shard_map/all_gather | solution.py:382
  114.1 48.0 %collective-permute-start.3 = (bf16[256,2048]{1,0:T(8,128)(2,1)}, bf16[256,2048]{1,0:T(8,128)(2,1)S(1)}, u32[]{:S(2)}, u32[]{:S(2)}) collective-permute-start(bf16[256,2048]{1,0:T(8,128)(2,1)} %dynamic-slice_bitcast_fusion.2), channel_id=1, source_target_pairs={{0,4},{4,0},{1,5},{5,1},{2,6},{6,2},{3,7},{7,3},{8,12},{12,8},{9,1... | collective-permute-start | bytes 3145736 | tf_op jit(solution)/shard_map/ppermute | solution.py:32
  126.3 104.7 %collective-permute-start = (bf16[256,2048]{1,0:T(8,128)(2,1)S(1)}, bf16[256,2048]{1,0:T(8,128)(2,1)S(1)}, u32[]{:S(2)}, u32[]{:S(2)}) collective-permute-start(bf16[256,2048]{1,0:T(8,128)(2,1)S(1)} %fusion.128.refs_0_), channel_id=1, source_target_pairs={{0,1},{1,0},{2,3},{3,2},{4,5},{5,4},{6,7},{7,6},{8,9},{9,8},{10,11... | collective-permute-start | bytes 3145736 | tf_op jit(solution)/shard_map/ppermute | solution.py:32
  126.4 48.7 %collective-permute-start.1 = (bf16[256,2048]{1,0:T(8,128)(2,1)S(1)}, bf16[256,2048]{1,0:T(8,128)(2,1)}, u32[]{:S(2)}, u32[]{:S(2)}) collective-permute-start(bf16[256,2048]{1,0:T(8,128)(2,1)S(1)} %fusion.128.refs_0_), channel_id=1, source_target_pairs={{0,2},{1,3},{2,0},{3,1},{4,6},{5,7},{6,4},{7,5},{8,10},{9,11},{10,... | collective-permute-start | bytes 3145736 | tf_op jit(solution)/shard_map/ppermute | solution.py:32
  128.3 368.8 %all-gather.15.cloned.1.call-start = ((), (), s32[]{:S(2)}) async-start(), calls=%async_computation.9 | async-start | bytes 10485760 | tf_op jit(solution)/shard_map/all_gather | solution.py:382
  131.7 93.9 %collective-permute-start.25 = (bf16[256,2048]{1,0:T(8,128)(2,1)}, bf16[256,2048]{1,0:T(8,128)(2,1)}, u32[]{:S(2)}, u32[]{:S(2)}) collective-permute-start(bf16[256,2048]{1,0:T(8,128)(2,1)} %get-tuple-element.133), channel_id=1, source_target_pairs={{0,4},{4,0},{1,5},{5,1},{2,6},{6,2},{3,7},{7,3},{8,12},{12,8},{9,1... | collective-permute-start | bytes 3145736 | tf_op jit(solution)/shard_map/ppermute | solution.py:32
  164.7 54.6 %collective-permute-start.5 = (bf16[256,2048]{1,0:T(8,128)(2,1)S(1)}, bf16[256,2048]{1,0:T(8,128)(2,1)}, u32[]{:S(2)}, u32[]{:S(2)}) collective-permute-start(bf16[256,2048]{1,0:T(8,128)(2,1)S(1)} %fusion.118.refs_4_), channel_id=1, source_target_pairs={{0,2},{1,3},{2,0},{3,1},{4,6},{5,7},{6,4},{7,5},{8,10},{9,11},{10,... | collective-permute-start | bytes 3145736 | tf_op jit(solution)/shard_map/ppermute | solution.py:32
  167.8 65.9 %collective-permute-start.4 = (bf16[256,2048]{1,0:T(8,128)(2,1)S(1)}, bf16[256,2048]{1,0:T(8,128)(2,1)S(1)}, u32[]{:S(2)}, u32[]{:S(2)}) collective-permute-start(bf16[256,2048]{1,0:T(8,128)(2,1)S(1)} %fusion.118.refs_4_), channel_id=1, source_target_pairs={{0,1},{1,0},{2,3},{3,2},{4,5},{5,4},{6,7},{7,6},{8,9},{9,8},{10,11... | collective-permute-start | bytes 3145736 | tf_op jit(solution)/shard_map/ppermute | solution.py:32
  175.1 58.6 %collective-permute-start.2 = (bf16[256,2048]{1,0:T(8,128)(2,1)}, bf16[256,2048]{1,0:T(8,128)(2,1)S(1)}, u32[]{:S(2)}, u32[]{:S(2)}) collective-permute-start(bf16[256,2048]{1,0:T(8,128)(2,1)} %collective-permute-done.1.refs_2_), channel_id=1, source_target_pairs={{0,1},{1,0},{2,3},{3,2},{4,5},{5,4},{6,7},{7,6},{8,9},{9,8},{10,11... | collective-permute-start | bytes 3145736 | tf_op jit(solution)/shard_map/ppermute | solution.py:32
  225.6 100.7 %collective-permute-start.20 = (bf16[512,2048]{1,0:T(8,128)(2,1)}, bf16[512,2048]{1,0:T(8,128)(2,1)}, u32[]{:S(2)}, u32[]{:S(2)}) collective-permute-start(bf16[512,2048]{1,0:T(8,128)(2,1)} %bitcast.148), channel_id=1, source_target_pairs={{0,4},{4,0},{1,5},{5,1},{2,6},{6,2},{3,7},{7,3},{8,12},{12,8},{9,1... | collective-permute-start | bytes 6291464 | tf_op jit(solution)/shard_map/ppermute | solution.py:32
  231.1 95.3 %collective-permute-start.27 = (bf16[2,256,2048]{2,1,0:T(8,128)(2,1)}, bf16[2,256,2048]{2,1,0:T(8,128)(2,1)}, u32[]{:S(2)}, u32[]{:S(2)}) collective-permute-start(bf16[2,256,2048]{2,1,0:T(8,128)(2,1)} %get-tuple-element.123), channel_id=1, source_target_pairs={{0,2},{1,3},{2,0},{3,1},{4,6},{5,7},{6,4},{7,5},{8,10},{9,11},{10,... | collective-permute-start | bytes 6291464 | tf_op jit(solution)/shard_map/ppermute | solution.py:32
  326.2 58.5 %collective-permute-start.26 = (bf16[2,256,2048]{2,1,0:T(8,128)(2,1)}, bf16[2,256,2048]{2,1,0:T(8,128)(2,1)}, u32[]{:S(2)}, u32[]{:S(2)}) collective-permute-start(bf16[2,256,2048]{2,1,0:T(8,128)(2,1)} %get-tuple-element.123), channel_id=1, source_target_pairs={{0,1},{1,0},{2,3},{3,2},{4,5},{5,4},{6,7},{7,6},{8,9},{9,8},{10,11... | collective-permute-start | bytes 6291464 | tf_op jit(solution)/shard_map/ppermute | solution.py:32
  326.3 754.0 %reduce-scatter.17.cloned.1.call-start = ((), (), s32[]{:S(2)}) async-start(), calls=%async_computation.17 | async-start | bytes 5242880 | tf_op jit(solution)/shard_map/reduce_scatter | solution.py:509
  326.4 60.2 %collective-permute-start.28 = (bf16[2,256,2048]{2,1,0:T(8,128)(2,1)}, bf16[2,256,2048]{2,1,0:T(8,128)(2,1)S(1)}, u32[]{:S(2)}, u32[]{:S(2)}) collective-permute-start(bf16[2,256,2048]{2,1,0:T(8,128)(2,1)} %collective-permute-done.27), channel_id=1, source_target_pairs={{0,1},{1,0},{2,3},{3,2},{4,5},{5,4},{6,7},{7,6},{8,9},{9,8},{10,11... | collective-permute-start | bytes 6291464 | tf_op jit(solution)/shard_map/ppermute | solution.py:32
  337.6 45.2 %collective-permute-start.16 = (bf16[256,2048]{1,0:T(8,128)(2,1)S(1)}, bf16[256,2048]{1,0:T(8,128)(2,1)S(1)}, u32[]{:S(2)}, u32[]{:S(2)}) collective-permute-start(bf16[256,2048]{1,0:T(8,128)(2,1)S(1)} %add_convert_fusion.8), channel_id=1, source_target_pairs={{0,2},{1,3},{2,0},{3,1},{4,6},{5,7},{6,4},{7,5},{8,10},{9,11},{10,... | collective-permute-start | bytes 3145736 | tf_op jit(solution)/shard_map/ppermute | solution.py:32
  362.0 43.4 %collective-permute-start.12 = (bf16[256,2048]{1,0:T(8,128)(2,1)S(1)}, bf16[256,2048]{1,0:T(8,128)(2,1)}, u32[]{:S(2)}, u32[]{:S(2)}) collective-permute-start(bf16[256,2048]{1,0:T(8,128)(2,1)S(1)} %multiply_convert_fusion.1.refs_0_), channel_id=1, source_target_pairs={{0,2},{1,3},{2,0},{3,1},{4,6},{5,7},{6,4},{7,5},{8,10},{9,11},{10,... | collective-permute-start | bytes 3145736 | tf_op jit(solution)/shard_map/ppermute | solution.py:32
  384.6 42.7 %collective-permute-start.18 = (bf16[256,2048]{1,0:T(8,128)(2,1)S(1)}, bf16[256,2048]{1,0:T(8,128)(2,1)}, u32[]{:S(2)}, u32[]{:S(2)}) collective-permute-start(bf16[256,2048]{1,0:T(8,128)(2,1)S(1)} %multiply_convert_fusion.refs_4_), channel_id=1, source_target_pairs={{0,2},{1,3},{2,0},{3,1},{4,6},{5,7},{6,4},{7,5},{8,10},{9,11},{10,... | collective-permute-start | bytes 3145736 | tf_op jit(solution)/shard_map/ppermute | solution.py:32
  392.2 49.7 %collective-permute-start.11 = (bf16[256,2048]{1,0:T(8,128)(2,1)S(1)}, bf16[256,2048]{1,0:T(8,128)(2,1)S(1)}, u32[]{:S(2)}, u32[]{:S(2)}) collective-permute-start(bf16[256,2048]{1,0:T(8,128)(2,1)S(1)} %multiply_convert_fusion.1.refs_0_), channel_id=1, source_target_pairs={{0,1},{1,0},{2,3},{3,2},{4,5},{5,4},{6,7},{7,6},{8,9},{9,8},{10,11... | collective-permute-start | bytes 3145736 | tf_op jit(solution)/shard_map/ppermute | solution.py:32
  392.2 49.7 %collective-permute-start.17 = (bf16[256,2048]{1,0:T(8,128)(2,1)S(1)}, bf16[256,2048]{1,0:T(8,128)(2,1)}, u32[]{:S(2)}, u32[]{:S(2)}) collective-permute-start(bf16[256,2048]{1,0:T(8,128)(2,1)S(1)} %multiply_convert_fusion.refs_4_), channel_id=1, source_target_pairs={{0,1},{1,0},{2,3},{3,2},{4,5},{5,4},{6,7},{7,6},{8,9},{9,8},{10,11... | collective-permute-start | bytes 3145736 | tf_op jit(solution)/shard_map/ppermute | solution.py:32
  405.4 36.5 %collective-permute-start.13 = (bf16[256,2048]{1,0:T(8,128)(2,1)}, bf16[256,2048]{1,0:T(8,128)(2,1)}, u32[]{:S(2)}, u32[]{:S(2)}) collective-permute-start(bf16[256,2048]{1,0:T(8,128)(2,1)} %collective-permute-done.12.refs_2_), channel_id=1, source_target_pairs={{0,1},{1,0},{2,3},{3,2},{4,5},{5,4},{6,7},{7,6},{8,9},{9,8},{10,11... | collective-permute-start | bytes 3145736 | tf_op jit(solution)/shard_map/ppermute | solution.py:32
  572.2 33.2 %collective-permute-start.33 = (bf16[256,2048]{1,0:T(8,128)(2,1)}, bf16[256,2048]{1,0:T(8,128)(2,1)}, u32[]{:S(2)}, u32[]{:S(2)}) collective-permute-start(bf16[256,2048]{1,0:T(8,128)(2,1)} %get-tuple-element.111), channel_id=1, source_target_pairs={{0,1},{1,0},{2,3},{3,2},{4,5},{5,4},{6,7},{7,6},{8,9},{9,8},{10,11... | collective-permute-start | bytes 3145736 | tf_op jit(solution)/shard_map/ppermute | solution.py:32
  604.8 37.0 %collective-permute-start.29 = (bf16[256,2048]{1,0:T(8,128)(2,1)}, bf16[256,2048]{1,0:T(8,128)(2,1)}, u32[]{:S(2)}, u32[]{:S(2)}) collective-permute-start(bf16[256,2048]{1,0:T(8,128)(2,1)} %get-tuple-element.112), channel_id=1, source_target_pairs={{0,1},{1,0},{2,3},{3,2},{4,5},{5,4},{6,7},{7,6},{8,9},{9,8},{10,11... | collective-permute-start | bytes 3145736 | tf_op jit(solution)/shard_map/ppermute | solution.py:32
  621.9 458.6 %reduce-scatter.9.cloned.1.call-start = ((), (), s32[]{:S(2)}) async-start(), calls=%async_computation.13 | async-start | bytes 5242880 | tf_op jit(solution)/shard_map/reduce_scatter | solution.py:509
  641.5 38.0 %collective-permute-start.37 = (bf16[256,2048]{1,0:T(8,128)(2,1)S(1)}, bf16[256,2048]{1,0:T(8,128)(2,1)S(1)}, u32[]{:S(2)}, u32[]{:S(2)}) collective-permute-start(bf16[256,2048]{1,0:T(8,128)(2,1)S(1)} %get-tuple-element.92.refs_0_), channel_id=1, source_target_pairs={{0,2},{1,3},{2,0},{3,1},{4,6},{5,7},{6,4},{7,5},{8,10},{9,11},{10,... | collective-permute-start | bytes 3145736 | tf_op jit(solution)/shard_map/ppermute | solution.py:32
  662.6 38.9 %collective-permute-start.40 = (bf16[256,2048]{1,0:T(8,128)(2,1)S(1)}, bf16[256,2048]{1,0:T(8,128)(2,1)S(1)}, u32[]{:S(2)}, u32[]{:S(2)}) collective-permute-start(bf16[256,2048]{1,0:T(8,128)(2,1)S(1)} %get-tuple-element.90.refs_4_), channel_id=1, source_target_pairs={{0,2},{1,3},{2,0},{3,1},{4,6},{5,7},{6,4},{7,5},{8,10},{9,11},{10,... | collective-permute-start | bytes 3145736 | tf_op jit(solution)/shard_map/ppermute | solution.py:32
  662.7 40.7 %collective-permute-start.36 = (bf16[256,2048]{1,0:T(8,128)(2,1)S(1)}, bf16[256,2048]{1,0:T(8,128)(2,1)S(1)}, u32[]{:S(2)}, u32[]{:S(2)}) collective-permute-start(bf16[256,2048]{1,0:T(8,128)(2,1)S(1)} %get-tuple-element.92.refs_0_), channel_id=1, source_target_pairs={{0,1},{1,0},{2,3},{3,2},{4,5},{5,4},{6,7},{7,6},{8,9},{9,8},{10,11... | collective-permute-start | bytes 3145736 | tf_op jit(solution)/shard_map/ppermute | solution.py:32
  662.7 40.7 %collective-permute-start.39 = (bf16[256,2048]{1,0:T(8,128)(2,1)S(1)}, bf16[256,2048]{1,0:T(8,128)(2,1)S(1)}, u32[]{:S(2)}, u32[]{:S(2)}) collective-permute-start(bf16[256,2048]{1,0:T(8,128)(2,1)S(1)} %get-tuple-element.90.refs_4_), channel_id=1, source_target_pairs={{0,1},{1,0},{2,3},{3,2},{4,5},{5,4},{6,7},{7,6},{8,9},{9,8},{10,11... | collective-permute-start | bytes 3145736 | tf_op jit(solution)/shard_map/ppermute | solution.py:32
  761.4 321.8 %reduce-scatter.13.cloned.1.call-start = ((), (), s32[]{:S(2)}) async-start(), calls=%async_computation.15 | async-start | bytes 10485760 | tf_op jit(solution)/shard_map/reduce_scatter | solution.py:509
  785.3 409.3 %reduce-scatter.15.cloned.1.call-start = ((), (), s32[]{:S(2)}) async-start(), calls=%async_computation.16 | async-start | bytes 5242880 | tf_op jit(solution)/shard_map/reduce_scatter | solution.py:509
  799.3 419.3 %reduce-scatter.7.cloned.1.call-start = ((), (), s32[]{:S(2)}) async-start(), calls=%async_computation.12 | async-start | bytes 5242880 | tf_op jit(solution)/shard_map/reduce_scatter | solution.py:509
  861.1 387.2 %reduce-scatter.11.cloned.1.call-start = ((), (), s32[]{:S(2)}) async-start(), calls=%async_computation.14 | async-start | bytes 10485760 | tf_op jit(solution)/shard_map/reduce_scatter | solution.py:509
  915.7 48.1 %collective-permute-start.24 = (bf16[2,256,2048]{2,1,0:T(8,128)(2,1)}, bf16[2,256,2048]{2,1,0:T(8,128)(2,1)}, u32[]{:S(2)}, u32[]{:S(2)}) collective-permute-start(bf16[2,256,2048]{2,1,0:T(8,128)(2,1)} %fusion.82), channel_id=1, source_target_pairs={{0,2},{1,3},{2,0},{3,1},{4,6},{5,7},{6,4},{7,5},{8,10},{9,11},{10,... | collective-permute-start | bytes 6291464 | tf_op jit(solution)/shard_map/ppermute | solution.py:32
  931.6 36.4 %collective-permute-start.46 = (bf16[256,2048]{1,0:T(8,128)(2,1)}, bf16[256,2048]{1,0:T(8,128)(2,1)S(1)}, u32[]{:S(2)}, u32[]{:S(2)}) collective-permute-start(bf16[256,2048]{1,0:T(8,128)(2,1)} %get-tuple-element.107), channel_id=1, source_target_pairs={{0,1},{1,0},{2,3},{3,2},{4,5},{5,4},{6,7},{7,6},{8,9},{9,8},{10,11... | collective-permute-start | bytes 3145736 | tf_op jit(solution)/shard_map/ppermute | solution.py:32
  967.5 43.7 %collective-permute-start.42 = (bf16[256,2048]{1,0:T(8,128)(2,1)S(1)}, bf16[256,2048]{1,0:T(8,128)(2,1)S(1)}, u32[]{:S(2)}, u32[]{:S(2)}) collective-permute-start(bf16[256,2048]{1,0:T(8,128)(2,1)S(1)} %get-tuple-element.104), channel_id=1, source_target_pairs={{0,1},{1,0},{2,3},{3,2},{4,5},{5,4},{6,7},{7,6},{8,9},{9,8},{10,11... | collective-permute-start | bytes 3145736 | tf_op jit(solution)/shard_map/ppermute | solution.py:32
  968.4 41.3 %collective-permute-start.47 = (bf16[256,2048]{1,0:T(8,128)(2,1)S(1)}, bf16[256,2048]{1,0:T(8,128)(2,1)S(1)}, u32[]{:S(2)}, u32[]{:S(2)}) collective-permute-start(bf16[256,2048]{1,0:T(8,128)(2,1)S(1)} %add_convert_fusion), channel_id=1, source_target_pairs={{0,2},{1,3},{2,0},{3,1},{4,6},{5,7},{6,4},{7,5},{8,10},{9,11},{10,... | collective-permute-start | bytes 3145736 | tf_op jit(solution)/shard_map/ppermute | solution.py:32
  969.0 69.6 %collective-permute-start.44 = (bf16[256,2048]{1,0:T(8,128)(2,1)S(1)}, bf16[256,2048]{1,0:T(8,128)(2,1)S(1)}, u32[]{:S(2)}, u32[]{:S(2)}) collective-permute-start(bf16[256,2048]{1,0:T(8,128)(2,1)S(1)} %add_convert_fusion.2), channel_id=1, source_target_pairs={{0,2},{1,3},{2,0},{3,1},{4,6},{5,7},{6,4},{7,5},{8,10},{9,11},{10,... | collective-permute-start | bytes 3145736 | tf_op jit(solution)/shard_map/ppermute | solution.py:32
  972.3 78.0 %collective-permute-start.35 = (bf16[256,2048]{1,0:T(8,128)(2,1)}, bf16[256,2048]{1,0:T(8,128)(2,1)}, u32[]{:S(2)}, u32[]{:S(2)}) collective-permute-start(bf16[256,2048]{1,0:T(8,128)(2,1)} %get-tuple-element.109), channel_id=1, source_target_pairs={{0,4},{4,0},{1,5},{5,1},{2,6},{6,2},{3,7},{7,3},{8,12},{12,8},{9,1... | collective-permute-start | bytes 3145736 | tf_op jit(solution)/shard_map/ppermute | solution.py:32
  1053.7 139.3 %collective-permute-start.48 = (bf16[256,2048]{1,0:T(8,128)(2,1)}, bf16[256,2048]{1,0:T(8,128)(2,1)S(1)}, u32[]{:S(2)}, u32[]{:S(2)}) collective-permute-start(bf16[256,2048]{1,0:T(8,128)(2,1)} %fusion.122), channel_id=1, source_target_pairs={{0,4},{4,0},{1,5},{5,1},{2,6},{6,2},{3,7},{7,3},{8,12},{12,8},{9,1... | collective-permute-start | bytes 3145736 | tf_op jit(solution)/shard_map/ppermute | solution.py:32
  1077.5 114.9 %collective-permute-start.53 = (f32[2,2048]{1,0:T(2,128)S(1)}, f32[2,2048]{1,0:T(2,128)S(1)}, u32[]{:S(2)}, u32[]{:S(2)}) collective-permute-start(f32[2,2048]{1,0:T(2,128)S(1)} %add.380), channel_id=1, source_target_pairs={{0,4},{4,0},{1,5},{5,1},{2,6},{6,2},{3,7},{7,3},{8,12},{12,8},{9,1... | collective-permute-start | bytes 49160 | tf_op jit(solution)/shard_map/ppermute | solution.py:32
  1080.3 134.6 %collective-permute-start.56 = (bf16[512,1024]{1,0:T(8,128)(2,1)}, bf16[512,1024]{1,0:T(8,128)(2,1)}, u32[]{:S(2)}, u32[]{:S(2)}) collective-permute-start(bf16[512,1024]{1,0:T(8,128)(2,1)} %reduce-scatter.17.cloned.1.call-done), channel_id=1, source_target_pairs={{0,4},{4,0},{1,5},{5,1},{2,6},{6,2},{3,7},{7,3},{8,12},{12,8},{9,1... | collective-permute-start | bytes 3145736 | tf_op jit(solution)/shard_map/ppermute | solution.py:32
  1080.5 156.9 %collective-permute-start.54 = (bf16[512,1024]{0,1:T(8,128)(2,1)}, bf16[512,1024]{0,1:T(8,128)(2,1)}, u32[]{:S(2)}, u32[]{:S(2)}) collective-permute-start(bf16[512,1024]{0,1:T(8,128)(2,1)} %reduce-scatter.9.cloned.1.call-done), channel_id=1, source_target_pairs={{0,4},{4,0},{1,5},{5,1},{2,6},{6,2},{3,7},{7,3},{8,12},{12,8},{9,1... | collective-permute-start | bytes 3145736 | tf_op jit(solution)/shard_map/ppermute | solution.py:32
  1083.2 199.1 %collective-permute-start.55 = (bf16[512,2048]{1,0:T(8,128)(2,1)}, bf16[512,2048]{1,0:T(8,128)(2,1)}, u32[]{:S(2)}, u32[]{:S(2)}) collective-permute-start(bf16[512,2048]{1,0:T(8,128)(2,1)} %reduce-scatter.13.cloned.1.call-done), channel_id=1, source_target_pairs={{0,4},{4,0},{1,5},{5,1},{2,6},{6,2},{3,7},{7,3},{8,12},{12,8},{9,1... | collective-permute-start | bytes 6291464 | tf_op jit(solution)/shard_map/ppermute | solution.py:32
  (90 other events, 1727.3 us)
Sparse Core Ops, SparseCore 0:
  11.4 55.2 all-gather.8
  68.6 52.6 all-gather.10
  123.1 52.4 all-gather.18
  177.9 87.4 all-gather.12
  267.0 52.4 all-gather.16
  326.4 85.0 all-gather.14
  622.1 51.0 reduce-scatter.16
  761.5 49.8 reduce-scatter.8
  814.5 86.3 reduce-scatter.12
  903.7 52.5 reduce-scatter.14
  959.3 52.5 reduce-scatter.6
  1014.9 86.6 reduce-scatter.10
